TPU v7x, 512 devices: a whole 4x4x16 slice. The times are simulated.
512 devices in a mesh: seq: 128 (over x_lo, y, z), mp: 4 (over x_hi, core).
Axes of the slice: x: 4 (x_hi: 2, x_lo: 2; x = x_hi * 2 + x_lo), y: 4, z: 16, core: 2. Of those that a mesh axis runs over, the one named last changes fastest.
Arguments:
- incoming_image_patches: bfloat16 [1, 128, 128, 1152], P(None, 'seq', 'mp'), may hold values from -6 to 6
- initial_standardize_scaling: float32 [1152], replicated, may hold values from 0.1 to 1.9
- acceptance_matrix: bfloat16 [1152, 1024], P(None, 'mp'), may hold values from -0.1875 to 0.1875
- addressing_matrix: bfloat16 [1152, 1024], P(None, 'mp'), may hold values from -0.1875 to 0.1875
- content_matrix: bfloat16 [1152, 1024], P(None, 'mp'), may hold values from -0.1875 to 0.1875
- forgetting_lowdim_left_factor: bfloat16 [1152, 64], replicated, may hold values from -0.1875 to 0.1875
- forgetting_lowdim_right_factor: bfloat16 [64, 1024], P(None, 'mp'), may hold values from -1.5 to 1.5
- forgetting_baseline: float32 [1024], P('mp'), may hold values from -6 to 1
- self_token_reward: float32 [1024], P('mp'), may hold values from -3 to 3
- horizontal_cluster_scaling: float32 [1024], P('mp'), may hold values from 0.1 to 1.9
- vertical_cluster_scaling: float32 [1024], P('mp'), may hold values from 0.1 to 1.9
- temporal_mix_projection_matrix: bfloat16 [1024, 1152], P('mp'), may hold values from -0.1875 to 0.1875
- later_standardize_scaling: float32 [1152], replicated, may hold values from 0.1 to 1.9
- feature_mix_addressing_matrix: bfloat16 [1152, 4608], P('seq', 'mp'), may hold values from -0.1875 to 0.1875
- feature_mix_content_matrix: bfloat16 [4608, 1152], P('mp', 'seq'), may hold values from -0.09375 to 0.09375
Outputs:
- block_out: bfloat16 [1, 128, 128, 1152], P(None, 'seq', 'mp')
All inputs are finite; a program needn't handle non-finite values.
Results may differ from a plain program's by a relative error of at most 0.017.
Values may be sent and summed in bfloat16 or wider, within the bound.
No kernel may reach another device: no remote copies, remote signals or barrier semaphores. Data moves between devices by JAX's collectives and lax.ppermute only.
A program may use at most 64 MiB of HBM per device.

v0:
```python
import jax
import jax.numpy as jnp
from jax import lax
from jax.sharding import Mesh
from jax.sharding import PartitionSpec as P

SUBSPACE_SIZE = 64
SEQ = ("seq_0", "seq_1", "seq_2")


def from_everyone(value, axis):
    copies = jnp.broadcast_to(value, (lax.axis_size(axis), *value.shape))
    return lax.all_to_all(copies, axis, split_axis=0, concat_axis=0, tiled=True)


def taken_together(value, axis):
    everything = from_everyone(value, axis)
    return jnp.sum(everything.astype(jnp.float32), axis=0)


def in_order(pieces, dim):
    pieces = jnp.moveaxis(pieces, 0, dim)
    lengths = pieces.shape
    return pieces.reshape(*lengths[:dim], lengths[dim] * lengths[dim + 1], *lengths[dim + 2 :])


def stacked_from(value, axes, turns):
    pieces = value
    for k in turns:
        pieces = lax.all_gather(pieces, axes[k])
    done = turns[::-1]
    back = [done.index(k) for k in range(len(axes))]
    pieces = pieces.transpose(*back, *range(len(axes), pieces.ndim))
    return pieces.reshape(-1, *value.shape)


def gathered_by_axis(value, axes, turns, dim):
    return in_order(stacked_from(value, axes, turns), dim)


def split_up(value, dim, size):
    lengths = value.shape
    pieces = value.reshape(*lengths[:dim], size, lengths[dim] // size, *lengths[dim + 1 :])
    return jnp.moveaxis(pieces, dim, 0)


def sent_and_summed(value, axis, dim):
    size = lax.axis_size(axis)
    pieces = lax.all_to_all(split_up(value, dim, size), axis, 0, 0, tiled=True)
    return jnp.sum(pieces.astype(jnp.float32), axis=0)


def layer_norm(inputs, gain):
    values = inputs.astype(jnp.float32)
    average = jnp.mean(values, axis=-1, keepdims=True)
    centred = values - average
    spread = jnp.mean(centred * centred, axis=-1, keepdims=True)
    return (centred * lax.rsqrt(spread + 1e-05) * gain).astype(jnp.bfloat16)


def heads_first(array, nheads):
    number, length, inner_width = array.shape
    shaped = array.astype(jnp.float32).reshape(number, length, nheads, inner_width // nheads)
    return shaped.transpose(0, 2, 1, 3)


def recurrence(recept_in, keying_in, decays_in, valued_in, boost_in, gain):
    number, length, inner_width = recept_in.shape
    nheads = inner_width // SUBSPACE_SIZE
    head_size = inner_width // nheads
    blocks = length // 16
    acceptance_horizontal_lines = heads_first(recept_in, nheads)
    addressing_horizontal_lines = heads_first(keying_in, nheads)
    decays = heads_first(decays_in, nheads)
    content_horizontal_lines = heads_first(valued_in, nheads)
    boost = boost_in.reshape(nheads, 1, head_size)
    running = jnp.cumsum(decays, axis=2)
    before = running - decays
    before_blocks = before.reshape(number, nheads, blocks, 16, head_size)
    anchor = before_blocks[:, :, :, :1, :]
    queries = acceptance_horizontal_lines.reshape(number, nheads, blocks, 16, head_size) * jnp.exp(
        before_blocks - anchor
    )
    places = jnp.arange(length)
    limits = (jnp.arange(blocks) + 1) * 16
    usable = places[None, :] < limits[:, None]
    exponent = anchor - running[:, :, None, :, :]
    exponent = jnp.where(usable[None, None, :, :, None], exponent, -10000.0)
    weighted = addressing_horizontal_lines[:, :, None, :, :] * jnp.exp(exponent)
    scores = jnp.einsum("nhbqc,nhbsc->nhbqs", queries, weighted, precision=lax.Precision.HIGHEST)
    query_places = places.reshape(blocks, 16)
    earlier = places[None, None, :] < query_places[:, :, None]
    scores = jnp.where(earlier[None, None], scores, 0.0)
    current = jnp.sum(acceptance_horizontal_lines * boost * addressing_horizontal_lines, axis=-1)
    summed = jnp.einsum(
        "nhbqs,nhsc->nhbqc", scores, content_horizontal_lines, precision=lax.Precision.HIGHEST
    )
    summed = (
        summed.reshape(number, nheads, length, head_size)
        + current[..., None] * content_horizontal_lines
    )
    average = jnp.mean(summed, axis=-1, keepdims=True)
    centred = summed - average
    spread = jnp.mean(centred * centred, axis=-1, keepdims=True)
    normed = (
        (centred * lax.rsqrt(spread + 0.00064))
        .transpose(0, 2, 1, 3)
        .reshape(number, length, inner_width)
    )
    return (normed * gain).astype(jnp.bfloat16)


def lines_of_columns(array):
    images, height, columns, inner_width = array.shape
    return jnp.swapaxes(array, 1, 2).reshape(images * columns, height, inner_width)


def shards(
    incoming_image_patches,
    initial_standardize_scaling,
    acceptance_matrix,
    addressing_matrix,
    content_matrix,
    forgetting_lowdim_left_factor,
    forgetting_lowdim_right_factor,
    forgetting_baseline,
    self_token_reward,
    horizontal_cluster_scaling,
    vertical_cluster_scaling,
    temporal_mix_projection_matrix,
    later_standardize_scaling,
    feature_mix_addressing_matrix,
    feature_mix_content_matrix,
):
    images, row_count, part_cols, model_width = incoming_image_patches.shape
    whole_rows = lax.all_gather(incoming_image_patches, "mp", axis=2, tiled=True)
    full_cols = whole_rows.shape[2]
    inner_width = acceptance_matrix.shape[1]
    grid_shape = (images, row_count, full_cols, inner_width)
    xn1 = layer_norm(whole_rows, initial_standardize_scaling).reshape(-1, model_width)
    acceptance_horizontal_lines = jnp.dot(
        xn1, acceptance_matrix, preferred_element_type=jnp.float32
    ).astype(jnp.bfloat16)
    addressing_horizontal_lines = jnp.dot(
        xn1, addressing_matrix, preferred_element_type=jnp.float32
    ).astype(jnp.bfloat16)
    content_horizontal_lines = jnp.dot(
        xn1, content_matrix, preferred_element_type=jnp.float32
    ).astype(jnp.bfloat16)
    latent = jnp.tanh(
        jnp.dot(xn1, forgetting_lowdim_left_factor, preferred_element_type=jnp.float32)
    ).astype(jnp.bfloat16)
    forgetting_log_amount = (
        -0.7
        * jax.nn.sigmoid(
            forgetting_baseline
            + jnp.dot(latent, forgetting_lowdim_right_factor, preferred_element_type=jnp.float32)
        )
    ).astype(jnp.bfloat16)
    recept_grid = acceptance_horizontal_lines.reshape(grid_shape)
    keying_grid = addressing_horizontal_lines.reshape(grid_shape)
    decay_grid = forgetting_log_amount.reshape(grid_shape)
    line_shape = (images * row_count, full_cols, inner_width)
    col_recept, col_keying, col_decay = (
        lax.all_to_all(recept_grid, SEQ, split_axis=2, concat_axis=1, tiled=True),
        lax.all_to_all(keying_grid, SEQ, split_axis=2, concat_axis=1, tiled=True),
        lax.all_to_all(decay_grid, SEQ, split_axis=2, concat_axis=1, tiled=True),
    )
    horizontal_recurrence_result = recurrence(
        acceptance_horizontal_lines.reshape(line_shape),
        addressing_horizontal_lines.reshape(line_shape),
        forgetting_log_amount.reshape(line_shape),
        content_horizontal_lines.reshape(line_shape),
        self_token_reward,
        horizontal_cluster_scaling,
    )
    col_valued = lax.all_to_all(
        horizontal_recurrence_result.reshape(grid_shape),
        SEQ,
        split_axis=2,
        concat_axis=1,
        tiled=True,
    )
    height = col_recept.shape[1]
    columns = col_recept.shape[2]
    vertical_recurrence_result = recurrence(
        lines_of_columns(col_recept),
        lines_of_columns(col_keying),
        lines_of_columns(col_decay),
        lines_of_columns(col_valued),
        self_token_reward,
        vertical_cluster_scaling,
    )
    back_grid = jnp.swapaxes(
        vertical_recurrence_result.reshape(images, columns, height, inner_width), 1, 2
    )
    row_grid = lax.all_to_all(back_grid, SEQ, split_axis=1, concat_axis=2, tiled=True)
    partial_value = jnp.dot(
        row_grid.reshape(-1, inner_width),
        temporal_mix_projection_matrix,
        preferred_element_type=jnp.float32,
    )
    partial_value = lax.optimization_barrier(partial_value.astype(jnp.bfloat16)).astype(jnp.float32)
    partial_value = partial_value.reshape(images, row_count, full_cols, model_width)
    totals = taken_together(partial_value.astype(jnp.bfloat16), "mp").astype(jnp.float32)
    residual_all = (whole_rows.astype(jnp.float32) + totals).astype(jnp.bfloat16)
    mix_input = layer_norm(residual_all, later_standardize_scaling)
    residual = lax.dynamic_slice_in_dim(
        residual_all, lax.axis_index("mp") * part_cols, part_cols, 2
    )
    flattened = mix_input.reshape(-1, model_width)
    full_hidden = gathered_by_axis(feature_mix_addressing_matrix, SEQ, (0, 1, 2), 0)
    hidden_pre = jnp.dot(flattened, full_hidden, preferred_element_type=jnp.float32)
    positive = jnp.maximum(hidden_pre, 0.0)
    hidden = (positive * positive).astype(jnp.bfloat16)
    full_down = gathered_by_axis(feature_mix_content_matrix, SEQ, (0, 1, 2), 1)
    downward = jnp.dot(hidden, full_down, preferred_element_type=jnp.float32)
    downward = lax.optimization_barrier(downward.astype(jnp.bfloat16)).astype(jnp.float32)
    downward = downward.reshape(images, row_count, full_cols, model_width)
    mixed = sent_and_summed(downward.astype(jnp.bfloat16), "mp", 2)
    return (residual.astype(jnp.float32) + mixed).astype(jnp.bfloat16)


def solution(mesh):
    torus = Mesh(
        mesh.devices.reshape(2, 4, 16, mesh.shape["mp"]), ("seq_0", "seq_1", "seq_2", "mp")
    )
    return jax.shard_map(
        shards,
        mesh=torus,
        in_specs=(
            P(None, SEQ, "mp", None),
            P(),
            P(None, "mp"),
            P(None, "mp"),
            P(None, "mp"),
            P(),
            P(None, "mp"),
            P("mp"),
            P("mp"),
            P("mp"),
            P("mp"),
            P("mp", None),
            P(),
            P(SEQ, "mp"),
            P("mp", SEQ),
        ),
        out_specs=P(None, SEQ, "mp", None),
        check_vma=False,
    )
```

profile of v0, /device:TPU:1, one launch (start us, length us, event | category | flops | bytes accessed | tf_op | source)
XLA Modules:
  0.0 247.1 jit_solution(220768828950292183)
XLA Ops:
  6.6 4.4 %all-gather.3 = bf16[2304,9]{0,1:T(8,128)(2,1)S(1)} all-gather(bf16[1152,9]{0,1:T(8,128)(2,1)} %param.29), channel_id=5, replica_groups=mesh['seq_0'=2,'seq_1'=4,'seq_2'=16,'mp'=4] {'seq_0'}, dimensions={0}, use_global_device_ids=true | all-gather | bytes 62208 | tf_op jit(solution)/shard_map/all_gather | solution.py:30
  11.1 10.2 %all-gather.4 = bf16[8,1152,9]{1,2,0:T(8,128)(2,1)S(1)} all-gather(bf16[2,1152,9]{1,2,0:T(8,128)(2,1)S(1)} %copy.222), channel_id=6, replica_groups=mesh['seq_0'=2,'seq_1'=4,'seq_2'=16,'mp'=4] {'seq_1'}, dimensions={0}, use_global_device_ids=true | all-gather | bytes 207360 | tf_op jit(solution)/shard_map/all_gather | solution.py:30
  21.3 0.8 copy.230
  22.1 17.1 %all_gather.39 = bf16[1,1,128,1152]{3,2,1,0:T(8,128)(2,1)S(1)} all-gather(bf16[1,1,32,1152]{3,2,1,0:T(8,128)(2,1)} %param.15), channel_id=1, replica_groups=mesh['seq_0'=2,'seq_1'=4,'seq_2'=16,'mp'=4] {'mp'}, dimensions={2}, use_global_device_ids=true | all-gather | bytes 368640 | tf_op jit(solution)/shard_map/all_gather | solution.py:136
  39.3 0.2 fusion.21
  39.5 1.4 convolution_convert_fusion.3
  41.0 0.5 broadcast.270
  41.6 1.0 reduce.13
  42.6 0.7 reshape.531
  43.2 15.1 %all-to-all-start.2 = ((bf16[128,2,128]{2,1,0:T(2,128)(2,1)}), bf16[128,2,128]{2,1,0:T(2,128)(2,1)S(1)}, u32[]{:S(2)}, u32[]{:S(2)}) async-start(bf16[128,2,128]{2,1,0:T(2,128)(2,1)} %reshape.531), calls=%async_computation.2 | async-start | bytes 131072 | tf_op jit(solution)/shard_map/all_to_all | solution.py:166
  58.4 3.9 %all-gather.6 = bf16[2,9,1152]{2,1,0:T(8,128)(2,1)S(1)} all-gather(bf16[1,9,1152]{2,1,0:T(8,128)(2,1)S(1)} %bitcast.194), channel_id=2, replica_groups=mesh['seq_0'=2,'seq_1'=4,'seq_2'=16,'mp'=4] {'seq_0'}, dimensions={0}, use_global_device_ids=true | all-gather | bytes 62208 | tf_op jit(solution)/shard_map/all_gather | solution.py:30
  62.3 10.9 %all-gather.1 = bf16[8,9,1152]{2,1,0:T(8,128)(2,1)S(1)} all-gather(bf16[2,9,1152]{2,1,0:T(8,128)(2,1)S(1)} %all-gather.6), channel_id=3, replica_groups=mesh['seq_0'=2,'seq_1'=4,'seq_2'=16,'mp'=4] {'seq_1'}, dimensions={0}, use_global_device_ids=true | all-gather | bytes 207360 | tf_op jit(solution)/shard_map/all_gather | solution.py:30
  73.1 0.8 copy.220
  74.0 0.3 convolution_convert_fusion.4
  74.4 0.5 fusion.7
  75.2 0.3 reduce_window_sum.18
  75.9 1.0 reduce.14
  76.9 0.6 reshape.533
  77.9 1.2 convolution_select_fusion
  79.1 15.9 %all-to-all-start = ((bf16[128,2,128]{2,1,0:T(2,128)(2,1)}), bf16[128,2,128]{2,1,0:T(2,128)(2,1)S(1)}, u32[]{:S(2)}, u32[]{:S(2)}) async-start(bf16[128,2,128]{2,1,0:T(2,128)(2,1)} %reshape.533), calls=%async_computation | async-start | bytes 131072 | tf_op jit(solution)/shard_map/all_to_all | solution.py:165
  95.1 0.3 convolution_convert_fusion.2
  95.5 1.0 reduce.12
  96.5 0.7 reshape.529
  97.3 0.3 fusion.73
  97.9 11.3 %all-to-all-done = bf16[128,2,128]{2,1,0:T(2,128)(2,1)S(1)} async-done(((bf16[128,2,128]{2,1,0:T(2,128)(2,1)}), bf16[128,2,128]{2,1,0:T(2,128)(2,1)S(1)}, u32[]{:S(2)}, u32[]{:S(2)}) %all-to-all-start) | async-done | bytes 65568 | tf_op jit(solution)/shard_map/all_to_all | solution.py:165
  109.3 6.3 %all-to-all-start.1 = ((bf16[128,2,128]{2,1,0:T(2,128)(2,1)}), bf16[128,2,128]{2,1,0:T(2,128)(2,1)S(1)}, u32[]{:S(2)}, u32[]{:S(2)}) async-start(bf16[128,2,128]{2,1,0:T(2,128)(2,1)} %reshape.529), calls=%async_computation.1 | async-start | bytes 131072 | tf_op jit(solution)/shard_map/all_to_all | solution.py:167
  116.0 13.6 %all-to-all-done.1 = bf16[128,2,128]{2,1,0:T(2,128)(2,1)S(1)} async-done(((bf16[128,2,128]{2,1,0:T(2,128)(2,1)}), bf16[128,2,128]{2,1,0:T(2,128)(2,1)S(1)}, u32[]{:S(2)}, u32[]{:S(2)}) %all-to-all-start.1) | async-done | bytes 65568 | tf_op jit(solution)/shard_map/all_to_all | solution.py:167
  130.0 0.3 reduce_window_sum.17
  130.5 1.0 reduce.15
  131.5 0.7 reshape.535
  132.1 6.2 %all-to-all-start.3 = ((bf16[128,2,128]{2,1,0:T(2,128)(2,1)}), bf16[128,2,128]{2,1,0:T(2,128)(2,1)S(1)}, u32[]{:S(2)}, u32[]{:S(2)}) async-start(bf16[128,2,128]{2,1,0:T(2,128)(2,1)} %reshape.535), calls=%async_computation.3 | async-start | bytes 131072 | tf_op jit(solution)/shard_map/all_to_all | solution.py:177
  138.6 1.2 convolution_select_fusion.1
  139.9 13.1 %all-to-all-done.3 = bf16[128,2,128]{2,1,0:T(2,128)(2,1)S(1)} async-done(((bf16[128,2,128]{2,1,0:T(2,128)(2,1)}), bf16[128,2,128]{2,1,0:T(2,128)(2,1)S(1)}, u32[]{:S(2)}, u32[]{:S(2)}) %all-to-all-start.3) | async-done | bytes 65568 | tf_op jit(solution)/shard_map/all_to_all | solution.py:177
  153.2 0.3 fusion.74
  153.9 1.0 reduce.16
  155.0 20.0 %all_to_all.55 = bf16[128,2,128]{2,1,0:T(2,128)(2,1)S(1)} all-to-all(bf16[128,2,128]{2,1,0:T(2,128)(2,1)S(1)} %reshape.537), channel_id=1, replica_groups=mesh['seq_0'=2,'seq_1'=4,'seq_2'=16,'mp'=4] {'seq_0','seq_1','seq_2'}, dimensions={0} | all-to-all | bytes 131072 | tf_op jit(solution)/shard_map/all_to_all | solution.py:197
  175.0 0.2 convolution_convert_fusion.1
  175.3 28.3 %all_to_all.56 = bf16[4,1,1,128,1152]{4,3,2,1,0:T(8,128)(2,1)S(1)} all-to-all(bf16[4,1,1,128,1152]{4,3,2,1,0:T(8,128)(2,1)S(1)} %broadcast_in_dim.42), channel_id=1, replica_groups=mesh['seq_0'=2,'seq_1'=4,'seq_2'=16,'mp'=4] {'mp'}, dimensions={0} | all-to-all | bytes 2359296 | tf_op jit(solution)/shard_map/all_to_all | solution.py:13
  203.8 0.2 convert_reduce_fusion.2
  203.9 0.2 fusion.24
  204.2 5.5 %copy.232 = bf16[2,4,16,1152,9]{3,4,2,1,0:T(8,128)(2,1)} copy(bf16[2,4,16,1152,9]{3,0,1,2,4:T(2,128)(2,1)} %bitcast.145) | data formatting | bytes 5308416 | tf_op jit(solution)/shard_map/transpose | solution.py:22
  209.7 4.3 %reshape.511 = bf16[1152,1152]{0,1:T(8,128)(2,1)S(1)} reshape(bf16[1152,128,9]{0,2,1:T(8,128)(2,1)} %bitcast.144) | data formatting | bytes 5308416 | tf_op jit(solution)/shard_map/reshape | solution.py:24
  214.1 4.5 %copy.221 = bf16[2,4,16,9,1152]{4,3,2,1,0:T(8,128)(2,1)} copy(bf16[2,4,16,9,1152]{4,0,3,1,2:T(2,128)(2,1)} %bitcast.146) | data formatting | bytes 5308416 | tf_op jit(solution)/shard_map/transpose | solution.py:33
  218.7 5.8 %reshape_reshape.3 = bf16[1152,1152]{1,0:T(8,128)(2,1)} reshape(bf16[2,4,16,9,1152]{4,3,2,1,0:T(8,128)(2,1)} %copy.221) | data formatting | bytes 5308416 | tf_op jit(solution)/shard_map/reshape;reshape | solution.py:24
  224.4 3.8 %convolution_convert_fusion = bf16[128,1152]{1,0:T(8,128)(2,1)} fusion(bf16[1152,1152]{0,1:T(8,128)(2,1)S(1)} %reshape.511, bf16[1152,1152]{1,0:T(8,128)(2,1)} %reshape_reshape.3, bf16[1,1,128,1152]{3,2,1,0:T(8,128)(2,1)S(1)} %get-tuple-element.8, f32[1152]{0:T(1024)S(1)} %copy-done.2, f32[128]{0:T(128)S(1)} %add_rsqrt_fusion.2, ...), kind=kOutput, calls=%fused_computation.3 | convolution fusion | flops 680804352 | bytes 5903872 | tf_op jit(solution)/shard_map/dot_general | solution.py:217
  228.2 4.5 %all-to-all-start.6 = ((bf16[4,1,1,32,1152]{4,3,2,1,0:T(8,128)(2,1)}), bf16[4,1,1,32,1152]{4,3,2,1,0:T(8,128)(2,1)S(1)}, u32[]{:S(2)}, u32[]{:S(2)}) async-start(bf16[4,1,1,32,1152]{4,3,2,1,0:T(8,128)(2,1)} %bitcast.158), calls=%async_computation.6 | async-start | bytes 589824 | tf_op jit(solution)/shard_map/all_to_all | solution.py:49
  232.7 6.9 %all-to-all-done.6 = bf16[4,1,1,32,1152]{4,3,2,1,0:T(8,128)(2,1)S(1)} async-done(((bf16[4,1,1,32,1152]{4,3,2,1,0:T(8,128)(2,1)}), bf16[4,1,1,32,1152]{4,3,2,1,0:T(8,128)(2,1)S(1)}, u32[]{:S(2)}, u32[]{:S(2)}) %all-to-all-start.6) | async-done | bytes 294944 | tf_op jit(solution)/shard_map/all_to_all | solution.py:49
  239.6 0.7 fusion.55
  (94 shorter events, 4.2 us)
Async XLA Ops:
  6.5 168.4 %copy-start = (bf16[256,1152]{1,0:T(8,128)(2,1)S(1)}, bf16[256,1152]{1,0:T(8,128)(2,1)}, u32[]{:S(2)}) copy-start(bf16[256,1152]{1,0:T(8,128)(2,1)} %param.26) | copy-start | bytes 1769476
  6.5 67.4 %copy-start.10 = (f32[1152]{0:T(1024)S(1)}, f32[1152]{0:T(1024)}, u32[]{:S(2)}) copy-start(f32[1152]{0:T(1024)} %param.16) | copy-start | bytes 13828
  6.5 51.8 %copy-start.1 = (bf16[9,1152]{1,0:T(8,128)(2,1)S(1)}, bf16[9,1152]{1,0:T(8,128)(2,1)}, u32[]{:S(2)}) copy-start(bf16[9,1152]{1,0:T(8,128)(2,1)} %param.28) | copy-start | bytes 62212
  6.5 67.5 %copy-start.6 = (bf16[1152,256]{1,0:T(8,128)(2,1)S(1)}, bf16[1152,256]{1,0:T(8,128)(2,1)}, u32[]{:S(2)}) copy-start(bf16[1152,256]{1,0:T(8,128)(2,1)} %param.17) | copy-start | bytes 1769476
  6.5 197.7 %all-gather.12.cloned.1.call-start = ((), (), s32[]{:S(2)}) async-start(), calls=%async_computation.8 | async-start | bytes 2820096 | tf_op jit(solution)/shard_map/all_gather | solution.py:30
  22.0 52.4 %copy-start.8 = (bf16[1152,64]{0,1:T(8,128)(2,1)S(1)}, bf16[1152,64]{0,1:T(8,128)(2,1)}, u32[]{:S(2)}) copy-start(bf16[1152,64]{0,1:T(8,128)(2,1)} %param.20) | copy-start | bytes 442372
  22.0 52.4 %copy-start.9 = (bf16[64,256]{1,0:T(8,128)(2,1)S(1)}, bf16[64,256]{1,0:T(8,128)(2,1)}, u32[]{:S(2)}) copy-start(bf16[64,256]{1,0:T(8,128)(2,1)} %param.21) | copy-start | bytes 98308
  22.0 52.4 %copy-start.11 = (f32[256]{0:T(256)S(1)}, f32[256]{0:T(256)}, u32[]{:S(2)}) copy-start(f32[256]{0:T(256)} %param.22) | copy-start | bytes 3076
  43.2 35.9 %all-to-all-start.2 = ((bf16[128,2,128]{2,1,0:T(2,128)(2,1)}), bf16[128,2,128]{2,1,0:T(2,128)(2,1)S(1)}, u32[]{:S(2)}, u32[]{:S(2)}) async-start(bf16[128,2,128]{2,1,0:T(2,128)(2,1)} %reshape.531), calls=%async_computation.2 | async-start | bytes 131072 | tf_op jit(solution)/shard_map/all_to_all | solution.py:166
  58.3 155.8 %all-gather.10.cloned.1.call-start = ((), (), s32[]{:S(2)}) async-start(), calls=%async_computation.7 | async-start | bytes 2820096 | tf_op jit(solution)/shard_map/all_gather | solution.py:30
  75.1 20.0 %copy-start.7 = (bf16[1152,256]{1,0:T(8,128)(2,1)S(1)}, bf16[1152,256]{1,0:T(8,128)(2,1)}, u32[]{:S(2)}) copy-start(bf16[1152,256]{1,0:T(8,128)(2,1)} %param.19) | copy-start | bytes 1769476
  77.7 20.0 %copy-start.5 = (f32[256]{0:T(256)S(1)}, f32[256]{0:T(256)}, u32[]{:S(2)}) copy-start(f32[256]{0:T(256)} %param.23) | copy-start | bytes 3076
  79.1 30.1 %all-to-all-start = ((bf16[128,2,128]{2,1,0:T(2,128)(2,1)}), bf16[128,2,128]{2,1,0:T(2,128)(2,1)S(1)}, u32[]{:S(2)}, u32[]{:S(2)}) async-start(bf16[128,2,128]{2,1,0:T(2,128)(2,1)} %reshape.533), calls=%async_computation | async-start | bytes 131072 | tf_op jit(solution)/shard_map/all_to_all | solution.py:165
  95.4 35.0 %copy-start.3 = (f32[256]{0:T(256)S(1)}, f32[256]{0:T(256)}, u32[]{:S(2)}) copy-start(f32[256]{0:T(256)} %param.24) | copy-start | bytes 3076
  109.3 20.4 %all-to-all-start.1 = ((bf16[128,2,128]{2,1,0:T(2,128)(2,1)}), bf16[128,2,128]{2,1,0:T(2,128)(2,1)S(1)}, u32[]{:S(2)}, u32[]{:S(2)}) async-start(bf16[128,2,128]{2,1,0:T(2,128)(2,1)} %reshape.529), calls=%async_computation.1 | async-start | bytes 131072 | tf_op jit(solution)/shard_map/all_to_all | solution.py:167
  132.1 20.9 %all-to-all-start.3 = ((bf16[128,2,128]{2,1,0:T(2,128)(2,1)}), bf16[128,2,128]{2,1,0:T(2,128)(2,1)S(1)}, u32[]{:S(2)}, u32[]{:S(2)}) async-start(bf16[128,2,128]{2,1,0:T(2,128)(2,1)} %reshape.535), calls=%async_computation.3 | async-start | bytes 131072 | tf_op jit(solution)/shard_map/all_to_all | solution.py:177
  138.3 15.5 %copy-start.4 = (f32[256]{0:T(256)S(1)}, f32[256]{0:T(256)}, u32[]{:S(2)}) copy-start(f32[256]{0:T(256)} %param.25) | copy-start | bytes 3076
  218.7 5.8 %copy-start.2 = (f32[1152]{0:T(1024)S(1)}, f32[1152]{0:T(1024)}, u32[]{:S(2)}) copy-start(f32[1152]{0:T(1024)} %param.27) | copy-start | bytes 13828
  228.2 11.3 %all-to-all-start.6 = ((bf16[4,1,1,32,1152]{4,3,2,1,0:T(8,128)(2,1)}), bf16[4,1,1,32,1152]{4,3,2,1,0:T(8,128)(2,1)S(1)}, u32[]{:S(2)}, u32[]{:S(2)}) async-start(bf16[4,1,1,32,1152]{4,3,2,1,0:T(8,128)(2,1)} %bitcast.158), calls=%async_computation.6 | async-start | bytes 589824 | tf_op jit(solution)/shard_map/all_to_all | solution.py:49
Sparse Core Ops, SparseCore 0:
  22.2 74.2 all-gather.11
  98.6 74.4 all-gather.9
where the time goes:
time: 248 us; the launch traced here: 247 us
  blocking collectives  94.7 us (38%)
  starting transfers between devices  48 us (19%)
  waiting for transfers between devices  45.1 us (18%)
  local copies, waits for them, and re-layouts  27.9 us (11%)
  between operations  14 us (6%)
  matrix products  9.6 us (4%)
  other arithmetic  7.74 us (3%)
    all_gather x4, blocking collectives, stacked_from(): pieces = lax.all_gather(pieces, axes[k])  29.3 us
    all_to_all x1, blocking collectives, from_everyone(): return lax.all_to_all(copies, axis, split_axis=0, concat_axis=0, tiled=True)  28.3 us
    all_to_all x1, blocking collectives, shards(): lax.all_to_all(back_grid, SEQ, split_axis=1, concat_axis=2, tiled=True)  20 us
    all_gather x1, blocking collectives, shards(): lax.all_gather(incoming_image_patches, 'mp', axis=2, tiled=True)  17.1 us
    all_to_all x1, starting transfers between devices, shards(): lax.all_to_all(recept_grid, SEQ, split_axis=2, concat_axis=1, tiled=True)  15.9 us
    all_to_all x1, starting transfers between devices, shards(): lax.all_to_all(keying_grid, SEQ, split_axis=2, concat_axis=1, tiled=True)  15.1 us
    all_to_all x1, waiting for transfers between devices, shards(): lax.all_to_all(decay_grid, SEQ, split_axis=2, concat_axis=1, tiled=True)  13.6 us
    all_to_all x1, waiting for transfers between devices, shards(): lax.all_to_all(horizontal_recurrence_result.reshape(grid_shape), SEQ, spl...  13.1 us
  transfers between devices with their start and end apart: 7, of which 4 were waited for; matrix products, arithmetic and copies ran while one was open for 12% of the time, Pallas kernels for 0%

commit v1 on v0

v1 whole, which is shorter than its diff:
```python
import jax
import jax.numpy as jnp
from jax import lax
from jax.sharding import Mesh
from jax.sharding import PartitionSpec as P

SUBSPACE_SIZE = 64
SEQ = ("x_lo", "y", "z")
MP = ("x_hi", "core")
PLANE = ("x_lo", "y")


def from_everyone(value, axis):
    copies = jnp.broadcast_to(value, (lax.axis_size(axis), *value.shape))
    return lax.all_to_all(copies, axis, split_axis=0, concat_axis=0, tiled=True)


def split_up(value, dim, size):
    lengths = value.shape
    pieces = value.reshape(*lengths[:dim], size, lengths[dim] // size, *lengths[dim + 1 :])
    return jnp.moveaxis(pieces, dim, 0)


def sent_and_summed(value, axis, dim):
    size = lax.axis_size(axis)
    pieces = lax.all_to_all(split_up(value, dim, size), axis, 0, 0, tiled=True)
    return jnp.sum(pieces.astype(jnp.float32), axis=0)


def layer_norm(inputs, gain):
    values = inputs.astype(jnp.float32)
    average = jnp.mean(values, axis=-1, keepdims=True)
    centred = values - average
    spread = jnp.mean(centred * centred, axis=-1, keepdims=True)
    return (centred * lax.rsqrt(spread + 1e-05) * gain).astype(jnp.bfloat16)


def heads_first(array, nheads):
    number, length, inner_width = array.shape
    shaped = array.astype(jnp.float32).reshape(number, length, nheads, inner_width // nheads)
    return shaped.transpose(0, 2, 1, 3)


def recurrence(recept_in, keying_in, decays_in, valued_in, boost_in, gain):
    number, length, inner_width = recept_in.shape
    nheads = inner_width // SUBSPACE_SIZE
    head_size = inner_width // nheads
    blocks = length // 16
    acceptance_horizontal_lines = heads_first(recept_in, nheads)
    addressing_horizontal_lines = heads_first(keying_in, nheads)
    decays = heads_first(decays_in, nheads)
    content_horizontal_lines = heads_first(valued_in, nheads)
    boost = boost_in.reshape(nheads, 1, head_size)
    running = jnp.cumsum(decays, axis=2)
    before = running - decays
    before_blocks = before.reshape(number, nheads, blocks, 16, head_size)
    anchor = before_blocks[:, :, :, :1, :]
    queries = acceptance_horizontal_lines.reshape(number, nheads, blocks, 16, head_size) * jnp.exp(
        before_blocks - anchor
    )
    places = jnp.arange(length)
    limits = (jnp.arange(blocks) + 1) * 16
    usable = places[None, :] < limits[:, None]
    exponent = anchor - running[:, :, None, :, :]
    exponent = jnp.where(usable[None, None, :, :, None], exponent, -10000.0)
    weighted = addressing_horizontal_lines[:, :, None, :, :] * jnp.exp(exponent)
    scores = jnp.einsum("nhbqc,nhbsc->nhbqs", queries, weighted, precision=lax.Precision.HIGHEST)
    query_places = places.reshape(blocks, 16)
    earlier = places[None, None, :] < query_places[:, :, None]
    scores = jnp.where(earlier[None, None], scores, 0.0)
    current = jnp.sum(acceptance_horizontal_lines * boost * addressing_horizontal_lines, axis=-1)
    summed = jnp.einsum(
        "nhbqs,nhsc->nhbqc", scores, content_horizontal_lines, precision=lax.Precision.HIGHEST
    )
    summed = (
        summed.reshape(number, nheads, length, head_size)
        + current[..., None] * content_horizontal_lines
    )
    average = jnp.mean(summed, axis=-1, keepdims=True)
    centred = summed - average
    spread = jnp.mean(centred * centred, axis=-1, keepdims=True)
    normed = (
        (centred * lax.rsqrt(spread + 0.00064))
        .transpose(0, 2, 1, 3)
        .reshape(number, length, inner_width)
    )
    return (normed * gain).astype(jnp.bfloat16)


def unit_order(planes, depth, width):
    stored = jnp.arange(planes * depth * width)
    z, rest = stored // (planes * width), stored % (planes * width)
    plane, row = rest // width, rest % width
    true_place = (plane * depth + z) * width + row
    return true_place


def shards(
    incoming_image_patches,
    initial_standardize_scaling,
    acceptance_matrix,
    addressing_matrix,
    content_matrix,
    forgetting_lowdim_left_factor,
    forgetting_lowdim_right_factor,
    forgetting_baseline,
    self_token_reward,
    horizontal_cluster_scaling,
    vertical_cluster_scaling,
    temporal_mix_projection_matrix,
    later_standardize_scaling,
    feature_mix_addressing_matrix,
    feature_mix_content_matrix,
):
    images, row_count, part_cols, model_width = incoming_image_patches.shape
    tokens = incoming_image_patches.reshape(part_cols, model_width)
    whole_rows = lax.all_gather(tokens, MP, axis=0, tiled=True)
    full_cols = whole_rows.shape[0]
    inner_width = acceptance_matrix.shape[1]

    planes, depth = lax.axis_size(PLANE), lax.axis_size("z")
    width = feature_mix_addressing_matrix.shape[0]
    pair = jnp.stack([feature_mix_addressing_matrix, feature_mix_content_matrix.T])
    plane_pair = from_everyone(pair, PLANE).reshape(planes, *pair.shape)
    plane_up = plane_pair[:, 0].reshape(planes * width, -1)
    plane_down = plane_pair[:, 1].reshape(planes * width, -1)
    full_up = lax.all_gather(plane_up, "z", axis=0, tiled=True)
    full_down = lax.all_gather(plane_down, "z", axis=0, tiled=True)

    xn1 = layer_norm(whole_rows, initial_standardize_scaling)
    recept = jnp.dot(xn1, acceptance_matrix, preferred_element_type=jnp.float32).astype(
        jnp.bfloat16
    )
    keying = jnp.dot(xn1, addressing_matrix, preferred_element_type=jnp.float32).astype(
        jnp.bfloat16
    )
    valued = jnp.dot(xn1, content_matrix, preferred_element_type=jnp.float32).astype(jnp.bfloat16)
    latent = jnp.tanh(
        jnp.dot(xn1, forgetting_lowdim_left_factor, preferred_element_type=jnp.float32)
    ).astype(jnp.bfloat16)
    decay = (
        -0.7
        * jax.nn.sigmoid(
            forgetting_baseline
            + jnp.dot(latent, forgetting_lowdim_right_factor, preferred_element_type=jnp.float32)
        )
    ).astype(jnp.bfloat16)
    row_out = recurrence(
        recept[None],
        keying[None],
        decay[None],
        valued[None],
        self_token_reward,
        horizontal_cluster_scaling,
    )[0]
    sent = jnp.stack([recept, keying, decay, row_out], axis=1)
    got = lax.all_to_all(
        sent.reshape(full_cols, 4 * inner_width // 128, 128),
        SEQ,
        split_axis=0,
        concat_axis=0,
        tiled=True,
    )
    height = got.shape[0]
    got = got.reshape(height, 4, inner_width)
    col_out = recurrence(
        got[None, :, 0],
        got[None, :, 1],
        got[None, :, 2],
        got[None, :, 3],
        self_token_reward,
        vertical_cluster_scaling,
    )[0]
    back = lax.all_to_all(
        col_out.reshape(height, inner_width // 128, 128),
        SEQ,
        split_axis=0,
        concat_axis=0,
        tiled=True,
    ).reshape(full_cols, inner_width)
    partial_value = jnp.dot(
        back, temporal_mix_projection_matrix, preferred_element_type=jnp.float32
    ).astype(jnp.bfloat16)
    attended = sent_and_summed(partial_value, MP, 0)
    residual = (tokens.astype(jnp.float32) + attended).astype(jnp.bfloat16)
    mix_input = layer_norm(residual, later_standardize_scaling)

    places = unit_order(planes, depth, width)
    moved = (jnp.arange(model_width)[:, None] == places[None, :]).astype(jnp.bfloat16)
    mix_input = jnp.dot(mix_input, moved, preferred_element_type=jnp.float32).astype(jnp.bfloat16)
    mix_all = lax.all_gather(mix_input, MP, axis=0, tiled=True)
    hidden_pre = jnp.dot(mix_all, full_up, preferred_element_type=jnp.float32)
    positive = jnp.maximum(hidden_pre, 0.0)
    hidden = (positive * positive).astype(jnp.bfloat16)
    downward = lax.dot_general(
        hidden, full_down, (((1,), (1,)), ((), ())), preferred_element_type=jnp.float32
    ).astype(jnp.bfloat16)
    downward = lax.dot_general(
        downward, moved, (((1,), (1,)), ((), ())), preferred_element_type=jnp.float32
    ).astype(jnp.bfloat16)
    mixed = sent_and_summed(downward, MP, 0)
    block_out = (residual.astype(jnp.float32) + mixed).astype(jnp.bfloat16)
    return block_out.reshape(images, row_count, part_cols, model_width)


def solution(mesh):
    torus = Mesh(mesh.devices.reshape(2, 4, 16, 2, 2), (*SEQ, *MP))
    return jax.shard_map(
        shards,
        mesh=torus,
        in_specs=(
            P(None, SEQ, MP, None),
            P(),
            P(None, MP),
            P(None, MP),
            P(None, MP),
            P(),
            P(None, MP),
            P(MP),
            P(MP),
            P(MP),
            P(MP),
            P(MP, None),
            P(),
            P(SEQ, MP),
            P(MP, SEQ),
        ),
        out_specs=P(None, SEQ, MP, None),
        check_vma=False,
    )
```

time: 248 us -> 207 us (0.83)
  starting transfers between devices: 48 us -> 22.8 us
  waiting for transfers between devices: 45.1 us -> 69.8 us
  local copies, waits for them, and re-layouts: 27.9 us -> 6.29 us
  blocking collectives: 94.7 us -> 76.4 us
  other arithmetic: 7.74 us -> 3.71 us
  matrix products: 9.6 us -> 13.6 us
    all_gather x2, waiting for transfers between devices: 0.04 us -> 40.7 us  [the longest x1 40.7 us: shards(): full_down = lax.all_gather(plane_down, 'z', axis=0, tiled=True)]
    all_to_all x4 -> x1, starting transfers between devices: 43.5 us -> 15.7 us  [shards(): lax.all_to_all(sent.reshape(full_cols, 4 * inner_width // 128, 128), SEQ,...]
    all_gather x5 -> x2, blocking collectives: 46.4 us -> 20 us  [the longest x1 11.8 us: shards(): whole_rows = lax.all_gather(tokens, MP, axis=0, tiled=True)]
    all_to_all x1 -> x2, blocking collectives: 20 us -> 44.1 us  [the longest x1 22.7 us: shards(): lax.all_to_all(col_out.reshape(height, inner_width // 128, 128), SEQ, spl...]
    all_to_all x1, blocking collectives: 28.3 us -> 12.3 us  [from_everyone(): return lax.all_to_all(copies, axis, split_axis=0, concat_axis=0, tiled=True)]
    all_to_all x4 -> x1, waiting for transfers between devices: 38.1 us -> 22.2 us  [shards(): lax.all_to_all(sent.reshape(full_cols, 4 * inner_width // 128, 128), SEQ,...]
    transpose x2 -> x0, local copies, waits for them, and re-layouts: 10.1 us -> none  [the longest x1 5.53 us: in_order(): pieces = jnp.moveaxis(pieces, 0, dim)]
    unnamed x5 -> x0, other arithmetic: 4.97 us -> none
  transfers between devices with their start and end apart: 7 -> 4, of which waited for: 4 -> 3; matrix products, arithmetic and copies ran while one was open for 12% -> 8% of each run, Pallas kernels for 0% -> 0%
where the time goes in v1:
time: 207 us
  blocking collectives  76.4 us (37%)
  waiting for transfers between devices  69.8 us (34%)
  starting transfers between devices  22.8 us (11%)
  between operations  13.9 us (7%)
  matrix products  13.6 us (7%)
  local copies, waits for them, and re-layouts  6.29 us (3%)
  other arithmetic  3.71 us (2%)
    all_gather x1, waiting for transfers between devices, shards(): full_down = lax.all_gather(plane_down, 'z', axis=0, tiled=True)  40.7 us
    all_to_all x1, blocking collectives, shards(): lax.all_to_all(col_out.reshape(height, inner_width // 128, 128), SEQ, spl...  22.7 us
    all_to_all x1, waiting for transfers between devices, shards(): lax.all_to_all(sent.reshape(full_cols, 4 * inner_width // 128, 128), SEQ,...  22.2 us
    all_to_all x1, blocking collectives, sent_and_summed(): pieces = lax.all_to_all(split_up(value, dim, size), axis, 0, 0, tiled=True)  21.4 us
    all_to_all x1, starting transfers between devices, shards(): lax.all_to_all(sent.reshape(full_cols, 4 * inner_width // 128, 128), SEQ,...  15.7 us
    all_to_all x1, blocking collectives, from_everyone(): return lax.all_to_all(copies, axis, split_axis=0, concat_axis=0, tiled=True)  12.3 us
    all_gather x1, blocking collectives, shards(): whole_rows = lax.all_gather(tokens, MP, axis=0, tiled=True)  11.8 us
    all_gather x1, blocking collectives, shards(): mix_all = lax.all_gather(mix_input, MP, axis=0, tiled=True)  8.17 us
  transfers between devices with their start and end apart: 4, of which 3 were waited for; matrix products, arithmetic and copies ran while one was open for 8% of the time, Pallas kernels for 0%

profile of v1, /device:TPU:1, one launch (start us, length us, event | category | flops | bytes accessed | tf_op | source)
XLA Modules:
  0.0 206.6 jit_solution(17887059847881086414)
XLA Ops:
  6.6 0.9 pad_maximum_fusion.1
  7.5 0.2 broadcast_in_dim.42
  7.7 12.3 %all_to_all.25 = bf16[8,2,9,1152]{3,1,2,0:T(2,128)(2,1)S(1)} all-to-all(bf16[8,2,9,1152]{3,1,2,0:T(2,128)(2,1)S(1)} %broadcast_in_dim.42), channel_id=1, replica_groups=mesh['x_lo'=2,'y'=4,'z'=16,'x_hi'=2,'core'=2] {'x_lo','y'}, dimensions={0} | all-to-all | bytes 663552 | tf_op jit(solution)/shard_map/all_to_all | solution.py:15
  20.1 1.5 slice_reduce_fusion
  21.6 0.7 reshape_squeeze.7
  22.4 11.8 %all-gather = bf16[1,1,128,1152]{3,2,1,0:T(8,128)(2,1)S(1)} all-gather(bf16[1,1,32,1152]{3,2,1,0:T(8,128)(2,1)S(1)} %copy-done.1), channel_id=2, replica_groups=mesh['x_lo'=2,'y'=4,'z'=16,'x_hi'=2,'core'=2] {'x_hi','core'}, dimensions={2}, use_global_device_ids=true | all-gather | bytes 368640 | tf_op jit(solution)/shard_map/all_gather | solution.py:117
  34.2 0.1 convert_reduce_fusion
  34.3 0.2 fusion.26
  34.6 0.5 fusion.13
  35.3 0.1 copy.94
  35.4 0.3 reduce_window_sum.17
  35.7 0.1 copy.96
  35.9 0.3 convolution_convert_fusion.4
  36.3 0.1 copy.92
  36.4 0.3 convolution_convert_fusion.3
  36.9 1.4 convolution_convert_fusion.2
  38.3 0.1 copy.97
  38.6 1.2 convolution_select_fusion.1
  39.8 0.2 fusion.94
  40.1 0.1 copy.98
  40.3 0.1 multiply_reduce_fusion.2
  40.7 0.2 copy.100
  40.9 0.9 copy.101
  41.8 15.7 %all-to-all-start = ((bf16[128,8,128]{2,1,0:T(8,128)(2,1)}), bf16[128,8,128]{2,1,0:T(8,128)(2,1)S(1)}, u32[]{:S(2)}, u32[]{:S(2)}) async-start(bf16[128,8,128]{2,1,0:T(8,128)(2,1)} %copy.101), calls=%async_computation | async-start | bytes 524288 | tf_op jit(solution)/shard_map/all_to_all | solution.py:157
  57.5 0.8 reshape_squeeze.8
  58.3 22.2 %all-to-all-done = bf16[128,8,128]{2,1,0:T(8,128)(2,1)S(1)} async-done(((bf16[128,8,128]{2,1,0:T(8,128)(2,1)}), bf16[128,8,128]{2,1,0:T(8,128)(2,1)S(1)}, u32[]{:S(2)}, u32[]{:S(2)}) %all-to-all-start) | async-done | bytes 262176 | tf_op jit(solution)/shard_map/all_to_all | solution.py:157
  80.5 0.2 copy.102
  80.8 0.1 copy.104
  80.9 0.3 reduce_window_sum.18
  81.2 0.1 copy.105
  81.3 0.1 copy.103
  81.5 1.2 convolution_select_fusion
  82.7 0.2 fusion.95
  83.0 0.1 copy.106
  83.1 0.1 fusion.55
  83.6 22.7 %all_to_all.26 = bf16[128,2,128]{2,1,0:T(2,128)(2,1)S(1)} all-to-all(bf16[128,2,128]{2,1,0:T(2,128)(2,1)S(1)} %copy.108), channel_id=1, replica_groups=mesh['x_lo'=2,'y'=4,'z'=16,'x_hi'=2,'core'=2] {'x_lo','y','z'}, dimensions={0} | all-to-all | bytes 131072 | tf_op jit(solution)/shard_map/all_to_all | solution.py:174
  106.3 1.0 convolution_convert_fusion.1
  107.2 7.1 %all-to-all-start.2 = ((bf16[4,32,1152]{2,1,0:T(8,128)(2,1)}), bf16[4,32,1152]{2,1,0:T(8,128)(2,1)S(1)}, u32[]{:S(2)}, u32[]{:S(2)}) async-start(bf16[4,32,1152]{2,1,0:T(8,128)(2,1)} %bitcast.53), calls=%async_computation.2 | async-start | bytes 589824 | tf_op jit(solution)/shard_map/all_to_all | solution.py:26
  114.3 6.9 %all-to-all-done.2 = bf16[4,32,1152]{2,1,0:T(8,128)(2,1)S(1)} async-done(((bf16[4,32,1152]{2,1,0:T(8,128)(2,1)}), bf16[4,32,1152]{2,1,0:T(8,128)(2,1)S(1)}, u32[]{:S(2)}, u32[]{:S(2)}) %all-to-all-start.2) | async-done | bytes 294944 | tf_op jit(solution)/shard_map/all_to_all | solution.py:26
  121.2 0.1 convert_reduce_fusion.3
  121.4 0.2 fusion.47
  121.6 1.1 fusion.7
  122.7 8.2 %all_gather.13 = bf16[128,1152]{1,0:T(8,128)(2,1)S(1)} all-gather(bf16[32,1152]{1,0:T(8,128)(2,1)S(1)} %fusion.7), channel_id=1, replica_groups=mesh['x_lo'=2,'y'=4,'z'=16,'x_hi'=2,'core'=2] {'x_hi','core'}, dimensions={0}, use_global_device_ids=true | all-gather | bytes 368640 | tf_op jit(solution)/shard_map/all_gather | solution.py:191
  130.9 2.4 %fusion.5 = bf16[128,1152]{1,0:T(8,128)(2,1)S(1)} fusion(bf16[128,1152]{1,0:T(8,128)(2,1)S(1)} %all_gather.13, bf16[1152,1152]{1,0:T(8,128)(2,1)} %all-gather.4.cloned.1.call-done), kind=kOutput, calls=%fused_computation.7 | convolution fusion | flops 340180992 | bytes 3244032 | tf_op jit(solution)/shard_map/dot_general | solution.py:192
  133.3 40.7 %all-gather.6.cloned.1.call-done = bf16[1152,1152]{1,0:T(8,128)(2,1)} async-done(((bf16[72,1152]{1,0:T(8,128)(2,1)}), bf16[1152,1152]{1,0:T(8,128)(2,1)}) %all-gather.6.cloned.1.call-update) | async-done | bytes 2654224 | tf_op jit(solution)/shard_map/all_gather | solution.py:128
  174.0 3.7 %fusion.6 = bf16[128,1152]{1,0:T(8,128)(2,1)S(1)} fusion(s32[1152]{0:T(1024)S(1)} %fusion.74, bf16[128,1152]{1,0:T(8,128)(2,1)S(1)} %fusion.5, bf16[1152,1152]{1,0:T(8,128)(2,1)} %all-gather.6.cloned.1.call-done), kind=kOutput, calls=%fused_computation.8 | convolution fusion | flops 681099264 | bytes 3248640 | tf_op jit(solution)/shard_map/dot_general | solution.py:198
  177.6 21.4 %all_to_all.27 = bf16[4,32,1152]{2,1,0:T(8,128)(2,1)S(1)} all-to-all(bf16[4,32,1152]{2,1,0:T(8,128)(2,1)S(1)} %bitcast.162), channel_id=1, replica_groups=mesh['x_lo'=2,'y'=4,'z'=16,'x_hi'=2,'core'=2] {'x_hi','core'}, dimensions={0} | all-to-all | bytes 589824 | tf_op jit(solution)/shard_map/all_to_all | solution.py:26
  199.1 0.7 fusion.53
  (66 shorter events, 1.6 us)
Async XLA Ops:
  6.5 99.7 %copy-start = (bf16[256,1152]{1,0:T(8,128)(2,1)S(1)}, bf16[256,1152]{1,0:T(8,128)(2,1)}, u32[]{:S(2)}) copy-start(bf16[256,1152]{1,0:T(8,128)(2,1)} %param.26) | copy-start | bytes 1769476
  6.5 15.8 %copy-start.1 = (bf16[1,1,32,1152]{3,2,1,0:T(8,128)(2,1)S(1)}, bf16[1,1,32,1152]{3,2,1,0:T(8,128)(2,1)}, u32[]{:S(2)}) copy-start(bf16[1,1,32,1152]{3,2,1,0:T(8,128)(2,1)} %param.15) | copy-start | bytes 221188
  6.5 28.0 %copy-start.9 = (f32[1152]{0:T(1024)S(1)}, f32[1152]{0:T(1024)}, u32[]{:S(2)}) copy-start(f32[1152]{0:T(1024)} %param.16) | copy-start | bytes 13828
  6.5 28.0 %copy-start.7 = (bf16[1152,64]{0,1:T(8,128)(2,1)S(1)}, bf16[1152,64]{0,1:T(8,128)(2,1)}, u32[]{:S(2)}) copy-start(bf16[1152,64]{0,1:T(8,128)(2,1)} %param.20) | copy-start | bytes 442372
  6.5 28.1 %copy-start.8 = (bf16[64,256]{1,0:T(8,128)(2,1)S(1)}, bf16[64,256]{1,0:T(8,128)(2,1)}, u32[]{:S(2)}) copy-start(bf16[64,256]{1,0:T(8,128)(2,1)} %param.21) | copy-start | bytes 98308
  6.5 28.1 %copy-start.11 = (f32[256]{0:T(256)S(1)}, f32[256]{0:T(256)}, u32[]{:S(2)}) copy-start(f32[256]{0:T(256)} %param.22) | copy-start | bytes 3076
  6.6 124.3 %all-gather.4.cloned.1.call-start = ((), (), s32[]{:S(2)}) async-start(), calls=%async_computation.5 | async-start | bytes 2820096 | tf_op jit(solution)/shard_map/all_gather | solution.py:127
  21.6 14.3 %copy-start.5 = (bf16[1152,256]{1,0:T(8,128)(2,1)S(1)}, bf16[1152,256]{1,0:T(8,128)(2,1)}, u32[]{:S(2)}) copy-start(bf16[1152,256]{1,0:T(8,128)(2,1)} %param.17) | copy-start | bytes 1769476
  34.6 1.8 copy-start.6
  36.4 3.7 %copy-start.4 = (f32[256]{0:T(256)S(1)}, f32[256]{0:T(256)}, u32[]{:S(2)}) copy-start(f32[256]{0:T(256)} %param.23) | copy-start | bytes 3076
  36.9 3.8 %copy-start.2 = (f32[256]{0:T(256)S(1)}, f32[256]{0:T(256)}, u32[]{:S(2)}) copy-start(f32[256]{0:T(256)} %param.24) | copy-start | bytes 3076
  41.8 38.7 %all-to-all-start = ((bf16[128,8,128]{2,1,0:T(8,128)(2,1)}), bf16[128,8,128]{2,1,0:T(8,128)(2,1)S(1)}, u32[]{:S(2)}, u32[]{:S(2)}) async-start(bf16[128,8,128]{2,1,0:T(8,128)(2,1)} %copy.101), calls=%async_computation | async-start | bytes 524288 | tf_op jit(solution)/shard_map/all_to_all | solution.py:157
  57.5 116.5 %all-gather.6.cloned.1.call-start = ((), (), s32[]{:S(2)}) async-start(), calls=%async_computation.6 | async-start | bytes 2820096 | tf_op jit(solution)/shard_map/all_gather | solution.py:128
  81.2 2.3 %copy-start.3 = (f32[256]{0:T(256)S(1)}, f32[256]{0:T(256)}, u32[]{:S(2)}) copy-start(f32[256]{0:T(256)} %param.25) | copy-start | bytes 3076
  82.7 38.9 %copy-start.10 = (f32[1152]{0:T(1024)S(1)}, f32[1152]{0:T(1024)}, u32[]{:S(2)}) copy-start(f32[1152]{0:T(1024)} %param.27) | copy-start | bytes 13828
  107.2 14.0 %all-to-all-start.2 = ((bf16[4,32,1152]{2,1,0:T(8,128)(2,1)}), bf16[4,32,1152]{2,1,0:T(8,128)(2,1)S(1)}, u32[]{:S(2)}, u32[]{:S(2)}) async-start(bf16[4,32,1152]{2,1,0:T(8,128)(2,1)} %bitcast.53), calls=%async_computation.2 | async-start | bytes 589824 | tf_op jit(solution)/shard_map/all_to_all | solution.py:26
Sparse Core Ops, SparseCore 0:
  22.5 78.9 all-gather.3
  103.5 70.3 all-gather.5

commit v2 on v1

--- a/solution.py
+++ b/solution.py
@@ -121,11 +121,13 @@
     planes, depth = lax.axis_size(PLANE), lax.axis_size("z")
     width = feature_mix_addressing_matrix.shape[0]
     pair = jnp.stack([feature_mix_addressing_matrix, feature_mix_content_matrix.T])
+    pair, whole_rows = lax.optimization_barrier((pair, whole_rows))
     plane_pair = from_everyone(pair, PLANE).reshape(planes, *pair.shape)
-    plane_up = plane_pair[:, 0].reshape(planes * width, -1)
-    plane_down = plane_pair[:, 1].reshape(planes * width, -1)
-    full_up = lax.all_gather(plane_up, "z", axis=0, tiled=True)
-    full_down = lax.all_gather(plane_down, "z", axis=0, tiled=True)
+    plane_pair = jnp.swapaxes(plane_pair, 0, 1).reshape(2 * planes * width, -1)
+    full_pair = lax.all_gather(plane_pair, "z", axis=0, tiled=True)
+    full_pair = full_pair.reshape(depth, 2, planes * width, -1)
+    full_up = full_pair[:, 0].reshape(model_width, -1)
+    full_down = full_pair[:, 1].reshape(model_width, -1)
 
     xn1 = layer_norm(whole_rows, initial_standardize_scaling)
     recept = jnp.dot(xn1, acceptance_matrix, preferred_element_type=jnp.float32).astype(

time: 207 us -> 156 us (0.75)
  waiting for transfers between devices: 69.8 us -> 6.88 us
  blocking collectives: 76.4 us -> 106 us
  starting transfers between devices: 22.8 us -> 6.59 us
  matrix products: 13.6 us -> 11.4 us
    all_gather x2 -> x1, waiting for transfers between devices: 40.7 us -> 0.01 us  [shards(): full_pair = lax.all_gather(plane_pair, 'z', axis=0, tiled=True)]
    all_to_all x0 -> x1, blocking collectives: none -> 38.6 us  [shards(): lax.all_to_all(sent.reshape(full_cols, 4 * inner_width // 128, 128), SEQ,...]
    all_to_all x1 -> x0, waiting for transfers between devices: 22.2 us -> none  [shards(): lax.all_to_all(sent.reshape(full_cols, 4 * inner_width // 128, 128), SEQ,...]
    all_to_all x1 -> x0, starting transfers between devices: 15.7 us -> none  [shards(): lax.all_to_all(sent.reshape(full_cols, 4 * inner_width // 128, 128), SEQ,...]
    all_to_all x1, blocking collectives: 21.4 us -> 11.2 us  [sent_and_summed(): pieces = lax.all_to_all(split_up(value, dim, size), axis, 0, 0, tiled=True)]
    all_gather x1, blocking collectives: 11.8 us -> 14.4 us  [shards(): whole_rows = lax.all_gather(tokens, MP, axis=0, tiled=True)]
    all_to_all x1, blocking collectives: 12.3 us -> 10.1 us  [from_everyone(): return lax.all_to_all(copies, axis, split_axis=0, concat_axis=0, tiled=True)]
  transfers between devices with their start and end apart: 4 -> 2, of which waited for: 3 -> 1; matrix products, arithmetic and copies ran while one was open for 8% -> 7% of each run, Pallas kernels for 0% -> 0%
where the time goes in v2:
time: 156 us; the launch traced here: 155 us
  blocking collectives  106 us (68%)
  between operations  13.9 us (9%)
  matrix products  11.4 us (7%)
  waiting for transfers between devices  6.88 us (4%)
  starting transfers between devices  6.59 us (4%)
  local copies, waits for them, and re-layouts  6.51 us (4%)
  other arithmetic  3.62 us (2%)
    all_to_all x1, blocking collectives, shards(): lax.all_to_all(sent.reshape(full_cols, 4 * inner_width // 128, 128), SEQ,...  38.6 us
    all_to_all x1, blocking collectives, shards(): lax.all_to_all(col_out.reshape(height, inner_width // 128, 128), SEQ, spl...  23.6 us
    all_gather x1, blocking collectives, shards(): whole_rows = lax.all_gather(tokens, MP, axis=0, tiled=True)  14.4 us
    all_to_all x1, blocking collectives, sent_and_summed(): pieces = lax.all_to_all(split_up(value, dim, size), axis, 0, 0, tiled=True)  11.2 us
    all_to_all x1, blocking collectives, from_everyone(): return lax.all_to_all(copies, axis, split_axis=0, concat_axis=0, tiled=True)  10.1 us
    all_gather x1, blocking collectives, shards(): mix_all = lax.all_gather(mix_input, MP, axis=0, tiled=True)  8.62 us
    all_to_all x1, waiting for transfers between devices, sent_and_summed(): pieces = lax.all_to_all(split_up(value, dim, size), axis, 0, 0, tiled=True)  6.87 us
    all_to_all x1, starting transfers between devices, sent_and_summed(): pieces = lax.all_to_all(split_up(value, dim, size), axis, 0, 0, tiled=True)  6.56 us
  transfers between devices with their start and end apart: 2, of which 1 were waited for; matrix products, arithmetic and copies ran while one was open for 7% of the time, Pallas kernels for 0%

profile of v2, /device:TPU:1, one launch (start us, length us, event | category | flops | bytes accessed | tf_op | source)
XLA Modules:
  0.0 155.4 jit_solution(13457779923798889176)
XLA Ops:
  6.6 14.4 %all-gather = bf16[1,1,128,1152]{3,2,1,0:T(8,128)(2,1)S(1)} all-gather(bf16[1,1,32,1152]{3,2,1,0:T(8,128)(2,1)} %param.15), channel_id=2, replica_groups=mesh['x_lo'=2,'y'=4,'z'=16,'x_hi'=2,'core'=2] {'x_hi','core'}, dimensions={2}, use_global_device_ids=true | all-gather | bytes 368640 | tf_op jit(solution)/shard_map/all_gather | solution.py:117
  21.0 0.8 pad_maximum_fusion.1
  21.8 0.2 broadcast_in_dim.42
  22.0 10.1 %all_to_all.25 = bf16[8,2,9,1152]{3,1,2,0:T(2,128)(2,1)S(1)} all-to-all(bf16[8,2,9,1152]{3,1,2,0:T(2,128)(2,1)S(1)} %broadcast_in_dim.42), channel_id=1, replica_groups=mesh['x_lo'=2,'y'=4,'z'=16,'x_hi'=2,'core'=2] {'x_lo','y'}, dimensions={0} | all-to-all | bytes 663552 | tf_op jit(solution)/shard_map/all_to_all | solution.py:15
  32.2 0.9 reshape.456
  33.2 0.1 convert_reduce_fusion
  33.4 0.2 fusion.25
  33.6 0.3 convolution_convert_fusion.2
  33.9 0.1 copy.99
  34.1 0.3 convolution_convert_fusion.3
  34.4 0.1 copy.97
  34.5 0.3 convolution_convert_fusion.4
  34.8 0.1 copy.93
  34.9 0.1 copy.94
  35.1 0.5 fusion.13
  35.6 0.1 copy.95
  35.7 0.1 copy.96
  35.9 0.3 reduce_window_sum.17
  36.1 0.1 copy.98
  36.5 1.2 convolution_select_fusion.1
  37.7 0.2 fusion.94
  38.0 0.1 copy.100
  38.1 0.1 multiply_reduce_fusion.2
  38.5 0.2 copy.102
  38.7 0.2 copy.103
  38.9 38.6 %all_to_all.26 = bf16[128,8,128]{2,1,0:T(8,128)(2,1)S(1)} all-to-all(bf16[128,8,128]{2,1,0:T(8,128)(2,1)S(1)} %copy.103), channel_id=1, replica_groups=mesh['x_lo'=2,'y'=4,'z'=16,'x_hi'=2,'core'=2] {'x_lo','y','z'}, dimensions={0} | all-to-all | bytes 524288 | tf_op jit(solution)/shard_map/all_to_all | solution.py:159
  77.5 0.2 copy.104
  77.8 0.1 copy.106
  77.9 0.3 reduce_window_sum.18
  78.2 0.1 copy.107
  78.4 0.1 copy.105
  78.5 1.2 convolution_select_fusion
  79.7 0.3 fusion.95
  80.0 0.1 copy.108
  80.1 0.1 fusion.54
  80.6 23.6 %all_to_all.27 = bf16[128,2,128]{2,1,0:T(2,128)(2,1)S(1)} all-to-all(bf16[128,2,128]{2,1,0:T(2,128)(2,1)S(1)} %copy.110), channel_id=1, replica_groups=mesh['x_lo'=2,'y'=4,'z'=16,'x_hi'=2,'core'=2] {'x_lo','y','z'}, dimensions={0} | all-to-all | bytes 131072 | tf_op jit(solution)/shard_map/all_to_all | solution.py:176
  104.2 1.0 convolution_convert_fusion.1
  105.2 6.6 %all-to-all-start.2 = ((bf16[4,32,1152]{2,1,0:T(8,128)(2,1)}), bf16[4,32,1152]{2,1,0:T(8,128)(2,1)S(1)}, u32[]{:S(2)}, u32[]{:S(2)}) async-start(bf16[4,32,1152]{2,1,0:T(8,128)(2,1)} %bitcast.56), calls=%async_computation.2 | async-start | bytes 589824 | tf_op jit(solution)/shard_map/all_to_all | solution.py:26
  111.8 6.9 %all-to-all-done.2 = bf16[4,32,1152]{2,1,0:T(8,128)(2,1)S(1)} async-done(((bf16[4,32,1152]{2,1,0:T(8,128)(2,1)}), bf16[4,32,1152]{2,1,0:T(8,128)(2,1)S(1)}, u32[]{:S(2)}, u32[]{:S(2)}) %all-to-all-start.2) | async-done | bytes 294944 | tf_op jit(solution)/shard_map/all_to_all | solution.py:26
  118.7 0.1 convert_reduce_fusion.3
  118.8 0.2 fusion.46
  119.0 1.1 fusion.7
  120.1 8.6 %all_gather.10 = bf16[128,1152]{1,0:T(8,128)(2,1)} all-gather(bf16[32,1152]{1,0:T(8,128)(2,1)S(1)} %fusion.7), channel_id=1, replica_groups=mesh['x_lo'=2,'y'=4,'z'=16,'x_hi'=2,'core'=2] {'x_hi','core'}, dimensions={0}, use_global_device_ids=true | all-gather | bytes 368640 | tf_op jit(solution)/shard_map/all_gather | solution.py:193
  128.8 3.0 %fusion.92 = (bf16[16,1,72,1152]{3,2,1,0:T(8,128)(2,1)S(1)}, bf16[16,1,72,1152]{3,2,1,0:T(8,128)(2,1)S(1)}) fusion(bf16[16,2,72,1152]{3,2,1,0:T(8,128)(2,1)} %bitcast.123), kind=kLoop, calls=%fused_computation.139 | loop fusion | bytes 10616832 | tf_op jit(solution)/shard_map/slice | solution.py:130
  131.8 1.3 fusion.5
  133.1 3.6 %fusion.6 = bf16[128,1152]{1,0:T(8,128)(2,1)} fusion(s32[1152]{0:T(1024)S(1)} %fusion.73, bf16[128,1152]{1,0:T(8,128)(2,1)} %fusion.5, bf16[1152,1152]{1,0:T(8,128)(2,1)S(1)} %bitcast.130), kind=kOutput, calls=%fused_computation.8 | convolution fusion | flops 681099264 | bytes 3248640 | tf_op jit(solution)/shard_map/dot_general | solution.py:200
  136.7 11.2 %all_to_all.28 = bf16[4,32,1152]{2,1,0:T(8,128)(2,1)S(1)} all-to-all(bf16[4,32,1152]{2,1,0:T(8,128)(2,1)} %bitcast.158), channel_id=1, replica_groups=mesh['x_lo'=2,'y'=4,'z'=16,'x_hi'=2,'core'=2] {'x_hi','core'}, dimensions={0} | all-to-all | bytes 589824 | tf_op jit(solution)/shard_map/all_to_all | solution.py:26
  147.9 0.7 fusion.52
  (66 shorter events, 1.3 us)
Async XLA Ops:
  6.5 97.7 %copy-start = (bf16[256,1152]{1,0:T(8,128)(2,1)S(1)}, bf16[256,1152]{1,0:T(8,128)(2,1)}, u32[]{:S(2)}) copy-start(bf16[256,1152]{1,0:T(8,128)(2,1)} %param.26) | copy-start | bytes 1769476
  6.5 26.6 %copy-start.5 = (f32[256]{0:T(256)S(1)}, f32[256]{0:T(256)}, u32[]{:S(2)}) copy-start(f32[256]{0:T(256)} %param.23) | copy-start | bytes 3076
  6.5 27.1 %copy-start.11 = (f32[1152]{0:T(1024)S(1)}, f32[1152]{0:T(1024)}, u32[]{:S(2)}) copy-start(f32[1152]{0:T(1024)} %param.16) | copy-start | bytes 13828
  6.5 27.1 %copy-start.6 = (bf16[1152,256]{1,0:T(8,128)(2,1)S(1)}, bf16[1152,256]{1,0:T(8,128)(2,1)}, u32[]{:S(2)}) copy-start(bf16[1152,256]{1,0:T(8,128)(2,1)} %param.19) | copy-start | bytes 1769476
  6.5 122.2 %all-gather.3.cloned.1.call-start = ((), (), s32[]{:S(2)}) async-start(), calls=%async_computation.5 | async-start | bytes 5640192 | tf_op jit(solution)/shard_map/all_gather | solution.py:127
  21.8 12.3 %copy-start.7 = (bf16[1152,256]{1,0:T(8,128)(2,1)S(1)}, bf16[1152,256]{1,0:T(8,128)(2,1)}, u32[]{:S(2)}) copy-start(bf16[1152,256]{1,0:T(8,128)(2,1)} %param.18) | copy-start | bytes 1769476
  32.2 2.3 %copy-start.8 = (bf16[1152,256]{1,0:T(8,128)(2,1)S(1)}, bf16[1152,256]{1,0:T(8,128)(2,1)}, u32[]{:S(2)}) copy-start(bf16[1152,256]{1,0:T(8,128)(2,1)} %param.17) | copy-start | bytes 1769476
  33.1 1.9 %copy-start.9 = (bf16[1152,64]{0,1:T(8,128)(2,1)S(1)}, bf16[1152,64]{0,1:T(8,128)(2,1)}, u32[]{:S(2)}) copy-start(bf16[1152,64]{0,1:T(8,128)(2,1)} %param.20) | copy-start | bytes 442372
  33.1 1.9 %copy-start.10 = (bf16[64,256]{1,0:T(8,128)(2,1)S(1)}, bf16[64,256]{1,0:T(8,128)(2,1)}, u32[]{:S(2)}) copy-start(bf16[64,256]{1,0:T(8,128)(2,1)} %param.21) | copy-start | bytes 98308
  33.1 2.0 %copy-start.13 = (f32[256]{0:T(256)S(1)}, f32[256]{0:T(256)}, u32[]{:S(2)}) copy-start(f32[256]{0:T(256)} %param.22) | copy-start | bytes 3076
  36.1 2.3 %copy-start.3 = (f32[256]{0:T(256)S(1)}, f32[256]{0:T(256)}, u32[]{:S(2)}) copy-start(f32[256]{0:T(256)} %param.24) | copy-start | bytes 3076
  78.2 2.3 %copy-start.4 = (f32[256]{0:T(256)S(1)}, f32[256]{0:T(256)}, u32[]{:S(2)}) copy-start(f32[256]{0:T(256)} %param.25) | copy-start | bytes 3076
  79.7 38.9 %copy-start.2 = (bf16[1,1,32,1152]{3,2,1,0:T(8,128)(2,1)S(1)}, bf16[1,1,32,1152]{3,2,1,0:T(8,128)(2,1)}, u32[]{:S(2)}) copy-start(bf16[1,1,32,1152]{3,2,1,0:T(8,128)(2,1)} %param.15) | copy-start | bytes 221188
  79.7 39.3 %copy-start.12 = (f32[1152]{0:T(1024)S(1)}, f32[1152]{0:T(1024)}, u32[]{:S(2)}) copy-start(f32[1152]{0:T(1024)} %param.27) | copy-start | bytes 13828
  105.2 13.4 %all-to-all-start.2 = ((bf16[4,32,1152]{2,1,0:T(8,128)(2,1)}), bf16[4,32,1152]{2,1,0:T(8,128)(2,1)S(1)}, u32[]{:S(2)}, u32[]{:S(2)}) async-start(bf16[4,32,1152]{2,1,0:T(8,128)(2,1)} %bitcast.56), calls=%async_computation.2 | async-start | bytes 589824 | tf_op jit(solution)/shard_map/all_to_all | solution.py:26
  128.8 3.0 %copy-start.1 = (bf16[128,1152]{1,0:T(8,128)(2,1)S(1)}, bf16[128,1152]{1,0:T(8,128)(2,1)}, u32[]{:S(2)}) copy-start(bf16[128,1152]{1,0:T(8,128)(2,1)} %all_gather.10) | copy-start | bytes 884740
Sparse Core Ops, SparseCore 0:
  33.3 88.0 all-gather.2

commit v3 on v2

--- a/solution.py
+++ b/solution.py
@@ -3,6 +3,7 @@
 from jax import lax
 from jax.sharding import Mesh
 from jax.sharding import PartitionSpec as P
+
 
 SUBSPACE_SIZE = 64
 SEQ = ("x_lo", "y", "z")
@@ -121,8 +122,8 @@
     planes, depth = lax.axis_size(PLANE), lax.axis_size("z")
     width = feature_mix_addressing_matrix.shape[0]
     pair = jnp.stack([feature_mix_addressing_matrix, feature_mix_content_matrix.T])
-    pair, whole_rows = lax.optimization_barrier((pair, whole_rows))
-    plane_pair = from_everyone(pair, PLANE).reshape(planes, *pair.shape)
+    plane_pair = from_everyone(pair, PLANE)
+    plane_pair = plane_pair.reshape(planes, *pair.shape)
     plane_pair = jnp.swapaxes(plane_pair, 0, 1).reshape(2 * planes * width, -1)
     full_pair = lax.all_gather(plane_pair, "z", axis=0, tiled=True)
     full_pair = full_pair.reshape(depth, 2, planes * width, -1)
@@ -156,13 +157,12 @@
         horizontal_cluster_scaling,
     )[0]
     sent = jnp.stack([recept, keying, decay, row_out], axis=1)
-    got = lax.all_to_all(
-        sent.reshape(full_cols, 4 * inner_width // 128, 128),
-        SEQ,
-        split_axis=0,
-        concat_axis=0,
-        tiled=True,
-    )
+    sent = sent.reshape(full_cols, 4 * inner_width // 128, 128)
+    sent, own_projection = lax.optimization_barrier((sent, temporal_mix_projection_matrix))
+    got = lax.all_to_all(sent, SEQ, split_axis=0, concat_axis=0, tiled=True)
+    projection = [own_projection]
+    for k in range(1, 4):
+        projection.append(lax.ppermute(own_projection, MP, [(i, i ^ k) for i in range(4)]))
     height = got.shape[0]
     got = got.reshape(height, 4, inner_width)
     col_out = recurrence(
@@ -180,18 +180,20 @@
         concat_axis=0,
         tiled=True,
     ).reshape(full_cols, inner_width)
-    partial_value = jnp.dot(
-        back, temporal_mix_projection_matrix, preferred_element_type=jnp.float32
-    ).astype(jnp.bfloat16)
-    attended = sent_and_summed(partial_value, MP, 0)
-    residual = (tokens.astype(jnp.float32) + attended).astype(jnp.bfloat16)
-    mix_input = layer_norm(residual, later_standardize_scaling)
+    group = lax.axis_index(MP)
+    groups = lax.all_gather(back, MP, axis=0, tiled=False)
+    attended = jnp.zeros((full_cols, model_width), jnp.float32)
+    for k in range(4):
+        one = lax.dynamic_index_in_dim(groups, group ^ k, 0, keepdims=False)
+        attended = attended + jnp.dot(one, projection[k], preferred_element_type=jnp.float32)
+    residual_all = (whole_rows.astype(jnp.float32) + attended).astype(jnp.bfloat16)
+    residual = lax.dynamic_slice_in_dim(residual_all, group * part_cols, part_cols, 0)
+    mix_input = layer_norm(residual_all, later_standardize_scaling)
 
     places = unit_order(planes, depth, width)
     moved = (jnp.arange(model_width)[:, None] == places[None, :]).astype(jnp.bfloat16)
     mix_input = jnp.dot(mix_input, moved, preferred_element_type=jnp.float32).astype(jnp.bfloat16)
-    mix_all = lax.all_gather(mix_input, MP, axis=0, tiled=True)
-    hidden_pre = jnp.dot(mix_all, full_up, preferred_element_type=jnp.float32)
+    hidden_pre = jnp.dot(mix_input, full_up, preferred_element_type=jnp.float32)
     positive = jnp.maximum(hidden_pre, 0.0)
     hidden = (positive * positive).astype(jnp.bfloat16)
     downward = lax.dot_general(

time: 156 us -> 157 us (level)
  blocking collectives: 106 us -> 83.4 us
  starting transfers between devices: 6.59 us -> 21.7 us
  waiting for transfers between devices: 6.88 us -> 11.4 us
  local copies, waits for them, and re-layouts: 6.51 us -> 9.29 us
  matrix products: 11.4 us -> 13.2 us
    all_to_all x3 -> x1, blocking collectives: 73.3 us -> 39.3 us  [shards(): got = lax.all_to_all(sent, SEQ, split_axis=0, concat_axis=0, tiled=True)]
    all_gather x1, blocking collectives: 8.62 us -> 19.9 us  [shards(): groups = lax.all_gather(back, MP, axis=0, tiled=False)]
    ppermute x0 -> x3, starting transfers between devices: none -> 10.1 us  [shards(): lax.ppermute(own_projection, MP, [(i, i ^ k) for i in range(4)])]
    all_to_all x0 -> x1, starting transfers between devices: none -> 8.04 us  [shards(): lax.all_to_all(col_out.reshape(height, inner_width // 128, 128), SEQ, spl...]
    all_to_all x0 -> x1, waiting for transfers between devices: none -> 4.41 us  [shards(): lax.all_to_all(col_out.reshape(height, inner_width // 128, 128), SEQ, spl...]
    all_to_all x1, starting transfers between devices: 6.56 us -> 3.59 us  [sent_and_summed(): pieces = lax.all_to_all(split_up(value, dim, size), axis, 0, 0, tiled=True)]
    all_gather x1, blocking collectives: 14.4 us -> 11.8 us  [shards(): whole_rows = lax.all_gather(tokens, MP, axis=0, tiled=True)]
    all_to_all x1, blocking collectives: 10.1 us -> 12.3 us  [from_everyone(): return lax.all_to_all(copies, axis, split_axis=0, concat_axis=0, tiled=True)]
  transfers between devices with their start and end apart: 2 -> 6, of which waited for: 1 -> 2; matrix products, arithmetic and copies ran while one was open for 7% -> 7% of each run, Pallas kernels for 0% -> 0%
where the time goes in v3:
time: 157 us
  blocking collectives  83.4 us (53%)
  starting transfers between devices  21.7 us (14%)
  between operations  14 us (9%)
  matrix products  13.2 us (8%)
  waiting for transfers between devices  11.4 us (7%)
  local copies, waits for them, and re-layouts  9.29 us (6%)
  other arithmetic  3.54 us (2%)
    all_to_all x1, blocking collectives, shards(): got = lax.all_to_all(sent, SEQ, split_axis=0, concat_axis=0, tiled=True)  39.3 us
    all_gather x1, blocking collectives, shards(): groups = lax.all_gather(back, MP, axis=0, tiled=False)  19.9 us
    all_to_all x1, blocking collectives, from_everyone(): return lax.all_to_all(copies, axis, split_axis=0, concat_axis=0, tiled=True)  12.3 us
    all_gather x1, blocking collectives, shards(): whole_rows = lax.all_gather(tokens, MP, axis=0, tiled=True)  11.8 us
    ppermute x3, starting transfers between devices, shards(): lax.ppermute(own_projection, MP, [(i, i ^ k) for i in range(4)])  10.1 us
    all_to_all x1, starting transfers between devices, shards(): lax.all_to_all(col_out.reshape(height, inner_width // 128, 128), SEQ, spl...  8.04 us
    all_to_all x1, waiting for transfers between devices, sent_and_summed(): pieces = lax.all_to_all(split_up(value, dim, size), axis, 0, 0, tiled=True)  6.9 us
    slice x1, local copies, waits for them, and re-layouts, shards(): full_down = full_pair[:, 1].reshape(model_width, -1)  4.48 us
  transfers between devices with their start and end apart: 6, of which 2 were waited for; matrix products, arithmetic and copies ran while one was open for 7% of the time, Pallas kernels for 0%

profile of v3, /device:TPU:1, one launch (start us, length us, event | category | flops | bytes accessed | tf_op | source)
XLA Modules:
  0.0 156.5 jit_solution(16406122255744322206)
XLA Ops:
  6.6 0.9 pad_maximum_fusion.1
  7.5 0.2 broadcast_in_dim.42
  7.7 12.3 %all_to_all.20 = bf16[8,2,9,1152]{3,1,2,0:T(2,128)(2,1)S(1)} all-to-all(bf16[8,2,9,1152]{3,1,2,0:T(2,128)(2,1)S(1)} %broadcast_in_dim.42), channel_id=1, replica_groups=mesh['x_lo'=2,'y'=4,'z'=16,'x_hi'=2,'core'=2] {'x_lo','y'}, dimensions={0} | all-to-all | bytes 663552 | tf_op jit(solution)/shard_map/all_to_all | solution.py:16
  20.1 0.9 reshape.448
  21.0 11.8 %all-gather = bf16[1,1,128,1152]{3,2,1,0:T(8,128)(2,1)S(1)} all-gather(bf16[1,1,32,1152]{3,2,1,0:T(8,128)(2,1)S(1)} %copy-done.2), channel_id=2, replica_groups=mesh['x_lo'=2,'y'=4,'z'=16,'x_hi'=2,'core'=2] {'x_hi','core'}, dimensions={2}, use_global_device_ids=true | all-gather | bytes 368640 | tf_op jit(solution)/shard_map/all_gather | solution.py:118
  32.9 0.1 convert_reduce_fusion
  33.0 0.2 fusion.31
  33.3 0.5 fusion.16
  34.0 0.1 copy.96
  34.1 0.3 reduce_window_sum.17
  34.5 0.3 convolution_convert_fusion.2
  35.0 0.3 convolution_convert_fusion.3
  35.4 0.1 copy.94
  35.5 0.3 convolution_convert_fusion.1
  35.9 0.1 copy.99
  36.2 1.2 convolution_select_fusion.1
  37.4 0.3 fusion.110
  37.7 0.1 copy.100
  37.9 0.1 multiply_reduce_fusion.2
  38.3 0.2 copy.102
  38.5 0.2 copy.103
  38.7 39.3 %all_to_all.21 = bf16[128,8,128]{2,1,0:T(8,128)(2,1)S(1)} all-to-all(bf16[128,8,128]{2,1,0:T(8,128)(2,1)S(1)} %copy.103), channel_id=1, replica_groups=mesh['x_lo'=2,'y'=4,'z'=16,'x_hi'=2,'core'=2] {'x_lo','y','z'}, dimensions={0} | all-to-all | bytes 524288 | tf_op jit(solution)/shard_map/all_to_all | solution.py:162
  78.0 0.2 copy.104
  78.4 0.3 reduce_window_sum.18
  78.9 0.1 copy.105
  79.0 1.2 convolution_select_fusion
  80.3 0.3 fusion.111
  80.5 0.1 copy.108
  80.6 0.1 fusion.62
  81.0 0.7 copy.110
  81.7 8.0 %all-to-all-start.1 = ((bf16[128,2,128]{2,1,0:T(2,128)(2,1)}), bf16[128,2,128]{2,1,0:T(2,128)(2,1)S(1)}, u32[]{:S(2)}, u32[]{:S(2)}) async-start(bf16[128,2,128]{2,1,0:T(2,128)(2,1)} %copy.110), calls=%async_computation.1 | async-start | bytes 131072 | tf_op jit(solution)/shard_map/all_to_all | solution.py:176
  89.8 5.5 %collective-permute-start.2 = (bf16[256,1152]{1,0:T(8,128)(2,1)S(1)}, bf16[256,1152]{1,0:T(8,128)(2,1)S(1)}, u32[]{:S(2)}, u32[]{:S(2)}) collective-permute-start(bf16[256,1152]{1,0:T(8,128)(2,1)S(1)} %copy-done.1), channel_id=1, source_target_pairs={{0,3},{1,2},{2,1},{3,0},{4,7},{5,6},{6,5},{7,4},{8,11},{9,10},{10,... | collective-permute-start | bytes 1769480 | tf_op jit(solution)/shard_map/ppermute | solution.py:165
  95.3 1.9 %collective-permute-start = (bf16[256,1152]{1,0:T(8,128)(2,1)S(1)}, bf16[256,1152]{1,0:T(8,128)(2,1)S(1)}, u32[]{:S(2)}, u32[]{:S(2)}) collective-permute-start(bf16[256,1152]{1,0:T(8,128)(2,1)S(1)} %copy-done.1), channel_id=1, source_target_pairs={{0,1},{1,0},{2,3},{3,2},{4,5},{5,4},{6,7},{7,6},{8,9},{9,8},{10,11... | collective-permute-start | bytes 1769480 | tf_op jit(solution)/shard_map/ppermute | solution.py:165
  97.3 2.6 %collective-permute-start.1 = (bf16[256,1152]{1,0:T(8,128)(2,1)S(1)}, bf16[256,1152]{1,0:T(8,128)(2,1)S(1)}, u32[]{:S(2)}, u32[]{:S(2)}) collective-permute-start(bf16[256,1152]{1,0:T(8,128)(2,1)S(1)} %copy-done.1), channel_id=1, source_target_pairs={{0,2},{1,3},{2,0},{3,1},{4,6},{5,7},{6,4},{7,5},{8,10},{9,11},{10,... | collective-permute-start | bytes 1769480 | tf_op jit(solution)/shard_map/ppermute | solution.py:165
  99.9 4.4 %all-to-all-done.1 = bf16[128,2,128]{2,1,0:T(2,128)(2,1)S(1)} async-done(((bf16[128,2,128]{2,1,0:T(2,128)(2,1)}), bf16[128,2,128]{2,1,0:T(2,128)(2,1)S(1)}, u32[]{:S(2)}, u32[]{:S(2)}) %all-to-all-start.1) | async-done | bytes 65568 | tf_op jit(solution)/shard_map/all_to_all | solution.py:176
  104.4 0.7 all_gather_reshape.3
  105.0 19.9 %all_gather.10 = bf16[4,128,256]{2,1,0:T(8,128)(2,1)S(1)} all-gather(bf16[1,128,256]{2,1,0:T(8,128)(2,1)} %all_gather_reshape.3), channel_id=1, replica_groups=mesh['x_lo'=2,'y'=4,'z'=16,'x_hi'=2,'core'=2] {'x_hi','core'}, dimensions={0}, use_global_device_ids=true | all-gather | bytes 327680 | tf_op jit(solution)/shard_map/all_gather | solution.py:184
  124.9 0.2 fusion.70
  125.2 0.2 fusion.66
  125.4 0.3 convolution_add_fusion.1
  125.7 0.4 convert_reduce_fusion.1
  126.1 0.2 fusion.34
  126.3 4.5 %fusion.108 = (bf16[16,1,72,1152]{3,2,1,0:T(8,128)(2,1)S(1)}, bf16[16,1,72,1152]{3,2,1,0:T(8,128)(2,1)}) fusion(bf16[16,2,72,1152]{3,2,1,0:T(8,128)(2,1)} %bitcast.140), kind=kLoop, calls=%fused_computation.150 | loop fusion | bytes 10616832 | tf_op jit(solution)/shard_map/slice | solution.py:131
  130.8 4.1 %fusion.8 = bf16[128,1152]{1,0:T(8,128)(2,1)} fusion(bf16[1152,1152]{1,0:T(8,128)(2,1)} %bitcast.142, s32[1152]{0:T(1024)S(1)} %fusion.86, bf16[128,1152]{1,0:T(8,128)(2,1)S(1)} %get-tuple-element.18, f32[1152]{0:T(1024)} %param.27, f32[128]{0:T(128)S(1)} %add_rsqrt_fusion.2, f32[128]{0:T(128)S(1)} %broadcast_multiply_fusion.2), kind=kOutput, calls=%fused_computation.12 | convolution fusion | flops 682131456 | bytes 3254272 | tf_op jit(solution)/shard_map/dot_general | solution.py:196
  135.0 3.6 %fusion.10 = bf16[128,1152]{1,0:T(8,128)(2,1)} fusion(s32[1152]{0:T(1024)S(1)} %fusion.86, bf16[128,1152]{1,0:T(8,128)(2,1)} %fusion.8, bf16[1152,1152]{1,0:T(8,128)(2,1)S(1)} %bitcast.141), kind=kOutput, calls=%fused_computation.14 | convolution fusion | flops 681099264 | bytes 3248640 | tf_op jit(solution)/shard_map/dot_general | solution.py:202
  138.5 3.6 %all-to-all-start.3 = ((bf16[4,32,1152]{2,1,0:T(8,128)(2,1)}), bf16[4,32,1152]{2,1,0:T(8,128)(2,1)S(1)}, u32[]{:S(2)}, u32[]{:S(2)}) async-start(bf16[4,32,1152]{2,1,0:T(8,128)(2,1)} %bitcast.170), calls=%async_computation.3 | async-start | bytes 589824 | tf_op jit(solution)/shard_map/all_to_all | solution.py:27
  142.1 6.9 %all-to-all-done.3 = bf16[4,32,1152]{2,1,0:T(8,128)(2,1)S(1)} async-done(((bf16[4,32,1152]{2,1,0:T(8,128)(2,1)}), bf16[4,32,1152]{2,1,0:T(8,128)(2,1)S(1)}, u32[]{:S(2)}, u32[]{:S(2)}) %all-to-all-start.3) | async-done | bytes 294944 | tf_op jit(solution)/shard_map/all_to_all | solution.py:27
  149.0 0.7 fusion.65
  (69 shorter events, 1.8 us)
Async XLA Ops:
  6.5 28.0 %copy-start = (bf16[1152,256]{1,0:T(8,128)(2,1)S(1)}, bf16[1152,256]{1,0:T(8,128)(2,1)}, u32[]{:S(2)}) copy-start(bf16[1152,256]{1,0:T(8,128)(2,1)} %param.18) | copy-start | bytes 1769476
  6.5 14.5 %copy-start.2 = (bf16[1,1,32,1152]{3,2,1,0:T(8,128)(2,1)S(1)}, bf16[1,1,32,1152]{3,2,1,0:T(8,128)(2,1)}, u32[]{:S(2)}) copy-start(bf16[1,1,32,1152]{3,2,1,0:T(8,128)(2,1)} %param.15) | copy-start | bytes 221188
  6.5 26.7 %copy-start.9 = (bf16[64,256]{1,0:T(8,128)(2,1)S(1)}, bf16[64,256]{1,0:T(8,128)(2,1)}, u32[]{:S(2)}) copy-start(bf16[64,256]{1,0:T(8,128)(2,1)} %param.21) | copy-start | bytes 98308
  6.5 26.7 %copy-start.8 = (bf16[1152,64]{0,1:T(8,128)(2,1)S(1)}, bf16[1152,64]{0,1:T(8,128)(2,1)}, u32[]{:S(2)}) copy-start(bf16[1152,64]{0,1:T(8,128)(2,1)} %param.20) | copy-start | bytes 442372
  6.5 26.7 %copy-start.11 = (f32[256]{0:T(256)S(1)}, f32[256]{0:T(256)}, u32[]{:S(2)}) copy-start(f32[256]{0:T(256)} %param.22) | copy-start | bytes 3076
  6.5 26.7 %copy-start.10 = (f32[1152]{0:T(1024)S(1)}, f32[1152]{0:T(1024)}, u32[]{:S(2)}) copy-start(f32[1152]{0:T(1024)} %param.16) | copy-start | bytes 13828
  6.6 119.8 %all-gather.3.cloned.1.call-start = ((), (), s32[]{:S(2)}) async-start(), calls=%async_computation.4 | async-start | bytes 5640192 | tf_op jit(solution)/shard_map/all_gather | solution.py:128
  33.0 1.9 %copy-start.6 = (bf16[1152,256]{1,0:T(8,128)(2,1)S(1)}, bf16[1152,256]{1,0:T(8,128)(2,1)}, u32[]{:S(2)}) copy-start(bf16[1152,256]{1,0:T(8,128)(2,1)} %param.17) | copy-start | bytes 1769476
  33.9 1.6 %copy-start.7 = (bf16[1152,256]{1,0:T(8,128)(2,1)S(1)}, bf16[1152,256]{1,0:T(8,128)(2,1)}, u32[]{:S(2)}) copy-start(bf16[1152,256]{1,0:T(8,128)(2,1)} %param.19) | copy-start | bytes 1769476
  35.0 2.8 %copy-start.5 = (f32[256]{0:T(256)S(1)}, f32[256]{0:T(256)}, u32[]{:S(2)}) copy-start(f32[256]{0:T(256)} %param.23) | copy-start | bytes 3076
  35.5 2.7 %copy-start.3 = (f32[256]{0:T(256)S(1)}, f32[256]{0:T(256)}, u32[]{:S(2)}) copy-start(f32[256]{0:T(256)} %param.24) | copy-start | bytes 3076
  78.7 2.3 %copy-start.4 = (f32[256]{0:T(256)S(1)}, f32[256]{0:T(256)}, u32[]{:S(2)}) copy-start(f32[256]{0:T(256)} %param.25) | copy-start | bytes 3076
  78.8 11.0 %copy-start.1 = (bf16[256,1152]{1,0:T(8,128)(2,1)S(1)}, bf16[256,1152]{1,0:T(8,128)(2,1)}, u32[]{:S(2)}) copy-start(bf16[256,1152]{1,0:T(8,128)(2,1)} %param.26) | copy-start | bytes 1769476
  81.7 22.6 %all-to-all-start.1 = ((bf16[128,2,128]{2,1,0:T(2,128)(2,1)}), bf16[128,2,128]{2,1,0:T(2,128)(2,1)S(1)}, u32[]{:S(2)}, u32[]{:S(2)}) async-start(bf16[128,2,128]{2,1,0:T(2,128)(2,1)} %copy.110), calls=%async_computation.1 | async-start | bytes 131072 | tf_op jit(solution)/shard_map/all_to_all | solution.py:176
  89.8 35.4 %collective-permute-start.2 = (bf16[256,1152]{1,0:T(8,128)(2,1)S(1)}, bf16[256,1152]{1,0:T(8,128)(2,1)S(1)}, u32[]{:S(2)}, u32[]{:S(2)}) collective-permute-start(bf16[256,1152]{1,0:T(8,128)(2,1)S(1)} %copy-done.1), channel_id=1, source_target_pairs={{0,3},{1,2},{2,1},{3,0},{4,7},{5,6},{6,5},{7,4},{8,11},{9,10},{10,... | collective-permute-start | bytes 1769480 | tf_op jit(solution)/shard_map/ppermute | solution.py:165
  95.3 30.1 %collective-permute-start = (bf16[256,1152]{1,0:T(8,128)(2,1)S(1)}, bf16[256,1152]{1,0:T(8,128)(2,1)S(1)}, u32[]{:S(2)}, u32[]{:S(2)}) collective-permute-start(bf16[256,1152]{1,0:T(8,128)(2,1)S(1)} %copy-done.1), channel_id=1, source_target_pairs={{0,1},{1,0},{2,3},{3,2},{4,5},{5,4},{6,7},{7,6},{8,9},{9,8},{10,11... | collective-permute-start | bytes 1769480 | tf_op jit(solution)/shard_map/ppermute | solution.py:165
  97.3 28.4 %collective-permute-start.1 = (bf16[256,1152]{1,0:T(8,128)(2,1)S(1)}, bf16[256,1152]{1,0:T(8,128)(2,1)S(1)}, u32[]{:S(2)}, u32[]{:S(2)}) collective-permute-start(bf16[256,1152]{1,0:T(8,128)(2,1)S(1)} %copy-done.1), channel_id=1, source_target_pairs={{0,2},{1,3},{2,0},{3,1},{4,6},{5,7},{6,4},{7,5},{8,10},{9,11},{10,... | collective-permute-start | bytes 1769480 | tf_op jit(solution)/shard_map/ppermute | solution.py:165
  138.5 10.5 %all-to-all-start.3 = ((bf16[4,32,1152]{2,1,0:T(8,128)(2,1)}), bf16[4,32,1152]{2,1,0:T(8,128)(2,1)S(1)}, u32[]{:S(2)}, u32[]{:S(2)}) async-start(bf16[4,32,1152]{2,1,0:T(8,128)(2,1)} %bitcast.170), calls=%async_computation.3 | async-start | bytes 589824 | tf_op jit(solution)/shard_map/all_to_all | solution.py:27
Sparse Core Ops, SparseCore 0:
  21.1 92.0 all-gather.2

commit v4 on v1

--- a/solution.py
+++ b/solution.py
@@ -4,10 +4,11 @@
 from jax.sharding import Mesh
 from jax.sharding import PartitionSpec as P
 
+
 SUBSPACE_SIZE = 64
 SEQ = ("x_lo", "y", "z")
 MP = ("x_hi", "core")
-PLANE = ("x_lo", "y")
+MIX = ("x_lo", "x_hi", "core")
 
 
 def from_everyone(value, axis):
@@ -87,12 +88,14 @@
     return (normed * gain).astype(jnp.bfloat16)
 
 
-def unit_order(planes, depth, width):
-    stored = jnp.arange(planes * depth * width)
-    z, rest = stored // (planes * width), stored % (planes * width)
-    plane, row = rest // width, rest % width
-    true_place = (plane * depth + z) * width + row
-    return true_place
+def unit_order(depth, width):
+    ring = lax.axis_size("y")
+    stored = jnp.arange(2 * ring * depth * width)
+    turn, rest = stored // (2 * depth * width), stored % (2 * depth * width)
+    z, rest = rest // (2 * width), rest % (2 * width)
+    x = rest // width
+    y = (turn + lax.axis_index("y")) % ring
+    return ((x * ring + y) * depth + z) * width + rest % width
 
 
 def shards(
@@ -118,14 +121,25 @@
     full_cols = whole_rows.shape[0]
     inner_width = acceptance_matrix.shape[1]
 
-    planes, depth = lax.axis_size(PLANE), lax.axis_size("z")
-    width = feature_mix_addressing_matrix.shape[0]
-    pair = jnp.stack([feature_mix_addressing_matrix, feature_mix_content_matrix.T])
-    plane_pair = from_everyone(pair, PLANE).reshape(planes, *pair.shape)
-    plane_up = plane_pair[:, 0].reshape(planes * width, -1)
-    plane_down = plane_pair[:, 1].reshape(planes * width, -1)
-    full_up = lax.all_gather(plane_up, "z", axis=0, tiled=True)
-    full_down = lax.all_gather(plane_down, "z", axis=0, tiled=True)
+    depth = lax.axis_size("z")
+    width, units = feature_mix_addressing_matrix.shape
+    first_half = lax.axis_index("x_lo") == 0
+    halves = [
+        jnp.concatenate(
+            [
+                feature_mix_addressing_matrix[:, start : start + units // 2],
+                feature_mix_content_matrix.T[:, start : start + units // 2],
+            ],
+            axis=1,
+        )
+        for start in (0, units // 2)
+    ]
+    kept = jnp.where(first_half, halves[0], halves[1])
+    given = jnp.where(first_half, halves[1], halves[0])
+    received = lax.ppermute(given, "x_lo", [(0, 1), (1, 0)])
+    pair = jnp.concatenate(
+        [jnp.where(first_half, kept, received), jnp.where(first_half, received, kept)], axis=0
+    )
 
     xn1 = layer_norm(whole_rows, initial_standardize_scaling)
     recept = jnp.dot(xn1, acceptance_matrix, preferred_element_type=jnp.float32).astype(
@@ -154,13 +168,10 @@
         horizontal_cluster_scaling,
     )[0]
     sent = jnp.stack([recept, keying, decay, row_out], axis=1)
-    got = lax.all_to_all(
-        sent.reshape(full_cols, 4 * inner_width // 128, 128),
-        SEQ,
-        split_axis=0,
-        concat_axis=0,
-        tiled=True,
-    )
+    sent = sent.reshape(full_cols, 4 * inner_width // 128, 128)
+    sent, pair = lax.optimization_barrier((sent, pair))
+    got = lax.all_to_all(sent, SEQ, split_axis=0, concat_axis=0, tiled=True)
+    ring_pair = lax.all_gather(pair, "z", axis=0, tiled=True)
     height = got.shape[0]
     got = got.reshape(height, 4, inner_width)
     col_out = recurrence(
@@ -171,13 +182,13 @@
         self_token_reward,
         vertical_cluster_scaling,
     )[0]
-    back = lax.all_to_all(
-        col_out.reshape(height, inner_width // 128, 128),
-        SEQ,
-        split_axis=0,
-        concat_axis=0,
-        tiled=True,
-    ).reshape(full_cols, inner_width)
+    col_sent = col_out.reshape(height, inner_width // 128, 128)
+    col_sent, ring_pair = lax.optimization_barrier((col_sent, ring_pair))
+    back = lax.all_to_all(col_sent, SEQ, split_axis=0, concat_axis=0, tiled=True)
+    back = back.reshape(full_cols, inner_width)
+    pieces = [ring_pair]
+    for k in range(1, 4):
+        pieces.append(lax.ppermute(ring_pair, "y", [(i, (i - k) % 4) for i in range(4)]))
     partial_value = jnp.dot(
         back, temporal_mix_projection_matrix, preferred_element_type=jnp.float32
     ).astype(jnp.bfloat16)
@@ -185,20 +196,22 @@
     residual = (tokens.astype(jnp.float32) + attended).astype(jnp.bfloat16)
     mix_input = layer_norm(residual, later_standardize_scaling)
 
-    places = unit_order(planes, depth, width)
+    places = unit_order(depth, width)
     moved = (jnp.arange(model_width)[:, None] == places[None, :]).astype(jnp.bfloat16)
     mix_input = jnp.dot(mix_input, moved, preferred_element_type=jnp.float32).astype(jnp.bfloat16)
-    mix_all = lax.all_gather(mix_input, MP, axis=0, tiled=True)
-    hidden_pre = jnp.dot(mix_all, full_up, preferred_element_type=jnp.float32)
-    positive = jnp.maximum(hidden_pre, 0.0)
+    mix_all = from_everyone(mix_input, MIX).reshape(-1, model_width)
+    weights = jnp.concatenate(pieces, axis=0)
+    hidden_pre = jnp.dot(mix_all, weights, preferred_element_type=jnp.float32)
+    positive = jnp.maximum(hidden_pre[:, : units // 2], 0.0)
     hidden = (positive * positive).astype(jnp.bfloat16)
+    hidden = jnp.pad(hidden, ((0, 0), (units // 2, 0)))
     downward = lax.dot_general(
-        hidden, full_down, (((1,), (1,)), ((), ())), preferred_element_type=jnp.float32
+        hidden, weights, (((1,), (1,)), ((), ())), preferred_element_type=jnp.float32
     ).astype(jnp.bfloat16)
     downward = lax.dot_general(
         downward, moved, (((1,), (1,)), ((), ())), preferred_element_type=jnp.float32
     ).astype(jnp.bfloat16)
-    mixed = sent_and_summed(downward, MP, 0)
+    mixed = sent_and_summed(downward, MIX, 0)
     block_out = (residual.astype(jnp.float32) + mixed).astype(jnp.bfloat16)
     return block_out.reshape(images, row_count, part_cols, model_width)
 

time: 207 us -> 170 us (0.82)
  waiting for transfers between devices: 69.8 us -> 17 us
  starting transfers between devices: 22.8 us -> 61.4 us
  blocking collectives: 76.4 us -> 62.3 us
  between operations: 13.9 us -> 0.52 us
  local copies, waits for them, and re-layouts: 6.29 us -> 9.7 us
    all_gather x2 -> x0, waiting for transfers between devices: 40.7 us -> none  [the longest x1 40.7 us: shards(): full_down = lax.all_gather(plane_down, 'z', axis=0, tiled=True)]
    all_to_all x2 -> x0, blocking collectives: 35 us -> none  [the longest x1 22.7 us: shards(): lax.all_to_all(col_out.reshape(height, inner_width // 128, 128), SEQ, spl...]
    all_gather x1, blocking collectives: 8.17 us -> 36 us  [shards(): ring_pair = lax.all_gather(pair, 'z', axis=0, tiled=True)]
    all_to_all x1 -> x3, starting transfers between devices: 15.7 us -> 36.4 us  [the longest x1 15.8 us: shards(): got = lax.all_to_all(sent, SEQ, split_axis=0, concat_axis=0, tiled=True)]
    ppermute x0 -> x4, starting transfers between devices: none -> 12.7 us  [the longest x3 8.76 us: shards(): lax.ppermute(ring_pair, 'y', [(i, (i - k) % 4) for i in range(4)])]
    all_to_all x1 -> x3, waiting for transfers between devices: 22.2 us -> 11 us  [the longest x1 5.66 us: from_everyone(): return lax.all_to_all(copies, axis, split_axis=0, concat_axis=0, tiled=True)]
    all_to_all x1, blocking collectives: 21.4 us -> 14.1 us  [sent_and_summed(): pieces = lax.all_to_all(split_up(value, dim, size), axis, 0, 0, tiled=True)]
    all_to_all x1, starting transfers between devices: 7.09 us -> 12.2 us  [sent_and_summed(): pieces = lax.all_to_all(split_up(value, dim, size), axis, 0, 0, tiled=True)]
  transfers between devices with their start and end apart: 4 -> 8, of which waited for: 3 -> 3; matrix products, arithmetic and copies ran while one was open for 8% -> 9% of each run, Pallas kernels for 0% -> 0%
where the time goes in v4:
time: 170 us; the launch traced here: 169 us
  blocking collectives  62.3 us (37%)
  starting transfers between devices  61.4 us (36%)
  waiting for transfers between devices  17 us (10%)
  matrix products  14.5 us (9%)
  local copies, waits for them, and re-layouts  9.7 us (6%)
  other arithmetic  3.73 us (2%)
    all_gather x1, blocking collectives, shards(): ring_pair = lax.all_gather(pair, 'z', axis=0, tiled=True)  36 us
    all_to_all x1, starting transfers between devices, shards(): got = lax.all_to_all(sent, SEQ, split_axis=0, concat_axis=0, tiled=True)  15.8 us
    all_to_all x1, starting transfers between devices, shards(): lax.all_to_all(col_sent, SEQ, split_axis=0, concat_axis=0, tiled=True)  15.6 us
    all_to_all x1, blocking collectives, sent_and_summed(): pieces = lax.all_to_all(split_up(value, dim, size), axis, 0, 0, tiled=True)  14.1 us
    all_to_all x1, starting transfers between devices, sent_and_summed(): pieces = lax.all_to_all(split_up(value, dim, size), axis, 0, 0, tiled=True)  12.2 us
    all_gather x1, blocking collectives, shards(): whole_rows = lax.all_gather(tokens, MP, axis=0, tiled=True)  12.2 us
    ppermute x3, starting transfers between devices, shards(): lax.ppermute(ring_pair, 'y', [(i, (i - k) % 4) for i in range(4)])  8.76 us
    all_to_all x1, waiting for transfers between devices, sent_and_summed(): pieces = lax.all_to_all(split_up(value, dim, size), axis, 0, 0, tiled=True)  6.01 us
  transfers between devices with their start and end apart: 8, of which 3 were waited for; matrix products, arithmetic and copies ran while one was open for 9% of the time, Pallas kernels for 0%

profile of v4, /device:TPU:1, one launch (start us, length us, event | category | flops | bytes accessed | tf_op | source)
XLA Modules:
  0.0 169.2 jit_solution(17671619287582020155)
XLA Ops:
  0.0 1.0 fusion.107
  1.1 3.9 %collective-permute-start = (bf16[9,1152]{1,0:T(8,128)(2,1)S(1)}, bf16[9,1152]{1,0:T(8,128)(2,1)S(1)}, u32[]{:S(2)}, u32[]{:S(2)}) collective-permute-start(bf16[9,1152]{1,0:T(8,128)(2,1)S(1)} %broadcast_select_fusion.2), channel_id=1, source_target_pairs={{0,256},{256,0},{1,257},{257,1},{2,258},{258,2},{3,259},{259,3},{4... | collective-permute-start | bytes 62216 | tf_op jit(solution)/shard_map/ppermute | solution.py:139
  5.0 12.2 %all-gather = bf16[1,1,128,1152]{3,2,1,0:T(8,128)(2,1)S(1)} all-gather(bf16[1,1,32,1152]{3,2,1,0:T(8,128)(2,1)} %param.15), channel_id=2, replica_groups=mesh['x_lo'=2,'y'=4,'z'=16,'x_hi'=2,'core'=2] {'x_hi','core'}, dimensions={2}, use_global_device_ids=true | all-gather | bytes 368640 | tf_op jit(solution)/shard_map/all_gather | solution.py:120
  17.3 0.1 convert_reduce_fusion.1
  17.4 0.2 fusion.35
  17.6 1.5 fusion.22
  19.2 0.1 copy.58
  19.3 0.3 reduce_window_sum.17
  19.8 0.3 convolution_convert_fusion.3
  20.3 0.3 convolution_convert_fusion.4
  20.7 0.1 copy.56
  21.0 1.4 convolution_convert_fusion.2
  22.5 1.2 convolution_select_fusion.1
  23.7 0.3 fusion.109
  24.2 0.1 multiply_reduce_fusion.2
  24.6 0.2 copy.64
  24.9 0.9 copy.65
  25.8 15.8 %all-to-all-start = ((bf16[128,8,128]{2,1,0:T(8,128)(2,1)}), bf16[128,8,128]{2,1,0:T(8,128)(2,1)S(1)}, u32[]{:S(2)}, u32[]{:S(2)}) async-start(bf16[128,8,128]{2,1,0:T(8,128)(2,1)} %copy.65), calls=%async_computation | async-start | bytes 524288 | tf_op jit(solution)/shard_map/all_to_all | solution.py:173
  41.6 36.0 %all-gather.1 = bf16[16,18,1152]{2,1,0:T(8,128)(2,1)S(1)} all-gather(bf16[1,18,1152]{2,1,0:T(8,128)(2,1)S(1)} %bitcast.169), channel_id=1, replica_groups=mesh['x_lo'=2,'y'=4,'z'=16,'x_hi'=2,'core'=2] {'z'}, dimensions={0}, use_global_device_ids=true | all-gather | bytes 705024 | tf_op jit(solution)/shard_map/all_gather | solution.py:174
  77.6 0.2 reshape.491
  77.9 0.2 copy.66
  78.3 0.3 reduce_window_sum.18
  78.7 0.1 copy.67
  78.9 1.2 convolution_select_fusion
  80.1 0.3 fusion.110
  80.9 0.7 multiply_convert_fusion
  81.6 15.6 %all-to-all-start.1 = ((bf16[128,2,128]{2,1,0:T(2,128)(2,1)}), bf16[128,2,128]{2,1,0:T(2,128)(2,1)S(1)}, u32[]{:S(2)}, u32[]{:S(2)}) async-start(bf16[128,2,128]{2,1,0:T(2,128)(2,1)} %multiply_convert_fusion), calls=%async_computation.1 | async-start | bytes 131072 | tf_op jit(solution)/shard_map/all_to_all | solution.py:187
  97.2 3.9 %collective-permute-start.1 = (bf16[288,1152]{1,0:T(8,128)(2,1)S(1)}, bf16[288,1152]{1,0:T(8,128)(2,1)}, u32[]{:S(2)}, u32[]{:S(2)}) collective-permute-start(bf16[288,1152]{1,0:T(8,128)(2,1)S(1)} %reshape.491), channel_id=1, source_target_pairs={{0,192},{64,0},{128,64},{192,128},{1,193},{65,1},{129,65},{193,129... | collective-permute-start | bytes 1990664 | tf_op jit(solution)/shard_map/ppermute | solution.py:191
  101.1 2.3 %collective-permute-start.2 = (bf16[288,1152]{1,0:T(8,128)(2,1)S(1)}, bf16[288,1152]{1,0:T(8,128)(2,1)S(1)}, u32[]{:S(2)}, u32[]{:S(2)}) collective-permute-start(bf16[288,1152]{1,0:T(8,128)(2,1)S(1)} %reshape.491), channel_id=1, source_target_pairs={{0,128},{64,192},{128,0},{192,64},{1,129},{65,193},{129,1},{193,65... | collective-permute-start | bytes 1990664 | tf_op jit(solution)/shard_map/ppermute | solution.py:191
  103.4 2.6 %collective-permute-start.3 = (bf16[288,1152]{1,0:T(8,128)(2,1)S(1)}, bf16[288,1152]{1,0:T(8,128)(2,1)S(1)}, u32[]{:S(2)}, u32[]{:S(2)}) collective-permute-start(bf16[288,1152]{1,0:T(8,128)(2,1)S(1)} %reshape.491), channel_id=1, source_target_pairs={{0,64},{64,128},{128,192},{192,0},{1,65},{65,129},{129,193},{193,1... | collective-permute-start | bytes 1990664 | tf_op jit(solution)/shard_map/ppermute | solution.py:191
  106.0 5.3 %all-to-all-done.1 = bf16[128,2,128]{2,1,0:T(2,128)(2,1)S(1)} async-done(((bf16[128,2,128]{2,1,0:T(2,128)(2,1)}), bf16[128,2,128]{2,1,0:T(2,128)(2,1)S(1)}, u32[]{:S(2)}, u32[]{:S(2)}) %all-to-all-start.1) | async-done | bytes 65568 | tf_op jit(solution)/shard_map/all_to_all | solution.py:187
  111.3 1.0 convolution_convert_fusion.1
  112.3 12.2 %all-to-all-start.2 = ((bf16[4,32,1152]{2,1,0:T(8,128)(2,1)}), bf16[4,32,1152]{2,1,0:T(8,128)(2,1)S(1)}, u32[]{:S(2)}, u32[]{:S(2)}) async-start(bf16[4,32,1152]{2,1,0:T(8,128)(2,1)} %bitcast.55), calls=%async_computation.2 | async-start | bytes 589824 | tf_op jit(solution)/shard_map/all_to_all | solution.py:27
  124.5 0.9 constant_dynamic-update-slice_fusion.3
  125.4 6.0 %all-to-all-done.2 = bf16[4,32,1152]{2,1,0:T(8,128)(2,1)S(1)} async-done(((bf16[4,32,1152]{2,1,0:T(8,128)(2,1)}), bf16[4,32,1152]{2,1,0:T(8,128)(2,1)S(1)}, u32[]{:S(2)}, u32[]{:S(2)}) %all-to-all-start.2) | async-done | bytes 294944 | tf_op jit(solution)/shard_map/all_to_all | solution.py:27
  131.4 0.1 convert_reduce_fusion.3
  131.6 0.2 fusion.58
  131.8 1.1 fusion.5
  132.9 0.9 broadcast_in_dim.42
  133.8 5.0 %all-to-all-start.3 = ((bf16[8,32,1152]{2,1,0:T(8,128)(2,1)}), bf16[8,32,1152]{2,1,0:T(8,128)(2,1)}, u32[]{:S(2)}, u32[]{:S(2)}) async-start(bf16[8,32,1152]{2,1,0:T(8,128)(2,1)} %broadcast_in_dim.42), calls=%async_computation.3 | async-start | bytes 1179648 | tf_op jit(solution)/shard_map/all_to_all | solution.py:16
  138.8 2.0 %constant_dynamic-update-slice_fusion.2 = bf16[1152,1152]{1,0:T(8,128)(2,1)} fusion(bf16[1152,1152]{1,0:T(8,128)(2,1)} %constant_dynamic-update-slice_fusion.3, bf16[288,1152]{1,0:T(8,128)(2,1)} %collective-permute-done.1), kind=kLoop, calls=%fused_computation.122 | loop fusion | bytes 1327104
  140.8 0.9 constant_dynamic-update-slice_fusion.1
  141.7 0.9 constant_dynamic-update-slice_fusion
  142.6 5.7 %all-to-all-done.3 = bf16[8,32,1152]{2,1,0:T(8,128)(2,1)} async-done(((bf16[8,32,1152]{2,1,0:T(8,128)(2,1)}), bf16[8,32,1152]{2,1,0:T(8,128)(2,1)}, u32[]{:S(2)}, u32[]{:S(2)}) %all-to-all-start.3) | async-done | bytes 589856 | tf_op jit(solution)/shard_map/all_to_all | solution.py:16
  148.3 2.3 %fusion.14 = bf16[256,576]{0,1:T(8,128)(2,1)S(1)} fusion(bf16[256,1152]{1,0:T(8,128)(2,1)} %bitcast.58, bf16[1152,1152]{1,0:T(8,128)(2,1)} %constant_dynamic-update-slice_fusion), kind=kOutput, calls=%fused_computation.13 | convolution fusion | flops 340180992 | bytes 2359296 | tf_op jit(solution)/shard_map/dot_general | solution.py:204
  150.6 3.8 %fusion.4 = bf16[256,1152]{1,0:T(8,128)(2,1)S(1)} fusion(s32[1152]{0:T(1024)S(1)} %fusion.83, bf16[1152,1152]{1,0:T(8,128)(2,1)} %constant_dynamic-update-slice_fusion, bf16[256,576]{0,1:T(8,128)(2,1)S(1)} %fusion.14), kind=kOutput, calls=%fused_computation.6 | convolution fusion | flops 1360871424 | bytes 3543552 | tf_op jit(solution)/shard_map/dot_general | solution.py:211
  154.3 14.1 %all_to_all.25 = bf16[8,32,1152]{2,1,0:T(8,128)(2,1)S(1)} all-to-all(bf16[8,32,1152]{2,1,0:T(8,128)(2,1)S(1)} %bitcast.150), channel_id=1, replica_groups=mesh['x_lo'=2,'y'=4,'z'=16,'x_hi'=2,'core'=2] {'x_lo','x_hi','core'}, dimensions={0} | all-to-all | bytes 1179648 | tf_op jit(solution)/shard_map/all_to_all | solution.py:27
  168.5 0.7 fusion.64
  (67 shorter events, 2.4 us)
Async XLA Ops:
  0.0 111.3 %copy-start = (bf16[256,1152]{1,0:T(8,128)(2,1)S(1)}, bf16[256,1152]{1,0:T(8,128)(2,1)}, u32[]{:S(2)}) copy-start(bf16[256,1152]{1,0:T(8,128)(2,1)} %param.26) | copy-start | bytes 1769476
  0.0 19.8 %copy-start.7 = (f32[1152]{0:T(1024)S(1)}, f32[1152]{0:T(1024)}, u32[]{:S(2)}) copy-start(f32[1152]{0:T(1024)} %param.16) | copy-start | bytes 13828
  0.0 19.8 %copy-start.5 = (bf16[1152,256]{1,0:T(8,128)(2,1)S(1)}, bf16[1152,256]{1,0:T(8,128)(2,1)}, u32[]{:S(2)}) copy-start(bf16[1152,256]{1,0:T(8,128)(2,1)} %param.18) | copy-start | bytes 1769476
  1.1 23.8 %collective-permute-start = (bf16[9,1152]{1,0:T(8,128)(2,1)S(1)}, bf16[9,1152]{1,0:T(8,128)(2,1)S(1)}, u32[]{:S(2)}, u32[]{:S(2)}) collective-permute-start(bf16[9,1152]{1,0:T(8,128)(2,1)S(1)} %broadcast_select_fusion.2), channel_id=1, source_target_pairs={{0,256},{256,0},{1,257},{257,1},{2,258},{258,2},{3,259},{259,3},{4... | collective-permute-start | bytes 62216 | tf_op jit(solution)/shard_map/ppermute | solution.py:139
  17.4 2.9 %copy-start.6 = (bf16[1152,256]{1,0:T(8,128)(2,1)S(1)}, bf16[1152,256]{1,0:T(8,128)(2,1)}, u32[]{:S(2)}) copy-start(bf16[1152,256]{1,0:T(8,128)(2,1)} %param.17) | copy-start | bytes 1769476
  20.3 3.8 %copy-start.4 = (f32[256]{0:T(256)S(1)}, f32[256]{0:T(256)}, u32[]{:S(2)}) copy-start(f32[256]{0:T(256)} %param.23) | copy-start | bytes 3076
  21.0 3.6 %copy-start.2 = (f32[256]{0:T(256)S(1)}, f32[256]{0:T(256)}, u32[]{:S(2)}) copy-start(f32[256]{0:T(256)} %param.24) | copy-start | bytes 3076
  25.8 52.0 %all-to-all-start = ((bf16[128,8,128]{2,1,0:T(8,128)(2,1)}), bf16[128,8,128]{2,1,0:T(8,128)(2,1)S(1)}, u32[]{:S(2)}, u32[]{:S(2)}) async-start(bf16[128,8,128]{2,1,0:T(8,128)(2,1)} %copy.65), calls=%async_computation | async-start | bytes 524288 | tf_op jit(solution)/shard_map/all_to_all | solution.py:173
  78.5 2.3 %copy-start.3 = (f32[256]{0:T(256)S(1)}, f32[256]{0:T(256)}, u32[]{:S(2)}) copy-start(f32[256]{0:T(256)} %param.25) | copy-start | bytes 3076
  80.4 51.1 %copy-start.1 = (bf16[1,1,32,1152]{3,2,1,0:T(8,128)(2,1)S(1)}, bf16[1,1,32,1152]{3,2,1,0:T(8,128)(2,1)}, u32[]{:S(2)}) copy-start(bf16[1,1,32,1152]{3,2,1,0:T(8,128)(2,1)} %param.15) | copy-start | bytes 221188
  80.5 51.3 %copy-start.8 = (f32[1152]{0:T(1024)S(1)}, f32[1152]{0:T(1024)}, u32[]{:S(2)}) copy-start(f32[1152]{0:T(1024)} %param.27) | copy-start | bytes 13828
  81.6 29.7 %all-to-all-start.1 = ((bf16[128,2,128]{2,1,0:T(2,128)(2,1)}), bf16[128,2,128]{2,1,0:T(2,128)(2,1)S(1)}, u32[]{:S(2)}, u32[]{:S(2)}) async-start(bf16[128,2,128]{2,1,0:T(2,128)(2,1)} %multiply_convert_fusion), calls=%async_computation.1 | async-start | bytes 131072 | tf_op jit(solution)/shard_map/all_to_all | solution.py:187
  97.2 41.6 %collective-permute-start.1 = (bf16[288,1152]{1,0:T(8,128)(2,1)S(1)}, bf16[288,1152]{1,0:T(8,128)(2,1)}, u32[]{:S(2)}, u32[]{:S(2)}) collective-permute-start(bf16[288,1152]{1,0:T(8,128)(2,1)S(1)} %reshape.491), channel_id=1, source_target_pairs={{0,192},{64,0},{128,64},{192,128},{1,193},{65,1},{129,65},{193,129... | collective-permute-start | bytes 1990664 | tf_op jit(solution)/shard_map/ppermute | solution.py:191
  101.1 39.7 %collective-permute-start.2 = (bf16[288,1152]{1,0:T(8,128)(2,1)S(1)}, bf16[288,1152]{1,0:T(8,128)(2,1)S(1)}, u32[]{:S(2)}, u32[]{:S(2)}) collective-permute-start(bf16[288,1152]{1,0:T(8,128)(2,1)S(1)} %reshape.491), channel_id=1, source_target_pairs={{0,128},{64,192},{128,0},{192,64},{1,129},{65,193},{129,1},{193,65... | collective-permute-start | bytes 1990664 | tf_op jit(solution)/shard_map/ppermute | solution.py:191
  103.4 38.3 %collective-permute-start.3 = (bf16[288,1152]{1,0:T(8,128)(2,1)S(1)}, bf16[288,1152]{1,0:T(8,128)(2,1)S(1)}, u32[]{:S(2)}, u32[]{:S(2)}) collective-permute-start(bf16[288,1152]{1,0:T(8,128)(2,1)S(1)} %reshape.491), channel_id=1, source_target_pairs={{0,64},{64,128},{128,192},{192,0},{1,65},{65,129},{129,193},{193,1... | collective-permute-start | bytes 1990664 | tf_op jit(solution)/shard_map/ppermute | solution.py:191
  112.3 19.1 %all-to-all-start.2 = ((bf16[4,32,1152]{2,1,0:T(8,128)(2,1)}), bf16[4,32,1152]{2,1,0:T(8,128)(2,1)S(1)}, u32[]{:S(2)}, u32[]{:S(2)}) async-start(bf16[4,32,1152]{2,1,0:T(8,128)(2,1)} %bitcast.55), calls=%async_computation.2 | async-start | bytes 589824 | tf_op jit(solution)/shard_map/all_to_all | solution.py:27
  133.8 14.5 %all-to-all-start.3 = ((bf16[8,32,1152]{2,1,0:T(8,128)(2,1)}), bf16[8,32,1152]{2,1,0:T(8,128)(2,1)}, u32[]{:S(2)}, u32[]{:S(2)}) async-start(bf16[8,32,1152]{2,1,0:T(8,128)(2,1)} %broadcast_in_dim.42), calls=%async_computation.3 | async-start | bytes 1179648 | tf_op jit(solution)/shard_map/all_to_all | solution.py:16

commit v5 on v4

--- a/solution.py
+++ b/solution.py
@@ -8,6 +8,7 @@
 SUBSPACE_SIZE = 64
 SEQ = ("x_lo", "y", "z")
 MP = ("x_hi", "core")
+PLANE = ("x_lo", "y")
 MIX = ("x_lo", "x_hi", "core")
 
 
@@ -88,14 +89,10 @@
     return (normed * gain).astype(jnp.bfloat16)
 
 
-def unit_order(depth, width):
-    ring = lax.axis_size("y")
-    stored = jnp.arange(2 * ring * depth * width)
-    turn, rest = stored // (2 * depth * width), stored % (2 * depth * width)
-    z, rest = rest // (2 * width), rest % (2 * width)
-    x = rest // width
-    y = (turn + lax.axis_index("y")) % ring
-    return ((x * ring + y) * depth + z) * width + rest % width
+def unit_order(planes, depth, width):
+    stored = jnp.arange(planes * depth * width)
+    z, rest = stored // (planes * width), stored % (planes * width)
+    return ((rest // width) * depth + z) * width + rest % width
 
 
 def shards(
@@ -121,9 +118,8 @@
     full_cols = whole_rows.shape[0]
     inner_width = acceptance_matrix.shape[1]
 
-    depth = lax.axis_size("z")
+    planes, depth, ring = lax.axis_size(PLANE), lax.axis_size("z"), lax.axis_size("y")
     width, units = feature_mix_addressing_matrix.shape
-    first_half = lax.axis_index("x_lo") == 0
     halves = [
         jnp.concatenate(
             [
@@ -134,12 +130,12 @@
         )
         for start in (0, units // 2)
     ]
-    kept = jnp.where(first_half, halves[0], halves[1])
-    given = jnp.where(first_half, halves[1], halves[0])
-    received = lax.ppermute(given, "x_lo", [(0, 1), (1, 0)])
-    pair = jnp.concatenate(
-        [jnp.where(first_half, kept, received), jnp.where(first_half, received, kept)], axis=0
-    )
+    shares = jnp.broadcast_to(jnp.stack(halves)[:, None], (2, ring, width, units))
+    plane = lax.all_to_all(shares.reshape(planes, width, units), PLANE, 0, 0, tiled=True)
+    plane, whole_rows = lax.optimization_barrier(
+        (plane.reshape(planes * width, units), whole_rows)
+    )
+    weights = lax.all_gather(plane, "z", axis=0, tiled=True)
 
     xn1 = layer_norm(whole_rows, initial_standardize_scaling)
     recept = jnp.dot(xn1, acceptance_matrix, preferred_element_type=jnp.float32).astype(
@@ -169,9 +165,18 @@
     )[0]
     sent = jnp.stack([recept, keying, decay, row_out], axis=1)
     sent = sent.reshape(full_cols, 4 * inner_width // 128, 128)
-    sent, pair = lax.optimization_barrier((sent, pair))
+    sent, own_projection, own_rows = lax.optimization_barrier(
+        (sent, temporal_mix_projection_matrix, whole_rows)
+    )
     got = lax.all_to_all(sent, SEQ, split_axis=0, concat_axis=0, tiled=True)
-    ring_pair = lax.all_gather(pair, "z", axis=0, tiled=True)
+    projection = [own_projection]
+    for k in range(1, 4):
+        projection.append(lax.ppermute(own_projection, MP, [(i, i ^ k) for i in range(4)]))
+    other_rows = lax.ppermute(own_rows, "x_lo", [(0, 1), (1, 0)])
+    first_half = lax.axis_index("x_lo") == 0
+    both_rows = jnp.stack(
+        [jnp.where(first_half, own_rows, other_rows), jnp.where(first_half, other_rows, own_rows)]
+    )
     height = got.shape[0]
     got = got.reshape(height, 4, inner_width)
     col_out = recurrence(
@@ -183,24 +188,29 @@
         vertical_cluster_scaling,
     )[0]
     col_sent = col_out.reshape(height, inner_width // 128, 128)
-    col_sent, ring_pair = lax.optimization_barrier((col_sent, ring_pair))
+    col_sent, projection, both_rows = lax.optimization_barrier((col_sent, projection, both_rows))
     back = lax.all_to_all(col_sent, SEQ, split_axis=0, concat_axis=0, tiled=True)
     back = back.reshape(full_cols, inner_width)
-    pieces = [ring_pair]
-    for k in range(1, 4):
-        pieces.append(lax.ppermute(ring_pair, "y", [(i, (i - k) % 4) for i in range(4)]))
-    partial_value = jnp.dot(
-        back, temporal_mix_projection_matrix, preferred_element_type=jnp.float32
-    ).astype(jnp.bfloat16)
-    attended = sent_and_summed(partial_value, MP, 0)
-    residual = (tokens.astype(jnp.float32) + attended).astype(jnp.bfloat16)
-    mix_input = layer_norm(residual, later_standardize_scaling)
-
-    places = unit_order(depth, width)
+    groups = from_everyone(back, MIX).reshape(2, 4, full_cols, inner_width)
+    group = lax.axis_index(MP)
+    attended = jnp.zeros((2 * full_cols, model_width), jnp.float32)
+    for k in range(4):
+        one = lax.dynamic_index_in_dim(groups, group ^ k, 1, keepdims=False)
+        attended = attended + jnp.dot(
+            one.reshape(2 * full_cols, inner_width),
+            projection[k],
+            preferred_element_type=jnp.float32,
+        )
+    both_rows = both_rows.reshape(2 * full_cols, model_width)
+    residual_all = (both_rows.astype(jnp.float32) + attended).astype(jnp.bfloat16)
+    residual = lax.dynamic_slice_in_dim(
+        residual_all, lax.axis_index(MIX) * part_cols, part_cols, 0
+    )
+    mix_all = layer_norm(residual_all, later_standardize_scaling)
+
+    places = unit_order(planes, depth, width)
     moved = (jnp.arange(model_width)[:, None] == places[None, :]).astype(jnp.bfloat16)
-    mix_input = jnp.dot(mix_input, moved, preferred_element_type=jnp.float32).astype(jnp.bfloat16)
-    mix_all = from_everyone(mix_input, MIX).reshape(-1, model_width)
-    weights = jnp.concatenate(pieces, axis=0)
+    mix_all = jnp.dot(mix_all, moved, preferred_element_type=jnp.float32).astype(jnp.bfloat16)
     hidden_pre = jnp.dot(mix_all, weights, preferred_element_type=jnp.float32)
     positive = jnp.maximum(hidden_pre[:, : units // 2], 0.0)
     hidden = (positive * positive).astype(jnp.bfloat16)

time: 170 us -> 171 us (level)
  waiting for transfers between devices: 17 us -> 38.5 us
  blocking collectives: 62.3 us -> 41.9 us
  starting transfers between devices: 61.4 us -> 47.1 us
  between operations: 0.52 us -> 14 us
  matrix products: 14.5 us -> 17.1 us
    all_gather x1 -> x0, blocking collectives: 36 us -> none  [shards(): ring_pair = lax.all_gather(pair, 'z', axis=0, tiled=True)]
    all_to_all x1, blocking collectives: 14.1 us -> 30.3 us  [shards(): lax.all_to_all(col_sent, SEQ, split_axis=0, concat_axis=0, tiled=True)]
    all_to_all x1, waiting for transfers between devices: 0.01 us -> 10.2 us  [shards(): got = lax.all_to_all(sent, SEQ, split_axis=0, concat_axis=0, tiled=True)]
    ppermute x4, waiting for transfers between devices: 0.01 us -> 10.1 us  [the longest x3 10.1 us: shards(): lax.ppermute(own_projection, MP, [(i, i ^ k) for i in range(4)])]
    all_to_all x1, starting transfers between devices: 15.6 us -> 5.94 us  [shards(): lax.all_to_all(shares.reshape(planes, width, units), PLANE, 0, 0, tiled=T...]
    all_to_all x1, starting transfers between devices: 12.2 us -> 4.68 us  [sent_and_summed(): pieces = lax.all_to_all(split_up(value, dim, size), axis, 0, 0, tiled=True)]
    all_to_all x1, waiting for transfers between devices: 5.31 us -> 0.01 us  [shards(): lax.all_to_all(shares.reshape(planes, width, units), PLANE, 0, 0, tiled=T...]
    all_to_all x1, waiting for transfers between devices: 6.01 us -> 9.36 us  [sent_and_summed(): pieces = lax.all_to_all(split_up(value, dim, size), axis, 0, 0, tiled=True)]
  transfers between devices with their start and end apart: 8 -> 9, of which waited for: 3 -> 4; matrix products, arithmetic and copies ran while one was open for 9% -> 6% of each run, Pallas kernels for 0% -> 0%
where the time goes in v5:
time: 171 us; the launch traced here: 170 us
  starting transfers between devices  47.1 us (28%)
  blocking collectives  41.9 us (25%)
  waiting for transfers between devices  38.5 us (23%)
  matrix products  17.1 us (10%)
  between operations  14 us (8%)
  local copies, waits for them, and re-layouts  8.25 us (5%)
  other arithmetic  3.69 us (2%)
    all_to_all x1, blocking collectives, shards(): lax.all_to_all(col_sent, SEQ, split_axis=0, concat_axis=0, tiled=True)  30.3 us
    all_to_all x1, starting transfers between devices, shards(): got = lax.all_to_all(sent, SEQ, split_axis=0, concat_axis=0, tiled=True)  17.2 us
    all_gather x1, blocking collectives, shards(): whole_rows = lax.all_gather(tokens, MP, axis=0, tiled=True)  11.5 us
    all_to_all x1, waiting for transfers between devices, shards(): got = lax.all_to_all(sent, SEQ, split_axis=0, concat_axis=0, tiled=True)  10.2 us
    ppermute x3, waiting for transfers between devices, shards(): lax.ppermute(own_projection, MP, [(i, i ^ k) for i in range(4)])  10.1 us
    ppermute x3, starting transfers between devices, shards(): lax.ppermute(own_projection, MP, [(i, i ^ k) for i in range(4)])  9.59 us
    all_to_all x1, waiting for transfers between devices, sent_and_summed(): pieces = lax.all_to_all(split_up(value, dim, size), axis, 0, 0, tiled=True)  9.36 us
    all_to_all x1, waiting for transfers between devices, from_everyone(): return lax.all_to_all(copies, axis, split_axis=0, concat_axis=0, tiled=True)  8.81 us
  transfers between devices with their start and end apart: 9, of which 4 were waited for; matrix products, arithmetic and copies ran while one was open for 6% of the time, Pallas kernels for 0%

profile of v5, /device:TPU:1, one launch (start us, length us, event | category | flops | bytes accessed | tf_op | source)
XLA Modules:
  0.0 170.5 jit_solution(9516914731434002555)
XLA Ops:
  6.5 0.9 fusion.108
  7.4 0.9 fusion.109
  8.5 0.7 broadcast_in_dim.41
  9.2 5.9 %all-to-all-start = ((bf16[8,9,1152]{2,1,0:T(8,128)(2,1)}), bf16[8,9,1152]{2,1,0:T(8,128)(2,1)S(1)}, u32[]{:S(2)}, u32[]{:S(2)}) async-start(bf16[8,9,1152]{2,1,0:T(8,128)(2,1)} %bitcast.3), calls=%async_computation | async-start | bytes 589824 | tf_op jit(solution)/shard_map/all_to_all | solution.py:134
  15.4 11.5 %all-gather = bf16[1,1,128,1152]{3,2,1,0:T(8,128)(2,1)S(1)} all-gather(bf16[1,1,32,1152]{3,2,1,0:T(8,128)(2,1)S(1)} %copy-done.3), channel_id=2, replica_groups=mesh['x_lo'=2,'y'=4,'z'=16,'x_hi'=2,'core'=2] {'x_hi','core'}, dimensions={2}, use_global_device_ids=true | all-gather | bytes 368640 | tf_op jit(solution)/shard_map/all_gather | solution.py:117
  26.9 0.8 reshape.455
  27.7 0.1 convert_reduce_fusion.2
  27.8 0.2 fusion.42
  28.1 0.5 fusion.30
  28.8 0.1 copy.61
  28.9 0.3 reduce_window_sum.17
  29.4 0.3 convolution_convert_fusion.3
  29.8 0.1 copy.59
  29.9 0.3 copy-done.7
  30.3 0.3 convolution_convert_fusion.2
  30.8 0.3 convolution_convert_fusion.1
  31.2 1.2 convolution_select_fusion.1
  32.5 0.3 fusion.110
  33.3 0.2 copy.67
  33.5 3.6 %collective-permute-start.3 = (bf16[128,1152]{1,0:T(8,128)(2,1)S(1)}, bf16[128,1152]{1,0:T(8,128)(2,1)S(1)}, u32[]{:S(2)}, u32[]{:S(2)}) collective-permute-start(bf16[128,1152]{1,0:T(8,128)(2,1)S(1)} %bitcast.129), channel_id=1, source_target_pairs={{0,256},{256,0},{1,257},{257,1},{2,258},{258,2},{3,259},{259,3},{4... | collective-permute-start | bytes 884744 | tf_op jit(solution)/shard_map/ppermute | solution.py:175
  37.0 0.9 copy.68
  37.9 17.2 %all-to-all-start.1 = ((bf16[128,8,128]{2,1,0:T(8,128)(2,1)}), bf16[128,8,128]{2,1,0:T(8,128)(2,1)S(1)}, u32[]{:S(2)}, u32[]{:S(2)}) async-start(bf16[128,8,128]{2,1,0:T(8,128)(2,1)} %copy.68), calls=%async_computation.1 | async-start | bytes 524288 | tf_op jit(solution)/shard_map/all_to_all | solution.py:171
  55.2 2.6 %collective-permute-start = (bf16[256,1152]{1,0:T(8,128)(2,1)S(1)}, bf16[256,1152]{1,0:T(8,128)(2,1)S(1)}, u32[]{:S(2)}, u32[]{:S(2)}) collective-permute-start(bf16[256,1152]{1,0:T(8,128)(2,1)S(1)} %copy-done.1), channel_id=1, source_target_pairs={{0,1},{1,0},{2,3},{3,2},{4,5},{5,4},{6,7},{7,6},{8,9},{9,8},{10,11... | collective-permute-start | bytes 1769480 | tf_op jit(solution)/shard_map/ppermute | solution.py:174
  57.8 3.3 %collective-permute-start.1 = (bf16[256,1152]{1,0:T(8,128)(2,1)S(1)}, bf16[256,1152]{1,0:T(8,128)(2,1)}, u32[]{:S(2)}, u32[]{:S(2)}) collective-permute-start(bf16[256,1152]{1,0:T(8,128)(2,1)S(1)} %copy-done.1), channel_id=1, source_target_pairs={{0,2},{1,3},{2,0},{3,1},{4,6},{5,7},{6,4},{7,5},{8,10},{9,11},{10,... | collective-permute-start | bytes 1769480 | tf_op jit(solution)/shard_map/ppermute | solution.py:174
  61.1 3.6 %collective-permute-start.2 = (bf16[256,1152]{1,0:T(8,128)(2,1)S(1)}, bf16[256,1152]{1,0:T(8,128)(2,1)}, u32[]{:S(2)}, u32[]{:S(2)}) collective-permute-start(bf16[256,1152]{1,0:T(8,128)(2,1)S(1)} %copy-done.1), channel_id=1, source_target_pairs={{0,3},{1,2},{2,1},{3,0},{4,7},{5,6},{6,5},{7,4},{8,11},{9,10},{10,... | collective-permute-start | bytes 1769480 | tf_op jit(solution)/shard_map/ppermute | solution.py:174
  64.9 10.2 %all-to-all-done.1 = bf16[128,8,128]{2,1,0:T(8,128)(2,1)S(1)} async-done(((bf16[128,8,128]{2,1,0:T(8,128)(2,1)}), bf16[128,8,128]{2,1,0:T(8,128)(2,1)S(1)}, u32[]{:S(2)}, u32[]{:S(2)}) %all-to-all-start.1) | async-done | bytes 262176 | tf_op jit(solution)/shard_map/all_to_all | solution.py:171
  75.2 0.2 copy.69
  75.4 0.7 fusion.107
  76.2 0.3 reduce_window_sum.18
  76.5 0.7 copy-done.2
  77.3 0.1 copy.70
  77.5 2.2 %convolution_select_fusion = f32[4,8,16,128]{3,2,1,0:T(8,128)S(1)} fusion(f32[4,128,64]{1,2,0:T(8,128)S(1)} %copy.72, f32[4,8,64]{2,1,0:T(8,128)S(1)} %bitcast.174, f32[4,128,64]{1,2,0:T(8,128)} %get-tuple-element.37, pred[8,128]{1,0:T(8,128)(4,1)S(1)} %iota_compare_fusion.10, f32[4,8,16,64]{3,2,1,0:T(8,128)S(1)} %bitcast.167, ...), kind=kOutput, calls=%fused_computation.26 | convolution fusion | flops 51249152 | bytes 812032 | tf_op jit(solution)/shard_map/nhbqc,nhbsc->nhbqs/dot_general | solution.py:69
  79.7 0.2 fusion.111
  80.6 10.0 %collective-permute-done.2 = bf16[256,1152]{1,0:T(8,128)(2,1)} collective-permute-done((bf16[256,1152]{1,0:T(8,128)(2,1)S(1)}, bf16[256,1152]{1,0:T(8,128)(2,1)}, u32[]{:S(2)}, u32[]{:S(2)}) %collective-permute-start.2) | collective-permute-done | bytes 589856 | tf_op jit(solution)/shard_map/ppermute | solution.py:174
  90.6 30.3 %all_to_all.25 = bf16[128,2,128]{2,1,0:T(2,128)(2,1)S(1)} all-to-all(bf16[128,2,128]{2,1,0:T(2,128)(2,1)S(1)} %multiply_convert_fusion), channel_id=1, replica_groups=mesh['x_lo'=2,'y'=4,'z'=16,'x_hi'=2,'core'=2] {'x_lo','y','z'}, dimensions={0} | all-to-all | bytes 131072 | tf_op jit(solution)/shard_map/all_to_all | solution.py:192
  120.9 0.8 broadcast_in_dim.45
  121.8 6.2 %all-to-all-start.3 = ((bf16[8,128,256]{2,1,0:T(8,128)(2,1)}), bf16[8,128,256]{2,1,0:T(8,128)(2,1)S(1)}, u32[]{:S(2)}, u32[]{:S(2)}) async-start(bf16[8,128,256]{2,1,0:T(8,128)(2,1)} %broadcast_in_dim.45), calls=%async_computation.3 | async-start | bytes 1048576 | tf_op jit(solution)/shard_map/all_to_all | solution.py:17
  128.0 8.8 %all-to-all-done.3 = bf16[8,128,256]{2,1,0:T(8,128)(2,1)S(1)} async-done(((bf16[8,128,256]{2,1,0:T(8,128)(2,1)}), bf16[8,128,256]{2,1,0:T(8,128)(2,1)S(1)}, u32[]{:S(2)}, u32[]{:S(2)}) %all-to-all-start.3) | async-done | bytes 524320 | tf_op jit(solution)/shard_map/all_to_all | solution.py:17
  136.8 0.3 fusion.112
  137.2 1.4 fusion.113
  138.6 1.4 fusion.114
  140.0 0.6 convert_reduce_fusion
  140.6 0.3 fusion.21
  141.0 3.3 %fusion.18 = bf16[256,576]{0,1:T(8,128)(2,1)S(1)} fusion(bf16[1152,1152]{1,0:T(8,128)(2,1)} %all-gather.3.cloned.1.call-done, s32[1152]{0:T(1024)S(1)} %fusion.86, bf16[256,1152]{1,0:T(8,128)(2,1)S(1)} %get-tuple-element.28, f32[1152]{0:T(1024)S(1)} %copy-done.12, f32[256]{0:T(256)S(1)} %add_rsqrt_fusion.2, f32[256]{0:T(256)S(1)} %broadcast_multiply_fusion.2), kind=kOutput, calls=%fused_computation.19 | convolution fusion | flops 1022754816 | bytes 2370560 | tf_op jit(solution)/shard_map/dot_general | solution.py:214
  144.3 4.6 %fusion.7 = bf16[256,1152]{1,0:T(8,128)(2,1)} fusion(s32[1152]{0:T(1024)S(1)} %fusion.86, bf16[1152,1152]{1,0:T(8,128)(2,1)} %all-gather.3.cloned.1.call-done, bf16[256,576]{0,1:T(8,128)(2,1)S(1)} %fusion.18), kind=kOutput, calls=%fused_computation.10 | convolution fusion | flops 1360871424 | bytes 3543552 | tf_op jit(solution)/shard_map/dot_general | solution.py:221
  148.9 4.7 %all-to-all-start.4 = ((bf16[8,32,1152]{2,1,0:T(8,128)(2,1)}), bf16[8,32,1152]{2,1,0:T(8,128)(2,1)S(1)}, u32[]{:S(2)}, u32[]{:S(2)}) async-start(bf16[8,32,1152]{2,1,0:T(8,128)(2,1)} %bitcast.65), calls=%async_computation.4 | async-start | bytes 1179648 | tf_op jit(solution)/shard_map/all_to_all | solution.py:28
  153.5 9.4 %all-to-all-done.4 = bf16[8,32,1152]{2,1,0:T(8,128)(2,1)S(1)} async-done(((bf16[8,32,1152]{2,1,0:T(8,128)(2,1)}), bf16[8,32,1152]{2,1,0:T(8,128)(2,1)S(1)}, u32[]{:S(2)}, u32[]{:S(2)}) %all-to-all-start.4) | async-done | bytes 589856 | tf_op jit(solution)/shard_map/all_to_all | solution.py:28
  163.0 0.7 fusion.75
  (80 shorter events, 2.7 us)
Async XLA Ops:
  6.5 22.8 %copy-start = (bf16[1152,256]{1,0:T(8,128)(2,1)S(1)}, bf16[1152,256]{1,0:T(8,128)(2,1)}, u32[]{:S(2)}) copy-start(bf16[1152,256]{1,0:T(8,128)(2,1)} %param.17) | copy-start | bytes 1769476
  6.5 8.8 %copy-start.6 = (f32[256]{0:T(256)S(1)}, f32[256]{0:T(256)}, u32[]{:S(2)}) copy-start(f32[256]{0:T(256)} %param.23) | copy-start | bytes 3076
  6.5 8.9 %copy-start.3 = (bf16[1,1,32,1152]{3,2,1,0:T(8,128)(2,1)S(1)}, bf16[1,1,32,1152]{3,2,1,0:T(8,128)(2,1)}, u32[]{:S(2)}) copy-start(bf16[1,1,32,1152]{3,2,1,0:T(8,128)(2,1)} %param.15) | copy-start | bytes 221188
  8.4 19.6 %copy-start.9 = (bf16[1152,64]{0,1:T(8,128)(2,1)S(1)}, bf16[1152,64]{0,1:T(8,128)(2,1)}, u32[]{:S(2)}) copy-start(bf16[1152,64]{0,1:T(8,128)(2,1)} %param.20) | copy-start | bytes 442372
  8.4 19.6 %copy-start.10 = (bf16[64,256]{1,0:T(8,128)(2,1)S(1)}, bf16[64,256]{1,0:T(8,128)(2,1)}, u32[]{:S(2)}) copy-start(bf16[64,256]{1,0:T(8,128)(2,1)} %param.21) | copy-start | bytes 98308
  8.4 19.6 %copy-start.11 = (f32[1152]{0:T(1024)S(1)}, f32[1152]{0:T(1024)}, u32[]{:S(2)}) copy-start(f32[1152]{0:T(1024)} %param.16) | copy-start | bytes 13828
  8.5 19.6 %copy-start.13 = (f32[256]{0:T(256)S(1)}, f32[256]{0:T(256)}, u32[]{:S(2)}) copy-start(f32[256]{0:T(256)} %param.22) | copy-start | bytes 3076
  9.2 17.7 %all-to-all-start = ((bf16[8,9,1152]{2,1,0:T(8,128)(2,1)}), bf16[8,9,1152]{2,1,0:T(8,128)(2,1)S(1)}, u32[]{:S(2)}, u32[]{:S(2)}) async-start(bf16[8,9,1152]{2,1,0:T(8,128)(2,1)} %bitcast.3), calls=%async_computation | async-start | bytes 589824 | tf_op jit(solution)/shard_map/all_to_all | solution.py:134
  29.2 1.1 copy-start.7
  29.7 1.1 copy-start.8
  32.4 0.8 copy-start.4
  33.2 21.9 %copy-start.1 = (bf16[256,1152]{1,0:T(8,128)(2,1)S(1)}, bf16[256,1152]{1,0:T(8,128)(2,1)}, u32[]{:S(2)}) copy-start(bf16[256,1152]{1,0:T(8,128)(2,1)} %param.26) | copy-start | bytes 1769476
  33.5 31.3 %collective-permute-start.3 = (bf16[128,1152]{1,0:T(8,128)(2,1)S(1)}, bf16[128,1152]{1,0:T(8,128)(2,1)S(1)}, u32[]{:S(2)}, u32[]{:S(2)}) collective-permute-start(bf16[128,1152]{1,0:T(8,128)(2,1)S(1)} %bitcast.129), channel_id=1, source_target_pairs={{0,256},{256,0},{1,257},{257,1},{2,258},{258,2},{3,259},{259,3},{4... | collective-permute-start | bytes 884744 | tf_op jit(solution)/shard_map/ppermute | solution.py:175
  37.9 37.3 %all-to-all-start.1 = ((bf16[128,8,128]{2,1,0:T(8,128)(2,1)}), bf16[128,8,128]{2,1,0:T(8,128)(2,1)S(1)}, u32[]{:S(2)}, u32[]{:S(2)}) async-start(bf16[128,8,128]{2,1,0:T(8,128)(2,1)} %copy.68), calls=%async_computation.1 | async-start | bytes 524288 | tf_op jit(solution)/shard_map/all_to_all | solution.py:171
  55.1 85.9 %all-gather.3.cloned.1.call-start = ((), (), s32[]{:S(2)}) async-start(), calls=%async_computation.5 | async-start | bytes 2820096 | tf_op jit(solution)/shard_map/all_gather | solution.py:138
  55.2 25.4 %collective-permute-start = (bf16[256,1152]{1,0:T(8,128)(2,1)S(1)}, bf16[256,1152]{1,0:T(8,128)(2,1)S(1)}, u32[]{:S(2)}, u32[]{:S(2)}) collective-permute-start(bf16[256,1152]{1,0:T(8,128)(2,1)S(1)} %copy-done.1), channel_id=1, source_target_pairs={{0,1},{1,0},{2,3},{3,2},{4,5},{5,4},{6,7},{7,6},{8,9},{9,8},{10,11... | collective-permute-start | bytes 1769480 | tf_op jit(solution)/shard_map/ppermute | solution.py:174
  57.8 22.8 %collective-permute-start.1 = (bf16[256,1152]{1,0:T(8,128)(2,1)S(1)}, bf16[256,1152]{1,0:T(8,128)(2,1)}, u32[]{:S(2)}, u32[]{:S(2)}) collective-permute-start(bf16[256,1152]{1,0:T(8,128)(2,1)S(1)} %copy-done.1), channel_id=1, source_target_pairs={{0,2},{1,3},{2,0},{3,1},{4,6},{5,7},{6,4},{7,5},{8,10},{9,11},{10,... | collective-permute-start | bytes 1769480 | tf_op jit(solution)/shard_map/ppermute | solution.py:174
  61.1 29.5 %collective-permute-start.2 = (bf16[256,1152]{1,0:T(8,128)(2,1)S(1)}, bf16[256,1152]{1,0:T(8,128)(2,1)}, u32[]{:S(2)}, u32[]{:S(2)}) collective-permute-start(bf16[256,1152]{1,0:T(8,128)(2,1)S(1)} %copy-done.1), channel_id=1, source_target_pairs={{0,3},{1,2},{2,1},{3,0},{4,7},{5,6},{6,5},{7,4},{8,11},{9,10},{10,... | collective-permute-start | bytes 1769480 | tf_op jit(solution)/shard_map/ppermute | solution.py:174
  76.5 0.7 copy-start.2
  79.7 0.8 copy-start.5
  121.8 15.0 %all-to-all-start.3 = ((bf16[8,128,256]{2,1,0:T(8,128)(2,1)}), bf16[8,128,256]{2,1,0:T(8,128)(2,1)S(1)}, u32[]{:S(2)}, u32[]{:S(2)}) async-start(bf16[8,128,256]{2,1,0:T(8,128)(2,1)} %broadcast_in_dim.45), calls=%async_computation.3 | async-start | bytes 1048576 | tf_op jit(solution)/shard_map/all_to_all | solution.py:17
  140.0 1.0 copy-start.12
  148.9 14.0 %all-to-all-start.4 = ((bf16[8,32,1152]{2,1,0:T(8,128)(2,1)}), bf16[8,32,1152]{2,1,0:T(8,128)(2,1)S(1)}, u32[]{:S(2)}, u32[]{:S(2)}) async-start(bf16[8,32,1152]{2,1,0:T(8,128)(2,1)} %bitcast.65), calls=%async_computation.4 | async-start | bytes 1179648 | tf_op jit(solution)/shard_map/all_to_all | solution.py:28
Sparse Core Ops, SparseCore 0:
  64.9 66.0 all-gather.2

commit v6 on v2

--- a/solution.py
+++ b/solution.py
@@ -3,6 +3,7 @@
 from jax import lax
 from jax.sharding import Mesh
 from jax.sharding import PartitionSpec as P
+
 
 SUBSPACE_SIZE = 64
 SEQ = ("x_lo", "y", "z")
@@ -121,8 +122,8 @@
     planes, depth = lax.axis_size(PLANE), lax.axis_size("z")
     width = feature_mix_addressing_matrix.shape[0]
     pair = jnp.stack([feature_mix_addressing_matrix, feature_mix_content_matrix.T])
-    pair, whole_rows = lax.optimization_barrier((pair, whole_rows))
-    plane_pair = from_everyone(pair, PLANE).reshape(planes, *pair.shape)
+    plane_pair = from_everyone(pair, PLANE)
+    plane_pair = plane_pair.reshape(planes, *pair.shape)
     plane_pair = jnp.swapaxes(plane_pair, 0, 1).reshape(2 * planes * width, -1)
     full_pair = lax.all_gather(plane_pair, "z", axis=0, tiled=True)
     full_pair = full_pair.reshape(depth, 2, planes * width, -1)
@@ -156,13 +157,8 @@
         horizontal_cluster_scaling,
     )[0]
     sent = jnp.stack([recept, keying, decay, row_out], axis=1)
-    got = lax.all_to_all(
-        sent.reshape(full_cols, 4 * inner_width // 128, 128),
-        SEQ,
-        split_axis=0,
-        concat_axis=0,
-        tiled=True,
-    )
+    sent = sent.reshape(full_cols, 4 * inner_width // 128, 128)
+    got = lax.all_to_all(sent, SEQ, split_axis=0, concat_axis=0, tiled=True)
     height = got.shape[0]
     got = got.reshape(height, 4, inner_width)
     col_out = recurrence(

time: 156 us -> 155 us (level)
    all_gather x1, blocking collectives: 14.4 us -> 12 us  [shards(): whole_rows = lax.all_gather(tokens, MP, axis=0, tiled=True)]
    all_to_all x1, blocking collectives: 10.1 us -> 12.5 us  [from_everyone(): return lax.all_to_all(copies, axis, split_axis=0, concat_axis=0, tiled=True)]
    all_to_all x1, blocking collectives: 23.6 us -> 21.9 us  [shards(): lax.all_to_all(col_out.reshape(height, inner_width // 128, 128), SEQ, spl...]
where the time goes in v6:
time: 155 us
  blocking collectives  105 us (68%)
  between operations  13.9 us (9%)
  matrix products  11.4 us (7%)
  starting transfers between devices  7.18 us (5%)
  waiting for transfers between devices  6.88 us (4%)
  local copies, waits for them, and re-layouts  6.52 us (4%)
  other arithmetic  3.71 us (2%)
    all_to_all x1, blocking collectives, shards(): got = lax.all_to_all(sent, SEQ, split_axis=0, concat_axis=0, tiled=True)  39.5 us
    all_to_all x1, blocking collectives, shards(): lax.all_to_all(col_out.reshape(height, inner_width // 128, 128), SEQ, spl...  21.9 us
    all_to_all x1, blocking collectives, from_everyone(): return lax.all_to_all(copies, axis, split_axis=0, concat_axis=0, tiled=True)  12.5 us
    all_gather x1, blocking collectives, shards(): whole_rows = lax.all_gather(tokens, MP, axis=0, tiled=True)  12 us
    all_to_all x1, blocking collectives, sent_and_summed(): pieces = lax.all_to_all(split_up(value, dim, size), axis, 0, 0, tiled=True)  10.9 us
    all_gather x1, blocking collectives, shards(): mix_all = lax.all_gather(mix_input, MP, axis=0, tiled=True)  8.62 us
    all_to_all x1, starting transfers between devices, sent_and_summed(): pieces = lax.all_to_all(split_up(value, dim, size), axis, 0, 0, tiled=True)  7.15 us
    all_to_all x1, waiting for transfers between devices, sent_and_summed(): pieces = lax.all_to_all(split_up(value, dim, size), axis, 0, 0, tiled=True)  6.87 us
  transfers between devices with their start and end apart: 2, of which 1 were waited for; matrix products, arithmetic and copies ran while one was open for 7% of the time, Pallas kernels for 0%

profile of v6, /device:TPU:1, one launch (start us, length us, event | category | flops | bytes accessed | tf_op | source)
XLA Modules:
  0.0 155.0 jit_solution(8712147483917950053)
XLA Ops:
  6.6 0.9 pad_maximum_fusion.1
  7.5 0.2 broadcast_in_dim.42
  7.7 12.5 %all_to_all.25 = bf16[8,2,9,1152]{3,1,2,0:T(2,128)(2,1)S(1)} all-to-all(bf16[8,2,9,1152]{3,1,2,0:T(2,128)(2,1)S(1)} %broadcast_in_dim.42), channel_id=1, replica_groups=mesh['x_lo'=2,'y'=4,'z'=16,'x_hi'=2,'core'=2] {'x_lo','y'}, dimensions={0} | all-to-all | bytes 663552 | tf_op jit(solution)/shard_map/all_to_all | solution.py:16
  20.3 0.9 reshape.456
  21.3 12.0 %all-gather = bf16[1,1,128,1152]{3,2,1,0:T(8,128)(2,1)S(1)} all-gather(bf16[1,1,32,1152]{3,2,1,0:T(8,128)(2,1)S(1)} %copy-done.2), channel_id=2, replica_groups=mesh['x_lo'=2,'y'=4,'z'=16,'x_hi'=2,'core'=2] {'x_hi','core'}, dimensions={2}, use_global_device_ids=true | all-gather | bytes 368640 | tf_op jit(solution)/shard_map/all_gather | solution.py:118
  33.3 0.1 convert_reduce_fusion
  33.4 0.2 fusion.26
  33.7 0.3 convolution_convert_fusion.2
  34.0 0.1 copy.99
  34.1 0.3 convolution_convert_fusion.3
  34.4 0.1 copy.97
  34.5 0.3 convolution_convert_fusion.4
  34.9 0.1 copy.93
  35.0 0.1 copy.94
  35.1 0.5 fusion.13
  35.7 0.1 copy.95
  35.8 0.1 copy.96
  35.9 0.3 reduce_window_sum.17
  36.2 0.1 copy.98
  36.6 1.2 convolution_select_fusion.1
  37.8 0.3 fusion.95
  38.1 0.1 copy.100
  38.2 0.1 multiply_reduce_fusion.2
  38.6 0.2 copy.102
  38.8 0.2 copy.103
  39.0 39.5 %all_to_all.26 = bf16[128,8,128]{2,1,0:T(8,128)(2,1)S(1)} all-to-all(bf16[128,8,128]{2,1,0:T(8,128)(2,1)S(1)} %copy.103), channel_id=1, replica_groups=mesh['x_lo'=2,'y'=4,'z'=16,'x_hi'=2,'core'=2] {'x_lo','y','z'}, dimensions={0} | all-to-all | bytes 524288 | tf_op jit(solution)/shard_map/all_to_all | solution.py:161
  78.5 0.2 copy.104
  78.8 0.1 copy.106
  78.9 0.3 reduce_window_sum.18
  79.2 0.1 copy.107
  79.4 0.1 copy.105
  79.5 1.2 convolution_select_fusion
  80.7 0.3 fusion.96
  81.0 0.1 copy.108
  81.1 0.1 fusion.55
  81.6 21.9 %all_to_all.27 = bf16[128,2,128]{2,1,0:T(2,128)(2,1)S(1)} all-to-all(bf16[128,2,128]{2,1,0:T(2,128)(2,1)S(1)} %copy.110), channel_id=1, replica_groups=mesh['x_lo'=2,'y'=4,'z'=16,'x_hi'=2,'core'=2] {'x_lo','y','z'}, dimensions={0} | all-to-all | bytes 131072 | tf_op jit(solution)/shard_map/all_to_all | solution.py:172
  103.5 1.0 convolution_convert_fusion.1
  104.5 7.1 %all-to-all-start.2 = ((bf16[4,32,1152]{2,1,0:T(8,128)(2,1)}), bf16[4,32,1152]{2,1,0:T(8,128)(2,1)S(1)}, u32[]{:S(2)}, u32[]{:S(2)}) async-start(bf16[4,32,1152]{2,1,0:T(8,128)(2,1)} %bitcast.53), calls=%async_computation.2 | async-start | bytes 589824 | tf_op jit(solution)/shard_map/all_to_all | solution.py:27
  111.7 6.9 %all-to-all-done.2 = bf16[4,32,1152]{2,1,0:T(8,128)(2,1)S(1)} async-done(((bf16[4,32,1152]{2,1,0:T(8,128)(2,1)}), bf16[4,32,1152]{2,1,0:T(8,128)(2,1)S(1)}, u32[]{:S(2)}, u32[]{:S(2)}) %all-to-all-start.2) | async-done | bytes 294944 | tf_op jit(solution)/shard_map/all_to_all | solution.py:27
  118.6 0.1 convert_reduce_fusion.3
  118.7 0.2 fusion.47
  118.9 1.1 fusion.7
  120.0 8.6 %all_gather.10 = bf16[128,1152]{1,0:T(8,128)(2,1)} all-gather(bf16[32,1152]{1,0:T(8,128)(2,1)S(1)} %fusion.7), channel_id=1, replica_groups=mesh['x_lo'=2,'y'=4,'z'=16,'x_hi'=2,'core'=2] {'x_hi','core'}, dimensions={0}, use_global_device_ids=true | all-gather | bytes 368640 | tf_op jit(solution)/shard_map/all_gather | solution.py:189
  128.7 3.0 %fusion.93 = (bf16[16,1,72,1152]{3,2,1,0:T(8,128)(2,1)S(1)}, bf16[16,1,72,1152]{3,2,1,0:T(8,128)(2,1)S(1)}) fusion(bf16[16,2,72,1152]{3,2,1,0:T(8,128)(2,1)} %bitcast.141), kind=kLoop, calls=%fused_computation.140 | loop fusion | bytes 10616832 | tf_op jit(solution)/shard_map/slice | solution.py:131
  131.7 1.3 fusion.5
  133.0 3.6 %fusion.6 = bf16[128,1152]{1,0:T(8,128)(2,1)} fusion(s32[1152]{0:T(1024)S(1)} %fusion.74, bf16[128,1152]{1,0:T(8,128)(2,1)} %fusion.5, bf16[1152,1152]{1,0:T(8,128)(2,1)S(1)} %bitcast.142), kind=kOutput, calls=%fused_computation.8 | convolution fusion | flops 681099264 | bytes 3248640 | tf_op jit(solution)/shard_map/dot_general | solution.py:196
  136.6 10.9 %all_to_all.28 = bf16[4,32,1152]{2,1,0:T(8,128)(2,1)S(1)} all-to-all(bf16[4,32,1152]{2,1,0:T(8,128)(2,1)} %bitcast.170), channel_id=1, replica_groups=mesh['x_lo'=2,'y'=4,'z'=16,'x_hi'=2,'core'=2] {'x_hi','core'}, dimensions={0} | all-to-all | bytes 589824 | tf_op jit(solution)/shard_map/all_to_all | solution.py:27
  147.5 0.7 fusion.53
  (66 shorter events, 1.3 us)
Async XLA Ops:
  6.5 97.0 %copy-start = (bf16[256,1152]{1,0:T(8,128)(2,1)S(1)}, bf16[256,1152]{1,0:T(8,128)(2,1)}, u32[]{:S(2)}) copy-start(bf16[256,1152]{1,0:T(8,128)(2,1)} %param.26) | copy-start | bytes 1769476
  6.5 14.7 %copy-start.5 = (f32[256]{0:T(256)S(1)}, f32[256]{0:T(256)}, u32[]{:S(2)}) copy-start(f32[256]{0:T(256)} %param.23) | copy-start | bytes 3076
  6.5 14.7 %copy-start.2 = (bf16[1,1,32,1152]{3,2,1,0:T(8,128)(2,1)S(1)}, bf16[1,1,32,1152]{3,2,1,0:T(8,128)(2,1)}, u32[]{:S(2)}) copy-start(bf16[1,1,32,1152]{3,2,1,0:T(8,128)(2,1)} %param.15) | copy-start | bytes 221188
  6.5 27.1 %copy-start.11 = (f32[1152]{0:T(1024)S(1)}, f32[1152]{0:T(1024)}, u32[]{:S(2)}) copy-start(f32[1152]{0:T(1024)} %param.16) | copy-start | bytes 13828
  6.5 27.1 %copy-start.6 = (bf16[1152,256]{1,0:T(8,128)(2,1)S(1)}, bf16[1152,256]{1,0:T(8,128)(2,1)}, u32[]{:S(2)}) copy-start(bf16[1152,256]{1,0:T(8,128)(2,1)} %param.19) | copy-start | bytes 1769476
  6.5 122.1 %all-gather.3.cloned.1.call-start = ((), (), s32[]{:S(2)}) async-start(), calls=%async_computation.5 | async-start | bytes 5640192 | tf_op jit(solution)/shard_map/all_gather | solution.py:128
  7.7 26.4 %copy-start.7 = (bf16[1152,256]{1,0:T(8,128)(2,1)S(1)}, bf16[1152,256]{1,0:T(8,128)(2,1)}, u32[]{:S(2)}) copy-start(bf16[1152,256]{1,0:T(8,128)(2,1)} %param.18) | copy-start | bytes 1769476
  20.3 14.3 %copy-start.8 = (bf16[1152,256]{1,0:T(8,128)(2,1)S(1)}, bf16[1152,256]{1,0:T(8,128)(2,1)}, u32[]{:S(2)}) copy-start(bf16[1152,256]{1,0:T(8,128)(2,1)} %param.17) | copy-start | bytes 1769476
  21.3 13.8 %copy-start.9 = (bf16[1152,64]{0,1:T(8,128)(2,1)S(1)}, bf16[1152,64]{0,1:T(8,128)(2,1)}, u32[]{:S(2)}) copy-start(bf16[1152,64]{0,1:T(8,128)(2,1)} %param.20) | copy-start | bytes 442372
  21.3 13.8 %copy-start.10 = (bf16[64,256]{1,0:T(8,128)(2,1)S(1)}, bf16[64,256]{1,0:T(8,128)(2,1)}, u32[]{:S(2)}) copy-start(bf16[64,256]{1,0:T(8,128)(2,1)} %param.21) | copy-start | bytes 98308
  21.3 13.8 %copy-start.13 = (f32[256]{0:T(256)S(1)}, f32[256]{0:T(256)}, u32[]{:S(2)}) copy-start(f32[256]{0:T(256)} %param.22) | copy-start | bytes 3076
  36.2 2.4 %copy-start.3 = (f32[256]{0:T(256)S(1)}, f32[256]{0:T(256)}, u32[]{:S(2)}) copy-start(f32[256]{0:T(256)} %param.24) | copy-start | bytes 3076
  79.2 2.3 %copy-start.4 = (f32[256]{0:T(256)S(1)}, f32[256]{0:T(256)}, u32[]{:S(2)}) copy-start(f32[256]{0:T(256)} %param.25) | copy-start | bytes 3076
  80.7 38.2 %copy-start.12 = (f32[1152]{0:T(1024)S(1)}, f32[1152]{0:T(1024)}, u32[]{:S(2)}) copy-start(f32[1152]{0:T(1024)} %param.27) | copy-start | bytes 13828
  104.5 14.0 %all-to-all-start.2 = ((bf16[4,32,1152]{2,1,0:T(8,128)(2,1)}), bf16[4,32,1152]{2,1,0:T(8,128)(2,1)S(1)}, u32[]{:S(2)}, u32[]{:S(2)}) async-start(bf16[4,32,1152]{2,1,0:T(8,128)(2,1)} %bitcast.53), calls=%async_computation.2 | async-start | bytes 589824 | tf_op jit(solution)/shard_map/all_to_all | solution.py:27
  128.7 3.0 %copy-start.1 = (bf16[128,1152]{1,0:T(8,128)(2,1)S(1)}, bf16[128,1152]{1,0:T(8,128)(2,1)}, u32[]{:S(2)}) copy-start(bf16[128,1152]{1,0:T(8,128)(2,1)} %all_gather.10) | copy-start | bytes 884740
Sparse Core Ops, SparseCore 0:
  21.3 92.0 all-gather.2

commit v7 on v4

--- a/solution.py
+++ b/solution.py
@@ -8,6 +8,7 @@
 SUBSPACE_SIZE = 64
 SEQ = ("x_lo", "y", "z")
 MP = ("x_hi", "core")
+PLANE = ("x_lo", "y")
 MIX = ("x_lo", "x_hi", "core")
 
 
@@ -88,14 +89,10 @@
     return (normed * gain).astype(jnp.bfloat16)
 
 
-def unit_order(depth, width):
-    ring = lax.axis_size("y")
-    stored = jnp.arange(2 * ring * depth * width)
-    turn, rest = stored // (2 * depth * width), stored % (2 * depth * width)
-    z, rest = rest // (2 * width), rest % (2 * width)
-    x = rest // width
-    y = (turn + lax.axis_index("y")) % ring
-    return ((x * ring + y) * depth + z) * width + rest % width
+def unit_order(planes, depth, width):
+    stored = jnp.arange(planes * depth * width)
+    z, rest = stored // (planes * width), stored % (planes * width)
+    return ((rest // width) * depth + z) * width + rest % width
 
 
 def shards(
@@ -121,9 +118,8 @@
     full_cols = whole_rows.shape[0]
     inner_width = acceptance_matrix.shape[1]
 
-    depth = lax.axis_size("z")
+    planes, depth, ring = lax.axis_size(PLANE), lax.axis_size("z"), lax.axis_size("y")
     width, units = feature_mix_addressing_matrix.shape
-    first_half = lax.axis_index("x_lo") == 0
     halves = [
         jnp.concatenate(
             [
@@ -134,12 +130,12 @@
         )
         for start in (0, units // 2)
     ]
-    kept = jnp.where(first_half, halves[0], halves[1])
-    given = jnp.where(first_half, halves[1], halves[0])
-    received = lax.ppermute(given, "x_lo", [(0, 1), (1, 0)])
-    pair = jnp.concatenate(
-        [jnp.where(first_half, kept, received), jnp.where(first_half, received, kept)], axis=0
-    )
+    halves = jnp.stack(halves)
+    halves, whole_rows = lax.optimization_barrier((halves, whole_rows))
+    shares = jnp.broadcast_to(halves[:, None], (2, ring, width, units))
+    plane = lax.all_to_all(shares.reshape(planes, width, units), PLANE, 0, 0, tiled=True)
+    plane = plane.reshape(planes * width, units)
+    weights = lax.all_gather(plane, "z", axis=0, tiled=True)
 
     xn1 = layer_norm(whole_rows, initial_standardize_scaling)
     recept = jnp.dot(xn1, acceptance_matrix, preferred_element_type=jnp.float32).astype(
@@ -169,9 +165,7 @@
     )[0]
     sent = jnp.stack([recept, keying, decay, row_out], axis=1)
     sent = sent.reshape(full_cols, 4 * inner_width // 128, 128)
-    sent, pair = lax.optimization_barrier((sent, pair))
     got = lax.all_to_all(sent, SEQ, split_axis=0, concat_axis=0, tiled=True)
-    ring_pair = lax.all_gather(pair, "z", axis=0, tiled=True)
     height = got.shape[0]
     got = got.reshape(height, 4, inner_width)
     col_out = recurrence(
@@ -183,12 +177,8 @@
         vertical_cluster_scaling,
     )[0]
     col_sent = col_out.reshape(height, inner_width // 128, 128)
-    col_sent, ring_pair = lax.optimization_barrier((col_sent, ring_pair))
     back = lax.all_to_all(col_sent, SEQ, split_axis=0, concat_axis=0, tiled=True)
     back = back.reshape(full_cols, inner_width)
-    pieces = [ring_pair]
-    for k in range(1, 4):
-        pieces.append(lax.ppermute(ring_pair, "y", [(i, (i - k) % 4) for i in range(4)]))
     partial_value = jnp.dot(
         back, temporal_mix_projection_matrix, preferred_element_type=jnp.float32
     ).astype(jnp.bfloat16)
@@ -196,11 +186,10 @@
     residual = (tokens.astype(jnp.float32) + attended).astype(jnp.bfloat16)
     mix_input = layer_norm(residual, later_standardize_scaling)
 
-    places = unit_order(depth, width)
+    places = unit_order(planes, depth, width)
     moved = (jnp.arange(model_width)[:, None] == places[None, :]).astype(jnp.bfloat16)
     mix_input = jnp.dot(mix_input, moved, preferred_element_type=jnp.float32).astype(jnp.bfloat16)
     mix_all = from_everyone(mix_input, MIX).reshape(-1, model_width)
-    weights = jnp.concatenate(pieces, axis=0)
     hidden_pre = jnp.dot(mix_all, weights, preferred_element_type=jnp.float32)
     positive = jnp.maximum(hidden_pre[:, : units // 2], 0.0)
     hidden = (positive * positive).astype(jnp.bfloat16)

time: 170 us -> 161 us (0.947)
  starting transfers between devices: 61.4 us -> 27.5 us
  between operations: 0.52 us -> 13.9 us
  waiting for transfers between devices: 17 us -> 25.6 us
  blocking collectives: 62.3 us -> 69.6 us
  local copies, waits for them, and re-layouts: 9.7 us -> 6.36 us
    all_to_all x0 -> x2, blocking collectives: none -> 36.9 us  [the longest x1 23.5 us: shards(): lax.all_to_all(col_sent, SEQ, split_axis=0, concat_axis=0, tiled=True)]
    all_gather x1 -> x0, blocking collectives: 36 us -> none  [shards(): ring_pair = lax.all_gather(pair, 'z', axis=0, tiled=True)]
    all_to_all x1, waiting for transfers between devices: 0.01 us -> 18.8 us  [shards(): got = lax.all_to_all(sent, SEQ, split_axis=0, concat_axis=0, tiled=True)]
    all_to_all x2 -> x1, starting transfers between devices: 20.6 us -> 3.42 us  [shards(): lax.all_to_all(shares.reshape(planes, width, units), PLANE, 0, 0, tiled=T...]
    ppermute x4 -> x0, starting transfers between devices: 12.7 us -> none  [the longest x3 8.76 us: shards(): lax.ppermute(ring_pair, 'y', [(i, (i - k) % 4) for i in range(4)])]
    all_to_all x2 -> x1, waiting for transfers between devices: 11 us -> 0.01 us  [shards(): lax.all_to_all(shares.reshape(planes, width, units), PLANE, 0, 0, tiled=T...]
    all_to_all x1, starting transfers between devices: 12.2 us -> 7.06 us  [sent_and_summed(): pieces = lax.all_to_all(split_up(value, dim, size), axis, 0, 0, tiled=True)]
    all_to_all x1, blocking collectives: 14.1 us -> 18.4 us  [sent_and_summed(): pieces = lax.all_to_all(split_up(value, dim, size), axis, 0, 0, tiled=True)]
  transfers between devices with their start and end apart: 8 -> 4, of which waited for: 3 -> 2; matrix products, arithmetic and copies ran while one was open for 9% -> 9% of each run, Pallas kernels for 0% -> 0%
where the time goes in v7:
time: 161 us; the launch traced here: 160 us
  blocking collectives  69.6 us (43%)
  starting transfers between devices  27.5 us (17%)
  waiting for transfers between devices  25.6 us (16%)
  matrix products  14.4 us (9%)
  between operations  13.9 us (9%)
  local copies, waits for them, and re-layouts  6.36 us (4%)
  other arithmetic  2.97 us (2%)
    all_to_all x1, blocking collectives, shards(): lax.all_to_all(col_sent, SEQ, split_axis=0, concat_axis=0, tiled=True)  23.5 us
    all_to_all x1, waiting for transfers between devices, shards(): got = lax.all_to_all(sent, SEQ, split_axis=0, concat_axis=0, tiled=True)  18.8 us
    all_to_all x1, blocking collectives, sent_and_summed(): pieces = lax.all_to_all(split_up(value, dim, size), axis, 0, 0, tiled=True)  18.4 us
    all_to_all x1, starting transfers between devices, shards(): got = lax.all_to_all(sent, SEQ, split_axis=0, concat_axis=0, tiled=True)  17 us
    all_gather x1, blocking collectives, shards(): whole_rows = lax.all_gather(tokens, MP, axis=0, tiled=True)  14.2 us
    all_to_all x1, blocking collectives, from_everyone(): return lax.all_to_all(copies, axis, split_axis=0, concat_axis=0, tiled=True)  13.5 us
    all_to_all x1, starting transfers between devices, sent_and_summed(): pieces = lax.all_to_all(split_up(value, dim, size), axis, 0, 0, tiled=True)  7.06 us
    all_to_all x1, waiting for transfers between devices, sent_and_summed(): pieces = lax.all_to_all(split_up(value, dim, size), axis, 0, 0, tiled=True)  6.87 us
  transfers between devices with their start and end apart: 4, of which 2 were waited for; matrix products, arithmetic and copies ran while one was open for 9% of the time, Pallas kernels for 0%

profile of v7, /device:TPU:1, one launch (start us, length us, event | category | flops | bytes accessed | tf_op | source)
XLA Modules:
  0.0 160.3 jit_solution(10452466675199081212)
XLA Ops:
  6.5 0.9 fusion.106
  7.4 0.9 fusion.107
  8.3 14.2 %all-gather = bf16[1,1,128,1152]{3,2,1,0:T(8,128)(2,1)S(1)} all-gather(bf16[1,1,32,1152]{3,2,1,0:T(8,128)(2,1)} %param.15), channel_id=2, replica_groups=mesh['x_lo'=2,'y'=4,'z'=16,'x_hi'=2,'core'=2] {'x_hi','core'}, dimensions={2}, use_global_device_ids=true | all-gather | bytes 368640 | tf_op jit(solution)/shard_map/all_gather | solution.py:117
  22.7 0.7 broadcast_in_dim.45
  23.4 3.4 %all-to-all-start.4 = ((bf16[8,9,1152]{2,1,0:T(8,128)(2,1)}), bf16[8,9,1152]{2,1,0:T(8,128)(2,1)S(1)}, u32[]{:S(2)}, u32[]{:S(2)}) async-start(bf16[8,9,1152]{2,1,0:T(8,128)(2,1)} %bitcast.60), calls=%async_computation.4 | async-start | bytes 589824 | tf_op jit(solution)/shard_map/all_to_all | solution.py:136
  26.9 0.1 convert_reduce_fusion.1
  27.0 0.2 fusion.34
  27.2 1.5 fusion.22
  28.9 0.1 copy.92
  29.0 0.3 reduce_window_sum.17
  29.3 0.1 copy.94
  29.5 0.3 convolution_convert_fusion.4
  29.8 0.1 copy.89
  29.9 0.1 copy.90
  30.0 0.3 convolution_convert_fusion.3
  30.4 0.1 copy.93
  30.6 1.4 convolution_convert_fusion.2
  32.0 0.1 copy.95
  32.1 1.2 convolution_select_fusion.1
  33.4 0.3 fusion.108
  33.6 0.1 copy.96
  33.8 0.1 multiply_reduce_fusion.2
  34.3 0.2 copy.98
  34.5 0.9 copy.99
  35.4 17.0 %all-to-all-start = ((bf16[128,8,128]{2,1,0:T(8,128)(2,1)}), bf16[128,8,128]{2,1,0:T(8,128)(2,1)S(1)}, u32[]{:S(2)}, u32[]{:S(2)}) async-start(bf16[128,8,128]{2,1,0:T(8,128)(2,1)} %copy.99), calls=%async_computation | async-start | bytes 524288 | tf_op jit(solution)/shard_map/all_to_all | solution.py:168
  52.4 0.8 reshape.462
  53.2 18.8 %all-to-all-done = bf16[128,8,128]{2,1,0:T(8,128)(2,1)S(1)} async-done(((bf16[128,8,128]{2,1,0:T(8,128)(2,1)}), bf16[128,8,128]{2,1,0:T(8,128)(2,1)S(1)}, u32[]{:S(2)}, u32[]{:S(2)}) %all-to-all-start) | async-done | bytes 262176 | tf_op jit(solution)/shard_map/all_to_all | solution.py:168
  71.9 0.2 copy.100
  72.2 0.1 copy.102
  72.3 0.3 reduce_window_sum.18
  72.7 0.1 copy.103
  72.8 0.1 copy.101
  72.9 1.2 convolution_select_fusion
  74.2 0.3 fusion.109
  74.4 0.1 copy.104
  74.6 0.1 fusion.65
  75.0 23.5 %all_to_all.30 = bf16[128,2,128]{2,1,0:T(2,128)(2,1)S(1)} all-to-all(bf16[128,2,128]{2,1,0:T(2,128)(2,1)S(1)} %copy.106), channel_id=1, replica_groups=mesh['x_lo'=2,'y'=4,'z'=16,'x_hi'=2,'core'=2] {'x_lo','y','z'}, dimensions={0} | all-to-all | bytes 131072 | tf_op jit(solution)/shard_map/all_to_all | solution.py:180
  98.5 1.0 convolution_convert_fusion.1
  99.5 7.1 %all-to-all-start.2 = ((bf16[4,32,1152]{2,1,0:T(8,128)(2,1)}), bf16[4,32,1152]{2,1,0:T(8,128)(2,1)S(1)}, u32[]{:S(2)}, u32[]{:S(2)}) async-start(bf16[4,32,1152]{2,1,0:T(8,128)(2,1)} %bitcast.56), calls=%async_computation.2 | async-start | bytes 589824 | tf_op jit(solution)/shard_map/all_to_all | solution.py:28
  106.5 6.9 %all-to-all-done.2 = bf16[4,32,1152]{2,1,0:T(8,128)(2,1)S(1)} async-done(((bf16[4,32,1152]{2,1,0:T(8,128)(2,1)}), bf16[4,32,1152]{2,1,0:T(8,128)(2,1)S(1)}, u32[]{:S(2)}, u32[]{:S(2)}) %all-to-all-start.2) | async-done | bytes 294944 | tf_op jit(solution)/shard_map/all_to_all | solution.py:28
  113.5 0.1 convert_reduce_fusion.3
  113.6 0.2 fusion.57
  113.8 1.1 fusion.5
  115.0 13.5 %all_to_all.31 = bf16[8,32,1152]{2,1,0:T(8,128)(2,1)S(1)} all-to-all(bf16[8,32,1152]{2,1,0:T(8,128)(2,1)S(1)} %broadcast_in_dim.44), channel_id=1, replica_groups=mesh['x_lo'=2,'y'=4,'z'=16,'x_hi'=2,'core'=2] {'x_lo','x_hi','core'}, dimensions={0} | all-to-all | bytes 1179648 | tf_op jit(solution)/shard_map/all_to_all | solution.py:17
  128.5 2.1 %fusion.14 = bf16[256,576]{0,1:T(8,128)(2,1)S(1)} fusion(bf16[256,1152]{1,0:T(8,128)(2,1)S(1)} %bitcast.142, bf16[1152,1152]{1,0:T(8,128)(2,1)} %all-gather.3.cloned.1.call-done), kind=kOutput, calls=%fused_computation.13 | convolution fusion | flops 340180992 | bytes 2359296 | tf_op jit(solution)/shard_map/dot_general | solution.py:193
  130.6 3.8 %fusion.4 = bf16[256,1152]{1,0:T(8,128)(2,1)S(1)} fusion(s32[1152]{0:T(1024)S(1)} %fusion.84, bf16[1152,1152]{1,0:T(8,128)(2,1)} %all-gather.3.cloned.1.call-done, bf16[256,576]{0,1:T(8,128)(2,1)S(1)} %fusion.14), kind=kOutput, calls=%fused_computation.6 | convolution fusion | flops 1360871424 | bytes 3543552 | tf_op jit(solution)/shard_map/dot_general | solution.py:200
  134.3 18.4 %all_to_all.32 = bf16[8,32,1152]{2,1,0:T(8,128)(2,1)S(1)} all-to-all(bf16[8,32,1152]{2,1,0:T(8,128)(2,1)S(1)} %bitcast.143), channel_id=1, replica_groups=mesh['x_lo'=2,'y'=4,'z'=16,'x_hi'=2,'core'=2] {'x_lo','x_hi','core'}, dimensions={0} | all-to-all | bytes 1179648 | tf_op jit(solution)/shard_map/all_to_all | solution.py:28
  152.8 0.7 fusion.63
  (59 shorter events, 1.5 us)
Async XLA Ops:
  6.5 92.0 %copy-start = (bf16[256,1152]{1,0:T(8,128)(2,1)S(1)}, bf16[256,1152]{1,0:T(8,128)(2,1)}, u32[]{:S(2)}) copy-start(bf16[256,1152]{1,0:T(8,128)(2,1)} %param.26) | copy-start | bytes 1769476
  22.7 6.8 %copy-start.5 = (bf16[1152,256]{1,0:T(8,128)(2,1)S(1)}, bf16[1152,256]{1,0:T(8,128)(2,1)}, u32[]{:S(2)}) copy-start(bf16[1152,256]{1,0:T(8,128)(2,1)} %param.17) | copy-start | bytes 1769476
  22.7 6.8 %copy-start.7 = (f32[1152]{0:T(1024)S(1)}, f32[1152]{0:T(1024)}, u32[]{:S(2)}) copy-start(f32[1152]{0:T(1024)} %param.16) | copy-start | bytes 13828
  23.4 12.0 %all-to-all-start.4 = ((bf16[8,9,1152]{2,1,0:T(8,128)(2,1)}), bf16[8,9,1152]{2,1,0:T(8,128)(2,1)S(1)}, u32[]{:S(2)}, u32[]{:S(2)}) async-start(bf16[8,9,1152]{2,1,0:T(8,128)(2,1)} %bitcast.60), calls=%async_computation.4 | async-start | bytes 589824 | tf_op jit(solution)/shard_map/all_to_all | solution.py:136
  27.2 2.8 %copy-start.6 = (bf16[1152,256]{1,0:T(8,128)(2,1)S(1)}, bf16[1152,256]{1,0:T(8,128)(2,1)}, u32[]{:S(2)}) copy-start(bf16[1152,256]{1,0:T(8,128)(2,1)} %param.18) | copy-start | bytes 1769476
  30.0 3.7 %copy-start.4 = (f32[256]{0:T(256)S(1)}, f32[256]{0:T(256)}, u32[]{:S(2)}) copy-start(f32[256]{0:T(256)} %param.23) | copy-start | bytes 3076
  30.6 3.6 %copy-start.2 = (f32[256]{0:T(256)S(1)}, f32[256]{0:T(256)}, u32[]{:S(2)}) copy-start(f32[256]{0:T(256)} %param.24) | copy-start | bytes 3076
  35.4 36.5 %all-to-all-start = ((bf16[128,8,128]{2,1,0:T(8,128)(2,1)}), bf16[128,8,128]{2,1,0:T(8,128)(2,1)S(1)}, u32[]{:S(2)}, u32[]{:S(2)}) async-start(bf16[128,8,128]{2,1,0:T(8,128)(2,1)} %copy.99), calls=%async_computation | async-start | bytes 524288 | tf_op jit(solution)/shard_map/all_to_all | solution.py:168
  52.4 76.1 %all-gather.3.cloned.1.call-start = ((), (), s32[]{:S(2)}) async-start(), calls=%async_computation.6 | async-start | bytes 2820096 | tf_op jit(solution)/shard_map/all_gather | solution.py:138
  72.6 2.3 %copy-start.3 = (f32[256]{0:T(256)S(1)}, f32[256]{0:T(256)}, u32[]{:S(2)}) copy-start(f32[256]{0:T(256)} %param.25) | copy-start | bytes 3076
  74.2 39.3 %copy-start.1 = (bf16[1,1,32,1152]{3,2,1,0:T(8,128)(2,1)S(1)}, bf16[1,1,32,1152]{3,2,1,0:T(8,128)(2,1)}, u32[]{:S(2)}) copy-start(bf16[1,1,32,1152]{3,2,1,0:T(8,128)(2,1)} %param.15) | copy-start | bytes 221188
  74.2 39.6 %copy-start.8 = (f32[1152]{0:T(1024)S(1)}, f32[1152]{0:T(1024)}, u32[]{:S(2)}) copy-start(f32[1152]{0:T(1024)} %param.27) | copy-start | bytes 13828
  99.5 13.9 %all-to-all-start.2 = ((bf16[4,32,1152]{2,1,0:T(8,128)(2,1)}), bf16[4,32,1152]{2,1,0:T(8,128)(2,1)S(1)}, u32[]{:S(2)}, u32[]{:S(2)}) async-start(bf16[4,32,1152]{2,1,0:T(8,128)(2,1)} %bitcast.56), calls=%async_computation.2 | async-start | bytes 589824 | tf_op jit(solution)/shard_map/all_to_all | solution.py:28
Sparse Core Ops, SparseCore 0:
  55.2 66.7 all-gather.2

commit v8 on v6

--- a/solution.py
+++ b/solution.py
@@ -1,6 +1,7 @@
 import jax
 import jax.numpy as jnp
 from jax import lax
+from jax.experimental import pallas as pl
 from jax.sharding import Mesh
 from jax.sharding import PartitionSpec as P
 
@@ -9,11 +10,6 @@
 SEQ = ("x_lo", "y", "z")
 MP = ("x_hi", "core")
 PLANE = ("x_lo", "y")
-
-
-def from_everyone(value, axis):
-    copies = jnp.broadcast_to(value, (lax.axis_size(axis), *value.shape))
-    return lax.all_to_all(copies, axis, split_axis=0, concat_axis=0, tiled=True)
 
 
 def split_up(value, dim, size):
@@ -86,6 +82,22 @@
         .reshape(number, length, inner_width)
     )
     return (normed * gain).astype(jnp.bfloat16)
+
+
+def copies_body(up_ref, down_ref, out_ref):
+    units = up_ref.shape[1]
+    for plane in range(out_ref.shape[0]):
+        out_ref[plane, :, :units] = up_ref[...]
+        out_ref[plane, :, units:] = down_ref[...]
+
+
+def side_by_side(up, down, planes):
+    width, units = up.shape
+    return pl.pallas_call(
+        copies_body,
+        out_shape=jax.ShapeDtypeStruct((planes, width, 2 * units), up.dtype),
+        name="side_by_side",
+    )(up, down)
 
 
 def unit_order(planes, depth, width):
@@ -115,20 +127,19 @@
 ):
     images, row_count, part_cols, model_width = incoming_image_patches.shape
     tokens = incoming_image_patches.reshape(part_cols, model_width)
-    whole_rows = lax.all_gather(tokens, MP, axis=0, tiled=True)
+    planes, depth = lax.axis_size(PLANE), lax.axis_size("z")
+    width, units = feature_mix_addressing_matrix.shape
+    copies = side_by_side(
+        feature_mix_addressing_matrix, feature_mix_content_matrix.T, planes
+    )
+    plane_pair = lax.all_to_all(copies, PLANE, 0, 0, tiled=True)
+    plane_pair = plane_pair.reshape(planes * width, 2 * units)
+    plane_pair, tokens_then = lax.optimization_barrier((plane_pair, tokens))
+    full_pair = lax.all_gather(plane_pair, "z", axis=0, tiled=True)
+
+    whole_rows = lax.all_gather(tokens_then, MP, axis=0, tiled=True)
     full_cols = whole_rows.shape[0]
     inner_width = acceptance_matrix.shape[1]
-
-    planes, depth = lax.axis_size(PLANE), lax.axis_size("z")
-    width = feature_mix_addressing_matrix.shape[0]
-    pair = jnp.stack([feature_mix_addressing_matrix, feature_mix_content_matrix.T])
-    plane_pair = from_everyone(pair, PLANE)
-    plane_pair = plane_pair.reshape(planes, *pair.shape)
-    plane_pair = jnp.swapaxes(plane_pair, 0, 1).reshape(2 * planes * width, -1)
-    full_pair = lax.all_gather(plane_pair, "z", axis=0, tiled=True)
-    full_pair = full_pair.reshape(depth, 2, planes * width, -1)
-    full_up = full_pair[:, 0].reshape(model_width, -1)
-    full_down = full_pair[:, 1].reshape(model_width, -1)
 
     xn1 = layer_norm(whole_rows, initial_standardize_scaling)
     recept = jnp.dot(xn1, acceptance_matrix, preferred_element_type=jnp.float32).astype(
@@ -187,11 +198,11 @@
     moved = (jnp.arange(model_width)[:, None] == places[None, :]).astype(jnp.bfloat16)
     mix_input = jnp.dot(mix_input, moved, preferred_element_type=jnp.float32).astype(jnp.bfloat16)
     mix_all = lax.all_gather(mix_input, MP, axis=0, tiled=True)
-    hidden_pre = jnp.dot(mix_all, full_up, preferred_element_type=jnp.float32)
+    hidden_pre = jnp.dot(mix_all, full_pair[:, :units], preferred_element_type=jnp.float32)
     positive = jnp.maximum(hidden_pre, 0.0)
     hidden = (positive * positive).astype(jnp.bfloat16)
     downward = lax.dot_general(
-        hidden, full_down, (((1,), (1,)), ((), ())), preferred_element_type=jnp.float32
+        hidden, full_pair[:, units:], (((1,), (1,)), ((), ())), preferred_element_type=jnp.float32
     ).astype(jnp.bfloat16)
     downward = lax.dot_general(
         downward, moved, (((1,), (1,)), ((), ())), preferred_element_type=jnp.float32

time: 155 us -> 157 us (1.013)
  local copies, waits for them, and re-layouts: 6.52 us -> 3.9 us
  matrix products: 11.4 us -> 13.5 us
  blocking collectives: 105 us -> 107 us
  Pallas kernels: 0 us -> 1.76 us
    slice x1 -> x0, local copies, waits for them, and re-layouts: 3 us -> none  [shards(): full_down = full_pair[:, 1].reshape(model_width, -1)]
    dot_general x1, matrix products: 1.3 us -> 3.89 us  [shards(): lax.dot_general(hidden, full_pair[:, units:], (((1,), (1,)), ((), ())), p...]
    dot_general x1, matrix products: 3.58 us -> 1.12 us  [shards(): lax.dot_general(downward, moved, (((1,), (1,)), ((), ())), preferred_elem...]
    pallas_call x0 -> x1, Pallas kernels: none -> 1.76 us  [side_by_side(): pl.pallas_call(copies_body, out_shape=jax.ShapeDtypeStruct((planes, width...]
  transfers between devices with their start and end apart: 2 -> 2, of which waited for: 1 -> 1; matrix products, arithmetic and copies ran while one was open for 7% -> 9% of each run, Pallas kernels for 0% -> 0%
where the time goes in v8:
time: 157 us
  blocking collectives  107 us (68%)
  between operations  13.8 us (9%)
  matrix products  13.5 us (9%)
  starting transfers between devices  7.54 us (5%)
  waiting for transfers between devices  6.88 us (4%)
  local copies, waits for them, and re-layouts  3.9 us (2%)
  other arithmetic  2.81 us (2%)
  Pallas kernels  1.76 us (1%)
    all_to_all x1, blocking collectives, shards(): got = lax.all_to_all(sent, SEQ, split_axis=0, concat_axis=0, tiled=True)  39.3 us
    all_to_all x1, blocking collectives, shards(): lax.all_to_all(col_out.reshape(height, inner_width // 128, 128), SEQ, spl...  22.4 us
    all_to_all x1, blocking collectives, shards(): plane_pair = lax.all_to_all(copies, PLANE, 0, 0, tiled=True)  13.9 us
    all_gather x1, blocking collectives, shards(): whole_rows = lax.all_gather(tokens_then, MP, axis=0, tiled=True)  12.9 us
    all_to_all x1, blocking collectives, sent_and_summed(): pieces = lax.all_to_all(split_up(value, dim, size), axis, 0, 0, tiled=True)  9.81 us
    all_gather x1, blocking collectives, shards(): mix_all = lax.all_gather(mix_input, MP, axis=0, tiled=True)  8.17 us
    all_to_all x1, starting transfers between devices, sent_and_summed(): pieces = lax.all_to_all(split_up(value, dim, size), axis, 0, 0, tiled=True)  7.51 us
    all_to_all x1, waiting for transfers between devices, sent_and_summed(): pieces = lax.all_to_all(split_up(value, dim, size), axis, 0, 0, tiled=True)  6.87 us
  transfers between devices with their start and end apart: 2, of which 1 were waited for; matrix products, arithmetic and copies ran while one was open for 9% of the time, Pallas kernels for 0%

profile of v8, /device:TPU:1, one launch (start us, length us, event | category | flops | bytes accessed | tf_op | source)
XLA Modules:
  0.0 156.8 jit_solution(5327620255501367851)
XLA Ops:
  6.6 1.8 %side_by_side.1 = bf16[8,9,2304]{2,1,0:T(8,128)(2,1)} custom-call(bf16[9,1152]{1,0:T(8,128)(2,1)} %up_ref.1, bf16[9,1152]{1,0:T(8,128)(2,1)} %bitcast.147), custom_call_target="tpu_custom_call" | custom-call | tf_op jit(solution)/shard_map/side_by_side/pallas_call | solution.py:96
  8.3 13.9 %all_to_all.25 = bf16[8,9,2304]{2,1,0:T(8,128)(2,1)S(1)} all-to-all(bf16[8,9,2304]{2,1,0:T(8,128)(2,1)} %side_by_side.1), channel_id=1, replica_groups=mesh['x_lo'=2,'y'=4,'z'=16,'x_hi'=2,'core'=2] {'x_lo','y'}, dimensions={0} | all-to-all | bytes 663552 | tf_op jit(solution)/shard_map/all_to_all | solution.py:135
  22.3 0.9 reshape.431
  23.2 0.8 mul.219
  24.1 12.9 %all_gather.9 = bf16[128,1152]{1,0:T(8,128)(2,1)S(1)} all-gather(bf16[32,1152]{1,0:T(8,128)(2,1)} %bitcast.127), channel_id=1, replica_groups=mesh['x_lo'=2,'y'=4,'z'=16,'x_hi'=2,'core'=2] {'x_hi','core'}, dimensions={0}, use_global_device_ids=true | all-gather | bytes 368640 | tf_op jit(solution)/shard_map/all_gather | solution.py:140
  37.0 0.1 convert_reduce_fusion
  37.2 0.2 fusion.41
  37.4 1.5 fusion.29
  38.9 0.1 copy.91
  39.0 0.1 copy.92
  39.1 0.3 reduce_window_sum.17
  39.5 0.1 copy.94
  39.6 0.3 convolution_convert_fusion.3
  39.9 0.1 copy.89
  40.0 0.1 copy.90
  40.2 0.3 convolution_convert_fusion.2
  40.5 0.1 copy.93
  40.6 1.4 convolution_convert_fusion.1
  42.0 0.1 copy.95
  42.1 1.2 convolution_select_fusion.1
  43.3 0.3 fusion.108
  43.6 0.1 copy.96
  43.7 0.1 multiply_reduce_fusion.2
  44.0 0.1 copy.97
  44.2 0.2 copy.98
  44.3 0.2 copy.99
  44.5 39.3 %all_to_all.26 = bf16[128,8,128]{2,1,0:T(8,128)(2,1)S(1)} all-to-all(bf16[128,8,128]{2,1,0:T(8,128)(2,1)S(1)} %copy.99), channel_id=1, replica_groups=mesh['x_lo'=2,'y'=4,'z'=16,'x_hi'=2,'core'=2] {'x_lo','y','z'}, dimensions={0} | all-to-all | bytes 524288 | tf_op jit(solution)/shard_map/all_to_all | solution.py:172
  83.8 0.2 copy.100
  84.1 0.1 copy.102
  84.2 0.3 reduce_window_sum.18
  84.5 0.1 copy.103
  84.7 0.1 copy.101
  84.8 1.2 convolution_select_fusion
  86.0 0.2 fusion.109
  86.3 0.1 copy.104
  86.4 0.1 fusion.69
  86.9 22.4 %all_to_all.27 = bf16[128,2,128]{2,1,0:T(2,128)(2,1)S(1)} all-to-all(bf16[128,2,128]{2,1,0:T(2,128)(2,1)S(1)} %copy.106), channel_id=1, replica_groups=mesh['x_lo'=2,'y'=4,'z'=16,'x_hi'=2,'core'=2] {'x_lo','y','z'}, dimensions={0} | all-to-all | bytes 131072 | tf_op jit(solution)/shard_map/all_to_all | solution.py:183
  109.3 1.0 convolution_convert_fusion
  110.3 7.5 %all-to-all-start.3 = ((bf16[4,32,1152]{2,1,0:T(8,128)(2,1)}), bf16[4,32,1152]{2,1,0:T(8,128)(2,1)S(1)}, u32[]{:S(2)}, u32[]{:S(2)}) async-start(bf16[4,32,1152]{2,1,0:T(8,128)(2,1)} %bitcast.54), calls=%async_computation.3 | async-start | bytes 589824 | tf_op jit(solution)/shard_map/all_to_all | solution.py:23
  117.8 6.9 %all-to-all-done.3 = bf16[4,32,1152]{2,1,0:T(8,128)(2,1)S(1)} async-done(((bf16[4,32,1152]{2,1,0:T(8,128)(2,1)}), bf16[4,32,1152]{2,1,0:T(8,128)(2,1)S(1)}, u32[]{:S(2)}, u32[]{:S(2)}) %all-to-all-start.3) | async-done | bytes 294944 | tf_op jit(solution)/shard_map/all_to_all | solution.py:23
  124.7 0.1 convert_reduce_fusion.3
  124.9 0.2 fusion.63
  125.1 1.1 fusion.21
  126.2 8.2 %all_gather.10 = bf16[128,1152]{1,0:T(8,128)(2,1)S(1)} all-gather(bf16[32,1152]{1,0:T(8,128)(2,1)S(1)} %fusion.21), channel_id=1, replica_groups=mesh['x_lo'=2,'y'=4,'z'=16,'x_hi'=2,'core'=2] {'x_hi','core'}, dimensions={0}, use_global_device_ids=true | all-gather | bytes 368640 | tf_op jit(solution)/shard_map/all_gather | solution.py:200
  134.4 3.9 %fusion.17 = bf16[128,1152]{1,0:T(8,128)(2,1)S(1)} fusion(bf16[1152,2304]{1,0:T(8,128)(2,1)} %all-gather.2.cloned.1.call-done, bf16[128,1152]{1,0:T(8,128)(2,1)S(1)} %all_gather.10), kind=kOutput, calls=%fused_computation.12 | convolution fusion | flops 680067072 | bytes 5898240 | tf_op jit(solution)/shard_map/dot_general | solution.py:204
  138.3 1.1 fusion.20
  139.4 9.8 %all_to_all.28 = bf16[4,32,1152]{2,1,0:T(8,128)(2,1)S(1)} all-to-all(bf16[4,32,1152]{2,1,0:T(8,128)(2,1)S(1)} %bitcast.137), channel_id=1, replica_groups=mesh['x_lo'=2,'y'=4,'z'=16,'x_hi'=2,'core'=2] {'x_hi','core'}, dimensions={0} | all-to-all | bytes 589824 | tf_op jit(solution)/shard_map/all_to_all | solution.py:23
  149.2 0.7 fusion.66
  (50 shorter events, 1.0 us)
Async XLA Ops:
  6.5 102.8 %copy-start = (bf16[256,1152]{1,0:T(8,128)(2,1)S(1)}, bf16[256,1152]{1,0:T(8,128)(2,1)}, u32[]{:S(2)}) copy-start(bf16[256,1152]{1,0:T(8,128)(2,1)} %param.26) | copy-start | bytes 1769476
  6.5 33.0 %copy-start.6 = (f32[1152]{0:T(1024)S(1)}, f32[1152]{0:T(1024)}, u32[]{:S(2)}) copy-start(f32[1152]{0:T(1024)} %param.16) | copy-start | bytes 13828
  6.5 33.0 %copy-start.4 = (bf16[1152,256]{1,0:T(8,128)(2,1)S(1)}, bf16[1152,256]{1,0:T(8,128)(2,1)}, u32[]{:S(2)}) copy-start(bf16[1152,256]{1,0:T(8,128)(2,1)} %param.17) | copy-start | bytes 1769476
  6.5 33.6 %copy-start.5 = (bf16[1152,256]{1,0:T(8,128)(2,1)S(1)}, bf16[1152,256]{1,0:T(8,128)(2,1)}, u32[]{:S(2)}) copy-start(bf16[1152,256]{1,0:T(8,128)(2,1)} %param.18) | copy-start | bytes 1769476
  6.5 127.8 %all-gather.2.cloned.1.call-start = ((), (), s32[]{:S(2)}) async-start(), calls=%async_computation.5 | async-start | bytes 5640192 | tf_op jit(solution)/shard_map/all_gather | solution.py:138
  39.0 5.1 %copy-start.2 = (f32[256]{0:T(256)S(1)}, f32[256]{0:T(256)}, u32[]{:S(2)}) copy-start(f32[256]{0:T(256)} %param.24) | copy-start | bytes 3076
  43.9 42.9 %copy-start.3 = (f32[256]{0:T(256)S(1)}, f32[256]{0:T(256)}, u32[]{:S(2)}) copy-start(f32[256]{0:T(256)} %param.25) | copy-start | bytes 3076
  44.5 80.2 %copy-start.1 = (bf16[1,1,32,1152]{3,2,1,0:T(8,128)(2,1)S(1)}, bf16[1,1,32,1152]{3,2,1,0:T(8,128)(2,1)}, u32[]{:S(2)}) copy-start(bf16[1,1,32,1152]{3,2,1,0:T(8,128)(2,1)} %param.15) | copy-start | bytes 221188
  83.8 41.2 %copy-start.7 = (f32[1152]{0:T(1024)S(1)}, f32[1152]{0:T(1024)}, u32[]{:S(2)}) copy-start(f32[1152]{0:T(1024)} %param.27) | copy-start | bytes 13828
  110.3 14.4 %all-to-all-start.3 = ((bf16[4,32,1152]{2,1,0:T(8,128)(2,1)}), bf16[4,32,1152]{2,1,0:T(8,128)(2,1)S(1)}, u32[]{:S(2)}, u32[]{:S(2)}) async-start(bf16[4,32,1152]{2,1,0:T(8,128)(2,1)} %bitcast.54), calls=%async_computation.3 | async-start | bytes 589824 | tf_op jit(solution)/shard_map/all_to_all | solution.py:23
Sparse Core Ops, SparseCore 0:
  23.3 93.6 all-gather.1

commit v9 on v6

--- a/solution.py
+++ b/solution.py
@@ -86,6 +86,11 @@
         .reshape(number, length, inner_width)
     )
     return (normed * gain).astype(jnp.bfloat16)
+
+
+def log_decay(latent, right_factor, baseline):
+    raised = baseline + jnp.dot(latent, right_factor, preferred_element_type=jnp.float32)
+    return (-0.7 * jax.nn.sigmoid(raised)).astype(jnp.bfloat16)
 
 
 def unit_order(planes, depth, width):
@@ -121,14 +126,11 @@
 
     planes, depth = lax.axis_size(PLANE), lax.axis_size("z")
     width = feature_mix_addressing_matrix.shape[0]
-    pair = jnp.stack([feature_mix_addressing_matrix, feature_mix_content_matrix.T])
+    pair = jnp.concatenate([feature_mix_addressing_matrix, feature_mix_content_matrix.T], axis=1)
+    units = feature_mix_addressing_matrix.shape[1]
     plane_pair = from_everyone(pair, PLANE)
-    plane_pair = plane_pair.reshape(planes, *pair.shape)
-    plane_pair = jnp.swapaxes(plane_pair, 0, 1).reshape(2 * planes * width, -1)
+    plane_pair = plane_pair.reshape(planes * width, 2 * units)
     full_pair = lax.all_gather(plane_pair, "z", axis=0, tiled=True)
-    full_pair = full_pair.reshape(depth, 2, planes * width, -1)
-    full_up = full_pair[:, 0].reshape(model_width, -1)
-    full_down = full_pair[:, 1].reshape(model_width, -1)
 
     xn1 = layer_norm(whole_rows, initial_standardize_scaling)
     recept = jnp.dot(xn1, acceptance_matrix, preferred_element_type=jnp.float32).astype(
@@ -141,13 +143,7 @@
     latent = jnp.tanh(
         jnp.dot(xn1, forgetting_lowdim_left_factor, preferred_element_type=jnp.float32)
     ).astype(jnp.bfloat16)
-    decay = (
-        -0.7
-        * jax.nn.sigmoid(
-            forgetting_baseline
-            + jnp.dot(latent, forgetting_lowdim_right_factor, preferred_element_type=jnp.float32)
-        )
-    ).astype(jnp.bfloat16)
+    decay = log_decay(latent, forgetting_lowdim_right_factor, forgetting_baseline)
     row_out = recurrence(
         recept[None],
         keying[None],
@@ -156,16 +152,23 @@
         self_token_reward,
         horizontal_cluster_scaling,
     )[0]
-    sent = jnp.stack([recept, keying, decay, row_out], axis=1)
-    sent = sent.reshape(full_cols, 4 * inner_width // 128, 128)
-    got = lax.all_to_all(sent, SEQ, split_axis=0, concat_axis=0, tiled=True)
+    rank = latent.shape[1]
+    lines = 3 * inner_width // 128 + 1
+    sent = jnp.concatenate(
+        [recept, keying, row_out, jnp.pad(latent, ((0, 0), (0, 128 - rank)))], axis=1
+    )
+    got = lax.all_to_all(
+        sent.reshape(full_cols, lines, 128), SEQ, split_axis=0, concat_axis=0, tiled=True
+    )
     height = got.shape[0]
-    got = got.reshape(height, 4, inner_width)
+    got = got.reshape(height, 128 * lines)
+    col_latent = got[:, 3 * inner_width : 3 * inner_width + rank]
+    col_decay = log_decay(col_latent, forgetting_lowdim_right_factor, forgetting_baseline)
     col_out = recurrence(
-        got[None, :, 0],
-        got[None, :, 1],
-        got[None, :, 2],
-        got[None, :, 3],
+        got[None, :, :inner_width],
+        got[None, :, inner_width : 2 * inner_width],
+        col_decay[None],
+        got[None, :, 2 * inner_width : 3 * inner_width],
         self_token_reward,
         vertical_cluster_scaling,
     )[0]
@@ -187,11 +190,11 @@
     moved = (jnp.arange(model_width)[:, None] == places[None, :]).astype(jnp.bfloat16)
     mix_input = jnp.dot(mix_input, moved, preferred_element_type=jnp.float32).astype(jnp.bfloat16)
     mix_all = lax.all_gather(mix_input, MP, axis=0, tiled=True)
-    hidden_pre = jnp.dot(mix_all, full_up, preferred_element_type=jnp.float32)
+    hidden_pre = jnp.dot(mix_all, full_pair[:, :units], preferred_element_type=jnp.float32)
     positive = jnp.maximum(hidden_pre, 0.0)
     hidden = (positive * positive).astype(jnp.bfloat16)
     downward = lax.dot_general(
-        hidden, full_down, (((1,), (1,)), ((), ())), preferred_element_type=jnp.float32
+        hidden, full_pair[:, units:], (((1,), (1,)), ((), ())), preferred_element_type=jnp.float32
     ).astype(jnp.bfloat16)
     downward = lax.dot_general(
         downward, moved, (((1,), (1,)), ((), ())), preferred_element_type=jnp.float32

time: 155 us -> 151 us (0.974)
  blocking collectives: 105 us -> 96 us
  starting transfers between devices: 7.18 us -> 12.4 us
  local copies, waits for them, and re-layouts: 6.52 us -> 4.87 us
    all_to_all x2 -> x1, blocking collectives: 52 us -> 43.5 us  [shards(): lax.all_to_all(sent.reshape(full_cols, lines, 128), SEQ, split_axis=0, co...]
    all_to_all x0 -> x1, starting transfers between devices: none -> 5.94 us  [from_everyone(): return lax.all_to_all(copies, axis, split_axis=0, concat_axis=0, tiled=True)]
    slice x1 -> x0, local copies, waits for them, and re-layouts: 3 us -> none  [shards(): full_down = full_pair[:, 1].reshape(model_width, -1)]
    dot_general x2 -> x4, matrix products: 1.84 us -> 4.58 us  [the longest x1 3.89 us: shards(): lax.dot_general(hidden, full_pair[:, units:], (((1,), (1,)), ((), ())), p...]
    dot_general x1, matrix products: 3.58 us -> 1.12 us  [shards(): lax.dot_general(downward, moved, (((1,), (1,)), ((), ())), preferred_elem...]
  transfers between devices with their start and end apart: 2 -> 3, of which waited for: 1 -> 1; matrix products, arithmetic and copies ran while one was open for 7% -> 9% of each run, Pallas kernels for 0% -> 0%
where the time goes in v9:
time: 151 us
  blocking collectives  96 us (64%)
  between operations  13.9 us (9%)
  matrix products  12.8 us (8%)
  starting transfers between devices  12.4 us (8%)
  waiting for transfers between devices  6.89 us (5%)
  local copies, waits for them, and re-layouts  4.87 us (3%)
  other arithmetic  3.72 us (2%)
    all_to_all x1, blocking collectives, shards(): lax.all_to_all(sent.reshape(full_cols, lines, 128), SEQ, split_axis=0, co...  43.5 us
    all_to_all x1, blocking collectives, shards(): lax.all_to_all(col_out.reshape(height, inner_width // 128, 128), SEQ, spl...  22.5 us
    all_gather x1, blocking collectives, shards(): whole_rows = lax.all_gather(tokens, MP, axis=0, tiled=True)  12.1 us
    all_to_all x1, blocking collectives, sent_and_summed(): pieces = lax.all_to_all(split_up(value, dim, size), axis, 0, 0, tiled=True)  9.82 us
    all_gather x1, blocking collectives, shards(): mix_all = lax.all_gather(mix_input, MP, axis=0, tiled=True)  8.17 us
    all_to_all x1, waiting for transfers between devices, sent_and_summed(): pieces = lax.all_to_all(split_up(value, dim, size), axis, 0, 0, tiled=True)  6.87 us
    all_to_all x1, starting transfers between devices, sent_and_summed(): pieces = lax.all_to_all(split_up(value, dim, size), axis, 0, 0, tiled=True)  6.44 us
    all_to_all x1, starting transfers between devices, from_everyone(): return lax.all_to_all(copies, axis, split_axis=0, concat_axis=0, tiled=True)  5.94 us
  transfers between devices with their start and end apart: 3, of which 1 were waited for; matrix products, arithmetic and copies ran while one was open for 9% of the time, Pallas kernels for 0%

profile of v9, /device:TPU:1, one launch (start us, length us, event | category | flops | bytes accessed | tf_op | source)
XLA Modules:
  0.0 150.6 jit_solution(13768158039658384066)
XLA Ops:
  6.6 0.9 pad_maximum_fusion
  7.5 0.8 broadcast_in_dim.42
  8.3 5.9 %all-to-all-start.3 = ((bf16[8,9,2304]{2,1,0:T(8,128)(2,1)}), bf16[8,9,2304]{2,1,0:T(8,128)(2,1)S(1)}, u32[]{:S(2)}, u32[]{:S(2)}) async-start(bf16[8,9,2304]{2,1,0:T(8,128)(2,1)} %broadcast_in_dim.42), calls=%async_computation.3 | async-start | bytes 1179648 | tf_op jit(solution)/shard_map/all_to_all | solution.py:16
  14.3 0.8 mul.212
  15.1 12.1 %all-gather = bf16[1,1,128,1152]{3,2,1,0:T(8,128)(2,1)S(1)} all-gather(bf16[1,1,32,1152]{3,2,1,0:T(8,128)(2,1)} %param.15), channel_id=2, replica_groups=mesh['x_lo'=2,'y'=4,'z'=16,'x_hi'=2,'core'=2] {'x_hi','core'}, dimensions={2}, use_global_device_ids=true | all-gather | bytes 368640 | tf_op jit(solution)/shard_map/all_gather | solution.py:123
  27.2 0.1 convert_reduce_fusion
  27.3 0.9 reshape.392
  28.2 0.2 fusion.50
  28.4 1.4 convolution_convert_fusion.1
  29.8 0.1 copy.105
  30.0 0.3 convolution_convert_fusion.2
  30.3 0.1 copy.103
  30.4 0.3 convolution_convert_fusion.3
  30.8 0.1 copy.99
  31.0 0.3 fusion.38
  31.3 0.2 fusion.37
  31.6 0.1 copy.102
  31.7 0.3 reduce_window_sum.17
  32.0 0.1 copy.104
  32.3 1.2 convolution_select_fusion.1
  33.6 0.3 fusion.122
  33.8 0.1 copy.106
  34.0 0.1 multiply_reduce_fusion.2
  34.4 0.2 copy.108
  34.6 0.2 copy.109
  34.8 43.5 %all_to_all.25 = bf16[128,7,128]{2,1,0:T(8,128)(2,1)S(1)} all-to-all(bf16[128,7,128]{2,1,0:T(8,128)(2,1)S(1)} %copy.109), channel_id=1, replica_groups=mesh['x_lo'=2,'y'=4,'z'=16,'x_hi'=2,'core'=2] {'x_lo','y','z'}, dimensions={0} | all-to-all | bytes 458752 | tf_op jit(solution)/shard_map/all_to_all | solution.py:160
  78.3 0.2 copy.110
  78.5 0.2 fusion.36
  78.8 0.1 copy.113
  79.0 0.3 reduce_window_sum.18
  79.2 0.1 copy.114
  79.5 0.1 copy.111
  79.6 1.2 convolution_select_fusion
  80.8 0.3 fusion.123
  81.1 0.1 copy.115
  81.2 0.1 fusion.82
  81.7 22.5 %all_to_all.26 = bf16[128,2,128]{2,1,0:T(2,128)(2,1)S(1)} all-to-all(bf16[128,2,128]{2,1,0:T(2,128)(2,1)S(1)} %copy.117), channel_id=1, replica_groups=mesh['x_lo'=2,'y'=4,'z'=16,'x_hi'=2,'core'=2] {'x_lo','y','z'}, dimensions={0} | all-to-all | bytes 131072 | tf_op jit(solution)/shard_map/all_to_all | solution.py:175
  104.2 1.0 convolution_convert_fusion
  105.2 6.4 %all-to-all-start.2 = ((bf16[4,32,1152]{2,1,0:T(8,128)(2,1)}), bf16[4,32,1152]{2,1,0:T(8,128)(2,1)S(1)}, u32[]{:S(2)}, u32[]{:S(2)}) async-start(bf16[4,32,1152]{2,1,0:T(8,128)(2,1)} %bitcast.50), calls=%async_computation.2 | async-start | bytes 589824 | tf_op jit(solution)/shard_map/all_to_all | solution.py:27
  111.6 6.9 %all-to-all-done.2 = bf16[4,32,1152]{2,1,0:T(8,128)(2,1)S(1)} async-done(((bf16[4,32,1152]{2,1,0:T(8,128)(2,1)}), bf16[4,32,1152]{2,1,0:T(8,128)(2,1)S(1)}, u32[]{:S(2)}, u32[]{:S(2)}) %all-to-all-start.2) | async-done | bytes 294944 | tf_op jit(solution)/shard_map/all_to_all | solution.py:27
  118.6 0.1 convert_reduce_fusion.3
  118.7 0.2 fusion.74
  118.9 1.1 fusion.21
  120.0 8.2 %all_gather.10 = bf16[128,1152]{1,0:T(8,128)(2,1)S(1)} all-gather(bf16[32,1152]{1,0:T(8,128)(2,1)S(1)} %fusion.21), channel_id=1, replica_groups=mesh['x_lo'=2,'y'=4,'z'=16,'x_hi'=2,'core'=2] {'x_hi','core'}, dimensions={0}, use_global_device_ids=true | all-gather | bytes 368640 | tf_op jit(solution)/shard_map/all_gather | solution.py:192
  128.2 3.9 %fusion.17 = bf16[128,1152]{1,0:T(8,128)(2,1)S(1)} fusion(bf16[1152,2304]{1,0:T(8,128)(2,1)} %all-gather.3.cloned.1.call-done, bf16[128,1152]{1,0:T(8,128)(2,1)S(1)} %all_gather.10), kind=kOutput, calls=%fused_computation.12 | convolution fusion | flops 680067072 | bytes 5898240 | tf_op jit(solution)/shard_map/dot_general | solution.py:196
  132.1 1.1 fusion.20
  133.2 9.8 %all_to_all.27 = bf16[4,32,1152]{2,1,0:T(8,128)(2,1)S(1)} all-to-all(bf16[4,32,1152]{2,1,0:T(8,128)(2,1)S(1)} %bitcast.156), channel_id=1, replica_groups=mesh['x_lo'=2,'y'=4,'z'=16,'x_hi'=2,'core'=2] {'x_hi','core'}, dimensions={0} | all-to-all | bytes 589824 | tf_op jit(solution)/shard_map/all_to_all | solution.py:27
  143.1 0.7 fusion.80
  (61 shorter events, 1.3 us)
Async XLA Ops:
  6.5 97.7 %copy-start = (bf16[256,1152]{1,0:T(8,128)(2,1)S(1)}, bf16[256,1152]{1,0:T(8,128)(2,1)}, u32[]{:S(2)}) copy-start(bf16[256,1152]{1,0:T(8,128)(2,1)} %param.26) | copy-start | bytes 1769476
  6.5 23.4 %copy-start.8 = (f32[1152]{0:T(1024)S(1)}, f32[1152]{0:T(1024)}, u32[]{:S(2)}) copy-start(f32[1152]{0:T(1024)} %param.16) | copy-start | bytes 13828
  6.5 23.4 %copy-start.4 = (bf16[1152,256]{1,0:T(8,128)(2,1)S(1)}, bf16[1152,256]{1,0:T(8,128)(2,1)}, u32[]{:S(2)}) copy-start(bf16[1152,256]{1,0:T(8,128)(2,1)} %param.18) | copy-start | bytes 1769476
  6.5 23.9 %copy-start.5 = (bf16[1152,256]{1,0:T(8,128)(2,1)S(1)}, bf16[1152,256]{1,0:T(8,128)(2,1)}, u32[]{:S(2)}) copy-start(bf16[1152,256]{1,0:T(8,128)(2,1)} %param.17) | copy-start | bytes 1769476
  6.5 24.4 %copy-start.6 = (bf16[1152,64]{0,1:T(8,128)(2,1)S(1)}, bf16[1152,64]{0,1:T(8,128)(2,1)}, u32[]{:S(2)}) copy-start(bf16[1152,64]{0,1:T(8,128)(2,1)} %param.20) | copy-start | bytes 442372
  6.5 24.7 %copy-start.10 = (f32[256]{0:T(256)S(1)}, f32[256]{0:T(256)}, u32[]{:S(2)}) copy-start(f32[256]{0:T(256)} %param.22) | copy-start | bytes 3076
  6.6 24.7 %copy-start.7 = (bf16[64,256]{1,0:T(8,128)(2,1)S(1)}, bf16[64,256]{1,0:T(8,128)(2,1)}, u32[]{:S(2)}) copy-start(bf16[64,256]{1,0:T(8,128)(2,1)} %param.21) | copy-start | bytes 98308
  8.3 18.9 %all-to-all-start.3 = ((bf16[8,9,2304]{2,1,0:T(8,128)(2,1)}), bf16[8,9,2304]{2,1,0:T(8,128)(2,1)S(1)}, u32[]{:S(2)}, u32[]{:S(2)}) async-start(bf16[8,9,2304]{2,1,0:T(8,128)(2,1)} %broadcast_in_dim.42), calls=%async_computation.3 | async-start | bytes 1179648 | tf_op jit(solution)/shard_map/all_to_all | solution.py:16
  14.3 113.9 %all-gather.3.cloned.1.call-start = ((), (), s32[]{:S(2)}) async-start(), calls=%async_computation.5 | async-start | bytes 5640192 | tf_op jit(solution)/shard_map/all_gather | solution.py:133
  30.0 4.4 %copy-start.2 = (f32[256]{0:T(256)S(1)}, f32[256]{0:T(256)}, u32[]{:S(2)}) copy-start(f32[256]{0:T(256)} %param.24) | copy-start | bytes 3076
  34.3 47.2 %copy-start.3 = (f32[256]{0:T(256)S(1)}, f32[256]{0:T(256)}, u32[]{:S(2)}) copy-start(f32[256]{0:T(256)} %param.25) | copy-start | bytes 3076
  78.3 40.3 %copy-start.1 = (bf16[1,1,32,1152]{3,2,1,0:T(8,128)(2,1)S(1)}, bf16[1,1,32,1152]{3,2,1,0:T(8,128)(2,1)}, u32[]{:S(2)}) copy-start(bf16[1,1,32,1152]{3,2,1,0:T(8,128)(2,1)} %param.15) | copy-start | bytes 221188
  78.5 40.4 %copy-start.9 = (f32[1152]{0:T(1024)S(1)}, f32[1152]{0:T(1024)}, u32[]{:S(2)}) copy-start(f32[1152]{0:T(1024)} %param.27) | copy-start | bytes 13828
  105.2 13.3 %all-to-all-start.2 = ((bf16[4,32,1152]{2,1,0:T(8,128)(2,1)}), bf16[4,32,1152]{2,1,0:T(8,128)(2,1)S(1)}, u32[]{:S(2)}, u32[]{:S(2)}) async-start(bf16[4,32,1152]{2,1,0:T(8,128)(2,1)} %bitcast.50), calls=%async_computation.2 | async-start | bytes 589824 | tf_op jit(solution)/shard_map/all_to_all | solution.py:27
Sparse Core Ops, SparseCore 0:
  28.3 90.2 all-gather.2

commit v10 on v9

--- a/solution.py
+++ b/solution.py
@@ -189,6 +189,10 @@
     places = unit_order(planes, depth, width)
     moved = (jnp.arange(model_width)[:, None] == places[None, :]).astype(jnp.bfloat16)
     mix_input = jnp.dot(mix_input, moved, preferred_element_type=jnp.float32).astype(jnp.bfloat16)
+    stored_residual = jnp.dot(residual, moved, preferred_element_type=jnp.float32).astype(
+        jnp.bfloat16
+    )
+    mix_input, stored_residual = lax.optimization_barrier((mix_input, stored_residual))
     mix_all = lax.all_gather(mix_input, MP, axis=0, tiled=True)
     hidden_pre = jnp.dot(mix_all, full_pair[:, :units], preferred_element_type=jnp.float32)
     positive = jnp.maximum(hidden_pre, 0.0)
@@ -196,11 +200,11 @@
     downward = lax.dot_general(
         hidden, full_pair[:, units:], (((1,), (1,)), ((), ())), preferred_element_type=jnp.float32
     ).astype(jnp.bfloat16)
-    downward = lax.dot_general(
-        downward, moved, (((1,), (1,)), ((), ())), preferred_element_type=jnp.float32
-    ).astype(jnp.bfloat16)
     mixed = sent_and_summed(downward, MP, 0)
-    block_out = (residual.astype(jnp.float32) + mixed).astype(jnp.bfloat16)
+    stored_out = (stored_residual.astype(jnp.float32) + mixed).astype(jnp.bfloat16)
+    block_out = lax.dot_general(
+        stored_out, moved, (((1,), (1,)), ((), ())), preferred_element_type=jnp.float32
+    ).astype(jnp.bfloat16)
     return block_out.reshape(images, row_count, part_cols, model_width)
 
 

time: 151 us -> 152 us (level)
  matrix products: 12.8 us -> 14.5 us
    dot_general x1 -> x2, matrix products: 1.12 us -> 2.85 us  [the longest x1 1.73 us: shards(): lax.dot_general(stored_out, moved, (((1,), (1,)), ((), ())), preferred_el...]
where the time goes in v10:
time: 152 us
  blocking collectives  96.3 us (63%)
  matrix products  14.5 us (10%)
  between operations  13.9 us (9%)
  starting transfers between devices  12 us (8%)
  waiting for transfers between devices  6.89 us (5%)
  local copies, waits for them, and re-layouts  4.87 us (3%)
  other arithmetic  3.06 us (2%)
    all_to_all x1, blocking collectives, shards(): lax.all_to_all(sent.reshape(full_cols, lines, 128), SEQ, split_axis=0, co...  43.4 us
    all_to_all x1, blocking collectives, shards(): lax.all_to_all(col_out.reshape(height, inner_width // 128, 128), SEQ, spl...  22.9 us
    all_gather x1, blocking collectives, shards(): whole_rows = lax.all_gather(tokens, MP, axis=0, tiled=True)  12.1 us
    all_to_all x1, blocking collectives, sent_and_summed(): pieces = lax.all_to_all(split_up(value, dim, size), axis, 0, 0, tiled=True)  9.82 us
    all_gather x1, blocking collectives, shards(): mix_all = lax.all_gather(mix_input, MP, axis=0, tiled=True)  8.17 us
    all_to_all x1, waiting for transfers between devices, sent_and_summed(): pieces = lax.all_to_all(split_up(value, dim, size), axis, 0, 0, tiled=True)  6.87 us
    all_to_all x1, starting transfers between devices, sent_and_summed(): pieces = lax.all_to_all(split_up(value, dim, size), axis, 0, 0, tiled=True)  6.02 us
    all_to_all x1, starting transfers between devices, from_everyone(): return lax.all_to_all(copies, axis, split_axis=0, concat_axis=0, tiled=True)  5.94 us
  transfers between devices with their start and end apart: 3, of which 1 were waited for; matrix products, arithmetic and copies ran while one was open for 9% of the time, Pallas kernels for 0%

profile of v10, /device:TPU:1, one launch (start us, length us, event | category | flops | bytes accessed | tf_op | source)
XLA Modules:
  0.0 151.5 jit_solution(5111828557107634260)
XLA Ops:
  6.6 0.9 pad_maximum_fusion
  7.5 0.8 broadcast_in_dim.42
  8.3 5.9 %all-to-all-start.3 = ((bf16[8,9,2304]{2,1,0:T(8,128)(2,1)}), bf16[8,9,2304]{2,1,0:T(8,128)(2,1)S(1)}, u32[]{:S(2)}, u32[]{:S(2)}) async-start(bf16[8,9,2304]{2,1,0:T(8,128)(2,1)} %broadcast_in_dim.42), calls=%async_computation.3 | async-start | bytes 1179648 | tf_op jit(solution)/shard_map/all_to_all | solution.py:16
  14.3 0.8 mul.216
  15.1 12.1 %all-gather = bf16[1,1,128,1152]{3,2,1,0:T(8,128)(2,1)S(1)} all-gather(bf16[1,1,32,1152]{3,2,1,0:T(8,128)(2,1)} %param.15), channel_id=2, replica_groups=mesh['x_lo'=2,'y'=4,'z'=16,'x_hi'=2,'core'=2] {'x_hi','core'}, dimensions={2}, use_global_device_ids=true | all-gather | bytes 368640 | tf_op jit(solution)/shard_map/all_gather | solution.py:123
  27.2 0.1 convert_reduce_fusion
  27.3 0.9 reshape.392
  28.2 0.2 fusion.54
  28.4 1.4 convolution_convert_fusion.1
  29.8 0.1 copy.105
  30.0 0.3 convolution_convert_fusion.2
  30.3 0.1 copy.103
  30.4 0.3 convolution_convert_fusion.3
  30.8 0.1 copy.99
  31.0 0.3 fusion.42
  31.3 0.2 fusion.41
  31.6 0.1 copy.102
  31.7 0.3 reduce_window_sum.17
  32.0 0.1 copy.104
  32.3 1.2 convolution_select_fusion.1
  33.6 0.3 fusion.123
  33.8 0.1 copy.106
  34.0 0.1 multiply_reduce_fusion.2
  34.4 0.2 copy.108
  34.6 0.2 copy.109
  34.8 43.4 %all_to_all.25 = bf16[128,7,128]{2,1,0:T(8,128)(2,1)S(1)} all-to-all(bf16[128,7,128]{2,1,0:T(8,128)(2,1)S(1)} %copy.109), channel_id=1, replica_groups=mesh['x_lo'=2,'y'=4,'z'=16,'x_hi'=2,'core'=2] {'x_lo','y','z'}, dimensions={0} | all-to-all | bytes 458752 | tf_op jit(solution)/shard_map/all_to_all | solution.py:160
  78.2 0.2 copy.110
  78.4 0.2 fusion.40
  78.7 0.1 copy.113
  78.9 0.3 reduce_window_sum.18
  79.1 0.1 copy.114
  79.4 0.1 copy.111
  79.5 1.2 convolution_select_fusion
  80.7 0.3 fusion.124
  81.0 0.1 copy.115
  81.1 0.1 fusion.83
  81.6 22.9 %all_to_all.26 = bf16[128,2,128]{2,1,0:T(2,128)(2,1)S(1)} all-to-all(bf16[128,2,128]{2,1,0:T(2,128)(2,1)S(1)} %copy.117), channel_id=1, replica_groups=mesh['x_lo'=2,'y'=4,'z'=16,'x_hi'=2,'core'=2] {'x_lo','y','z'}, dimensions={0} | all-to-all | bytes 131072 | tf_op jit(solution)/shard_map/all_to_all | solution.py:175
  104.5 1.0 convolution_convert_fusion
  105.5 6.0 %all-to-all-start.2 = ((bf16[4,32,1152]{2,1,0:T(8,128)(2,1)}), bf16[4,32,1152]{2,1,0:T(8,128)(2,1)S(1)}, u32[]{:S(2)}, u32[]{:S(2)}) async-start(bf16[4,32,1152]{2,1,0:T(8,128)(2,1)} %bitcast.51), calls=%async_computation.2 | async-start | bytes 589824 | tf_op jit(solution)/shard_map/all_to_all | solution.py:27
  111.5 6.9 %all-to-all-done.2 = bf16[4,32,1152]{2,1,0:T(8,128)(2,1)S(1)} async-done(((bf16[4,32,1152]{2,1,0:T(8,128)(2,1)}), bf16[4,32,1152]{2,1,0:T(8,128)(2,1)S(1)}, u32[]{:S(2)}, u32[]{:S(2)}) %all-to-all-start.2) | async-done | bytes 294944 | tf_op jit(solution)/shard_map/all_to_all | solution.py:27
  118.4 0.1 convert_reduce_fusion.3
  118.6 0.2 fusion.78
  118.8 1.1 fusion.23
  119.9 1.1 fusion.22
  121.0 8.2 %all_gather.10 = bf16[128,1152]{1,0:T(8,128)(2,1)S(1)} all-gather(bf16[32,1152]{1,0:T(8,128)(2,1)S(1)} %fusion.22), channel_id=1, replica_groups=mesh['x_lo'=2,'y'=4,'z'=16,'x_hi'=2,'core'=2] {'x_hi','core'}, dimensions={0}, use_global_device_ids=true | all-gather | bytes 368640 | tf_op jit(solution)/shard_map/all_gather | solution.py:196
  129.2 3.9 %fusion.19 = bf16[128,1152]{1,0:T(8,128)(2,1)S(1)} fusion(bf16[1152,2304]{1,0:T(8,128)(2,1)} %all-gather.3.cloned.1.call-done, bf16[128,1152]{1,0:T(8,128)(2,1)S(1)} %all_gather.10), kind=kOutput, calls=%fused_computation.14 | convolution fusion | flops 680067072 | bytes 5898240 | tf_op jit(solution)/shard_map/dot_general | solution.py:200
  133.1 9.8 %all_to_all.27 = bf16[4,32,1152]{2,1,0:T(8,128)(2,1)S(1)} all-to-all(bf16[4,32,1152]{2,1,0:T(8,128)(2,1)S(1)} %bitcast.147), channel_id=1, replica_groups=mesh['x_lo'=2,'y'=4,'z'=16,'x_hi'=2,'core'=2] {'x_hi','core'}, dimensions={0} | all-to-all | bytes 589824 | tf_op jit(solution)/shard_map/all_to_all | solution.py:27
  142.9 1.7 %fusion.25 = bf16[1,1,32,1152]{3,2,1,0:T(8,128)(2,1)} fusion(s32[1152]{0:T(1024)S(1)} %fusion.103, f32[32,1152]{1,0:T(8,128)S(1)} %convert_reduce_fusion.1, bf16[32,1152]{1,0:T(8,128)(2,1)S(1)} %fusion.23), kind=kOutput, calls=%fused_computation.19 | convolution fusion | flops 86409216 | bytes 299520 | tf_op jit(solution)/shard_map/dot_general | solution.py:205
  (61 shorter events, 1.3 us)
Async XLA Ops:
  6.5 97.9 %copy-start = (bf16[256,1152]{1,0:T(8,128)(2,1)S(1)}, bf16[256,1152]{1,0:T(8,128)(2,1)}, u32[]{:S(2)}) copy-start(bf16[256,1152]{1,0:T(8,128)(2,1)} %param.26) | copy-start | bytes 1769476
  6.5 23.4 %copy-start.8 = (f32[1152]{0:T(1024)S(1)}, f32[1152]{0:T(1024)}, u32[]{:S(2)}) copy-start(f32[1152]{0:T(1024)} %param.16) | copy-start | bytes 13828
  6.5 23.4 %copy-start.4 = (bf16[1152,256]{1,0:T(8,128)(2,1)S(1)}, bf16[1152,256]{1,0:T(8,128)(2,1)}, u32[]{:S(2)}) copy-start(bf16[1152,256]{1,0:T(8,128)(2,1)} %param.18) | copy-start | bytes 1769476
  6.5 23.9 %copy-start.5 = (bf16[1152,256]{1,0:T(8,128)(2,1)S(1)}, bf16[1152,256]{1,0:T(8,128)(2,1)}, u32[]{:S(2)}) copy-start(bf16[1152,256]{1,0:T(8,128)(2,1)} %param.17) | copy-start | bytes 1769476
  6.5 24.4 %copy-start.6 = (bf16[1152,64]{0,1:T(8,128)(2,1)S(1)}, bf16[1152,64]{0,1:T(8,128)(2,1)}, u32[]{:S(2)}) copy-start(bf16[1152,64]{0,1:T(8,128)(2,1)} %param.20) | copy-start | bytes 442372
  6.5 24.7 %copy-start.10 = (f32[256]{0:T(256)S(1)}, f32[256]{0:T(256)}, u32[]{:S(2)}) copy-start(f32[256]{0:T(256)} %param.22) | copy-start | bytes 3076
  6.6 24.7 %copy-start.7 = (bf16[64,256]{1,0:T(8,128)(2,1)S(1)}, bf16[64,256]{1,0:T(8,128)(2,1)}, u32[]{:S(2)}) copy-start(bf16[64,256]{1,0:T(8,128)(2,1)} %param.21) | copy-start | bytes 98308
  8.3 18.9 %all-to-all-start.3 = ((bf16[8,9,2304]{2,1,0:T(8,128)(2,1)}), bf16[8,9,2304]{2,1,0:T(8,128)(2,1)S(1)}, u32[]{:S(2)}, u32[]{:S(2)}) async-start(bf16[8,9,2304]{2,1,0:T(8,128)(2,1)} %broadcast_in_dim.42), calls=%async_computation.3 | async-start | bytes 1179648 | tf_op jit(solution)/shard_map/all_to_all | solution.py:16
  14.3 114.9 %all-gather.3.cloned.1.call-start = ((), (), s32[]{:S(2)}) async-start(), calls=%async_computation.5 | async-start | bytes 5640192 | tf_op jit(solution)/shard_map/all_gather | solution.py:133
  30.0 4.4 %copy-start.2 = (f32[256]{0:T(256)S(1)}, f32[256]{0:T(256)}, u32[]{:S(2)}) copy-start(f32[256]{0:T(256)} %param.24) | copy-start | bytes 3076
  34.3 47.1 %copy-start.3 = (f32[256]{0:T(256)S(1)}, f32[256]{0:T(256)}, u32[]{:S(2)}) copy-start(f32[256]{0:T(256)} %param.25) | copy-start | bytes 3076
  78.2 40.3 %copy-start.1 = (bf16[1,1,32,1152]{3,2,1,0:T(8,128)(2,1)S(1)}, bf16[1,1,32,1152]{3,2,1,0:T(8,128)(2,1)}, u32[]{:S(2)}) copy-start(bf16[1,1,32,1152]{3,2,1,0:T(8,128)(2,1)} %param.15) | copy-start | bytes 221188
  79.1 40.8 %copy-start.9 = (f32[1152]{0:T(1024)S(1)}, f32[1152]{0:T(1024)}, u32[]{:S(2)}) copy-start(f32[1152]{0:T(1024)} %param.27) | copy-start | bytes 13828
  105.5 12.9 %all-to-all-start.2 = ((bf16[4,32,1152]{2,1,0:T(8,128)(2,1)}), bf16[4,32,1152]{2,1,0:T(8,128)(2,1)S(1)}, u32[]{:S(2)}, u32[]{:S(2)}) async-start(bf16[4,32,1152]{2,1,0:T(8,128)(2,1)} %bitcast.51), calls=%async_computation.2 | async-start | bytes 589824 | tf_op jit(solution)/shard_map/all_to_all | solution.py:27
Sparse Core Ops, SparseCore 0:
  28.3 90.2 all-gather.2

commit v11 on v6

--- a/solution.py
+++ b/solution.py
@@ -121,14 +121,11 @@
 
     planes, depth = lax.axis_size(PLANE), lax.axis_size("z")
     width = feature_mix_addressing_matrix.shape[0]
-    pair = jnp.stack([feature_mix_addressing_matrix, feature_mix_content_matrix.T])
+    pair = jnp.concatenate([feature_mix_addressing_matrix, feature_mix_content_matrix.T], axis=1)
+    units = feature_mix_addressing_matrix.shape[1]
     plane_pair = from_everyone(pair, PLANE)
-    plane_pair = plane_pair.reshape(planes, *pair.shape)
-    plane_pair = jnp.swapaxes(plane_pair, 0, 1).reshape(2 * planes * width, -1)
+    plane_pair = plane_pair.reshape(planes * width, 2 * units)
     full_pair = lax.all_gather(plane_pair, "z", axis=0, tiled=True)
-    full_pair = full_pair.reshape(depth, 2, planes * width, -1)
-    full_up = full_pair[:, 0].reshape(model_width, -1)
-    full_down = full_pair[:, 1].reshape(model_width, -1)
 
     xn1 = layer_norm(whole_rows, initial_standardize_scaling)
     recept = jnp.dot(xn1, acceptance_matrix, preferred_element_type=jnp.float32).astype(
@@ -156,7 +153,7 @@
         self_token_reward,
         horizontal_cluster_scaling,
     )[0]
-    sent = jnp.stack([recept, keying, decay, row_out], axis=1)
+    sent = jnp.concatenate([recept, keying, decay, row_out], axis=1)
     sent = sent.reshape(full_cols, 4 * inner_width // 128, 128)
     got = lax.all_to_all(sent, SEQ, split_axis=0, concat_axis=0, tiled=True)
     height = got.shape[0]
@@ -187,11 +184,11 @@
     moved = (jnp.arange(model_width)[:, None] == places[None, :]).astype(jnp.bfloat16)
     mix_input = jnp.dot(mix_input, moved, preferred_element_type=jnp.float32).astype(jnp.bfloat16)
     mix_all = lax.all_gather(mix_input, MP, axis=0, tiled=True)
-    hidden_pre = jnp.dot(mix_all, full_up, preferred_element_type=jnp.float32)
+    hidden_pre = jnp.dot(mix_all, full_pair[:, :units], preferred_element_type=jnp.float32)
     positive = jnp.maximum(hidden_pre, 0.0)
     hidden = (positive * positive).astype(jnp.bfloat16)
     downward = lax.dot_general(
-        hidden, full_down, (((1,), (1,)), ((), ())), preferred_element_type=jnp.float32
+        hidden, full_pair[:, units:], (((1,), (1,)), ((), ())), preferred_element_type=jnp.float32
     ).astype(jnp.bfloat16)
     downward = lax.dot_general(
         downward, moved, (((1,), (1,)), ((), ())), preferred_element_type=jnp.float32

time: 155 us -> 155 us (level)
  local copies, waits for them, and re-layouts: 6.52 us -> 3.8 us
  blocking collectives: 105 us -> 107 us
    slice x1 -> x0, local copies, waits for them, and re-layouts: 3 us -> none  [shards(): full_down = full_pair[:, 1].reshape(model_width, -1)]
    dot_general x1, matrix products: 1.3 us -> 3.87 us  [shards(): lax.dot_general(hidden, full_pair[:, units:], (((1,), (1,)), ((), ())), p...]
    dot_general x1, matrix products: 3.58 us -> 1.12 us  [shards(): lax.dot_general(downward, moved, (((1,), (1,)), ((), ())), preferred_elem...]
  transfers between devices with their start and end apart: 2 -> 2, of which waited for: 1 -> 1; matrix products, arithmetic and copies ran while one was open for 7% -> 8% of each run, Pallas kernels for 0% -> 0%
where the time goes in v11:
time: 155 us
  blocking collectives  107 us (69%)
  between operations  13.9 us (9%)
  matrix products  12.6 us (8%)
  waiting for transfers between devices  6.88 us (4%)
  starting transfers between devices  6.66 us (4%)
  local copies, waits for them, and re-layouts  3.8 us (2%)
  other arithmetic  3.71 us (2%)
    all_to_all x1, blocking collectives, shards(): got = lax.all_to_all(sent, SEQ, split_axis=0, concat_axis=0, tiled=True)  41 us
    all_to_all x1, blocking collectives, shards(): lax.all_to_all(col_out.reshape(height, inner_width // 128, 128), SEQ, spl...  22.4 us
    all_to_all x1, blocking collectives, from_everyone(): return lax.all_to_all(copies, axis, split_axis=0, concat_axis=0, tiled=True)  13.9 us
    all_gather x1, blocking collectives, shards(): whole_rows = lax.all_gather(tokens, MP, axis=0, tiled=True)  12.1 us
    all_to_all x1, blocking collectives, sent_and_summed(): pieces = lax.all_to_all(split_up(value, dim, size), axis, 0, 0, tiled=True)  9.82 us
    all_gather x1, blocking collectives, shards(): mix_all = lax.all_gather(mix_input, MP, axis=0, tiled=True)  8.17 us
    all_to_all x1, waiting for transfers between devices, sent_and_summed(): pieces = lax.all_to_all(split_up(value, dim, size), axis, 0, 0, tiled=True)  6.87 us
    all_to_all x1, starting transfers between devices, sent_and_summed(): pieces = lax.all_to_all(split_up(value, dim, size), axis, 0, 0, tiled=True)  6.62 us
  transfers between devices with their start and end apart: 2, of which 1 were waited for; matrix products, arithmetic and copies ran while one was open for 8% of the time, Pallas kernels for 0%

profile of v11, /device:TPU:1, one launch (start us, length us, event | category | flops | bytes accessed | tf_op | source)
XLA Modules:
  0.0 154.9 jit_solution(12695652589653416136)
XLA Ops:
  6.6 0.9 pad_maximum_fusion.1
  7.6 13.9 %all_to_all.25 = bf16[8,9,2304]{2,1,0:T(8,128)(2,1)S(1)} all-to-all(bf16[8,9,2304]{2,1,0:T(8,128)(2,1)S(1)} %broadcast_in_dim.42), channel_id=1, replica_groups=mesh['x_lo'=2,'y'=4,'z'=16,'x_hi'=2,'core'=2] {'x_lo','y'}, dimensions={0} | all-to-all | bytes 663552 | tf_op jit(solution)/shard_map/all_to_all | solution.py:16
  21.4 0.9 reshape.434
  22.3 12.1 %all-gather = bf16[1,1,128,1152]{3,2,1,0:T(8,128)(2,1)S(1)} all-gather(bf16[1,1,32,1152]{3,2,1,0:T(8,128)(2,1)} %param.15), channel_id=2, replica_groups=mesh['x_lo'=2,'y'=4,'z'=16,'x_hi'=2,'core'=2] {'x_hi','core'}, dimensions={2}, use_global_device_ids=true | all-gather | bytes 368640 | tf_op jit(solution)/shard_map/all_gather | solution.py:118
  34.4 0.1 convert_reduce_fusion
  34.5 0.2 fusion.42
  34.8 1.4 convolution_convert_fusion.3
  36.3 0.1 copy.106
  36.4 0.3 convolution_convert_fusion.2
  36.8 0.1 copy.107
  37.0 0.5 fusion.29
  37.7 0.1 copy.108
  37.8 0.1 copy.112
  37.9 0.3 reduce_window_sum.17
  38.2 0.1 copy.114
  38.3 0.1 copy.110
  38.5 0.3 convolution_convert_fusion.1
  38.8 0.1 copy.115
  39.1 1.2 convolution_select_fusion.1
  40.3 0.2 fusion.112
  40.6 0.1 copy.116
  40.8 0.1 multiply_reduce_fusion.2
  41.2 0.1 copy.118
  41.3 0.1 copy.119
  41.4 0.1 copy.120
  41.7 0.2 copy.121
  41.8 41.0 %all_to_all.26 = bf16[128,8,128]{2,1,0:T(8,128)(2,1)S(1)} all-to-all(bf16[128,8,128]{2,1,0:T(8,128)(2,1)S(1)} %copy.121), channel_id=1, replica_groups=mesh['x_lo'=2,'y'=4,'z'=16,'x_hi'=2,'core'=2] {'x_lo','y','z'}, dimensions={0} | all-to-all | bytes 524288 | tf_op jit(solution)/shard_map/all_to_all | solution.py:158
  82.8 0.2 copy.122
  83.1 0.1 copy.124
  83.2 0.3 reduce_window_sum.18
  83.5 0.1 copy.125
  83.7 0.1 copy.123
  83.8 1.2 convolution_select_fusion
  85.0 0.2 fusion.113
  85.3 0.1 copy.126
  85.4 0.1 fusion.72
  85.9 22.4 %all_to_all.27 = bf16[128,2,128]{2,1,0:T(2,128)(2,1)S(1)} all-to-all(bf16[128,2,128]{2,1,0:T(2,128)(2,1)S(1)} %copy.128), channel_id=1, replica_groups=mesh['x_lo'=2,'y'=4,'z'=16,'x_hi'=2,'core'=2] {'x_lo','y','z'}, dimensions={0} | all-to-all | bytes 131072 | tf_op jit(solution)/shard_map/all_to_all | solution.py:169
  108.3 1.0 convolution_convert_fusion
  109.3 6.6 %all-to-all-start.2 = ((bf16[4,32,1152]{2,1,0:T(8,128)(2,1)}), bf16[4,32,1152]{2,1,0:T(8,128)(2,1)S(1)}, u32[]{:S(2)}, u32[]{:S(2)}) async-start(bf16[4,32,1152]{2,1,0:T(8,128)(2,1)} %bitcast.53), calls=%async_computation.2 | async-start | bytes 589824 | tf_op jit(solution)/shard_map/all_to_all | solution.py:27
  115.9 6.9 %all-to-all-done.2 = bf16[4,32,1152]{2,1,0:T(8,128)(2,1)S(1)} async-done(((bf16[4,32,1152]{2,1,0:T(8,128)(2,1)}), bf16[4,32,1152]{2,1,0:T(8,128)(2,1)S(1)}, u32[]{:S(2)}, u32[]{:S(2)}) %all-to-all-start.2) | async-done | bytes 294944 | tf_op jit(solution)/shard_map/all_to_all | solution.py:27
  122.8 0.1 convert_reduce_fusion.3
  123.0 0.2 fusion.64
  123.2 1.1 fusion.21
  124.3 8.2 %all_gather.10 = bf16[128,1152]{1,0:T(8,128)(2,1)S(1)} all-gather(bf16[32,1152]{1,0:T(8,128)(2,1)S(1)} %fusion.21), channel_id=1, replica_groups=mesh['x_lo'=2,'y'=4,'z'=16,'x_hi'=2,'core'=2] {'x_hi','core'}, dimensions={0}, use_global_device_ids=true | all-gather | bytes 368640 | tf_op jit(solution)/shard_map/all_gather | solution.py:186
  132.5 3.9 %fusion.17 = bf16[128,1152]{1,0:T(8,128)(2,1)S(1)} fusion(bf16[1152,2304]{1,0:T(8,128)(2,1)} %all-gather.3.cloned.1.call-done, bf16[128,1152]{1,0:T(8,128)(2,1)S(1)} %all_gather.10), kind=kOutput, calls=%fused_computation.12 | convolution fusion | flops 680067072 | bytes 5898240 | tf_op jit(solution)/shard_map/dot_general | solution.py:190
  136.4 1.1 fusion.20
  137.5 9.8 %all_to_all.28 = bf16[4,32,1152]{2,1,0:T(8,128)(2,1)S(1)} all-to-all(bf16[4,32,1152]{2,1,0:T(8,128)(2,1)S(1)} %bitcast.156), channel_id=1, replica_groups=mesh['x_lo'=2,'y'=4,'z'=16,'x_hi'=2,'core'=2] {'x_hi','core'}, dimensions={0} | all-to-all | bytes 589824 | tf_op jit(solution)/shard_map/all_to_all | solution.py:27
  147.3 0.7 fusion.70
  (64 shorter events, 1.5 us)
Async XLA Ops:
  6.5 101.7 %copy-start = (bf16[256,1152]{1,0:T(8,128)(2,1)S(1)}, bf16[256,1152]{1,0:T(8,128)(2,1)}, u32[]{:S(2)}) copy-start(bf16[256,1152]{1,0:T(8,128)(2,1)} %param.26) | copy-start | bytes 1769476
  6.5 29.9 %copy-start.9 = (f32[1152]{0:T(1024)S(1)}, f32[1152]{0:T(1024)}, u32[]{:S(2)}) copy-start(f32[1152]{0:T(1024)} %param.16) | copy-start | bytes 13828
  6.5 29.9 %copy-start.5 = (bf16[1152,256]{1,0:T(8,128)(2,1)S(1)}, bf16[1152,256]{1,0:T(8,128)(2,1)}, u32[]{:S(2)}) copy-start(bf16[1152,256]{1,0:T(8,128)(2,1)} %param.18) | copy-start | bytes 1769476
  6.5 30.4 %copy-start.7 = (bf16[1152,64]{0,1:T(8,128)(2,1)S(1)}, bf16[1152,64]{0,1:T(8,128)(2,1)}, u32[]{:S(2)}) copy-start(bf16[1152,64]{0,1:T(8,128)(2,1)} %param.20) | copy-start | bytes 442372
  6.5 30.4 %copy-start.8 = (bf16[64,256]{1,0:T(8,128)(2,1)S(1)}, bf16[64,256]{1,0:T(8,128)(2,1)}, u32[]{:S(2)}) copy-start(bf16[64,256]{1,0:T(8,128)(2,1)} %param.21) | copy-start | bytes 98308
  6.5 30.4 %copy-start.11 = (f32[256]{0:T(256)S(1)}, f32[256]{0:T(256)}, u32[]{:S(2)}) copy-start(f32[256]{0:T(256)} %param.22) | copy-start | bytes 3076
  6.6 125.9 %all-gather.3.cloned.1.call-start = ((), (), s32[]{:S(2)}) async-start(), calls=%async_computation.5 | async-start | bytes 5640192 | tf_op jit(solution)/shard_map/all_gather | solution.py:128
  7.5 30.9 %copy-start.6 = (bf16[1152,256]{1,0:T(8,128)(2,1)S(1)}, bf16[1152,256]{1,0:T(8,128)(2,1)}, u32[]{:S(2)}) copy-start(bf16[1152,256]{1,0:T(8,128)(2,1)} %param.19) | copy-start | bytes 1769476
  36.2 4.5 %copy-start.4 = (f32[256]{0:T(256)S(1)}, f32[256]{0:T(256)}, u32[]{:S(2)}) copy-start(f32[256]{0:T(256)} %param.23) | copy-start | bytes 3076
  36.7 4.8 %copy-start.2 = (f32[256]{0:T(256)S(1)}, f32[256]{0:T(256)}, u32[]{:S(2)}) copy-start(f32[256]{0:T(256)} %param.24) | copy-start | bytes 3076
  41.0 44.8 %copy-start.3 = (f32[256]{0:T(256)S(1)}, f32[256]{0:T(256)}, u32[]{:S(2)}) copy-start(f32[256]{0:T(256)} %param.25) | copy-start | bytes 3076
  41.8 81.0 %copy-start.1 = (bf16[1,1,32,1152]{3,2,1,0:T(8,128)(2,1)S(1)}, bf16[1,1,32,1152]{3,2,1,0:T(8,128)(2,1)}, u32[]{:S(2)}) copy-start(bf16[1,1,32,1152]{3,2,1,0:T(8,128)(2,1)} %param.15) | copy-start | bytes 221188
  82.8 40.3 %copy-start.10 = (f32[1152]{0:T(1024)S(1)}, f32[1152]{0:T(1024)}, u32[]{:S(2)}) copy-start(f32[1152]{0:T(1024)} %param.27) | copy-start | bytes 13828
  109.3 13.5 %all-to-all-start.2 = ((bf16[4,32,1152]{2,1,0:T(8,128)(2,1)}), bf16[4,32,1152]{2,1,0:T(8,128)(2,1)S(1)}, u32[]{:S(2)}, u32[]{:S(2)}) async-start(bf16[4,32,1152]{2,1,0:T(8,128)(2,1)} %bitcast.53), calls=%async_computation.2 | async-start | bytes 589824 | tf_op jit(solution)/shard_map/all_to_all | solution.py:27
Sparse Core Ops, SparseCore 0:
  22.5 93.4 all-gather.2
